TPU v7x, 16 devices: a 4x2x1 block of a 4x4x8 slice. The times are simulated.
16 devices in a mesh: data: 2 (over y, z), model: 8 (over x, core).
Axes of the slice: x: 4, y: 2, z: 1, core: 2. Of those that a mesh axis runs over, the one named last changes fastest.
The devices are a block of a 4x4x8 slice.
Arguments:
- hidden: bfloat16 [256, 3072], P(('data', 'model')), parts along dimension 0
- positions: int32 [256], P('data'), parts along dimension 0
- attn_gain: bfloat16 [1, 3072], replicated
- mlp_gain: bfloat16 [1, 3072], replicated
- w_query: bfloat16 [1, 3072, 4096], P(None, None, 'model')
- w_key: bfloat16 [1, 3072, 4096], P(None, None, 'model')
- w_value: bfloat16 [1, 3072, 4096], P(None, None, 'model')
- w_out: bfloat16 [1, 4096, 3072], P(None, 'model')
- w_gate: bfloat16 [1, 3072, 24576], P(None, None, 'model')
- w_up: bfloat16 [1, 3072, 24576], P(None, None, 'model')
- w_down: bfloat16 [1, 24576, 3072], P(None, 'model')
- k_cache: bfloat16 [1, 256, 64, 16, 256], P(None, 'data', None, 'model'), parts along dimension 1
- v_cache: bfloat16 [1, 256, 64, 16, 256], P(None, 'data', None, 'model'), parts along dimension 1
Outputs:
- output 1: bfloat16 [256, 3072], P(('data', 'model')), parts along dimension 0
- output 2: bfloat16 [1, 256, 64, 16, 256], P(None, 'data', None, 'model'), parts along dimension 1
- output 3: bfloat16 [1, 256, 64, 16, 256], P(None, 'data', None, 'model'), parts along dimension 1
There are 2 independent parts. A program takes and returns all parts, laid end to end along the dimension named above; an argument that names none is the same for every part.
All inputs are finite; a program needn't handle non-finite values.
Results may differ from a plain program's by a relative error of at most 0.0145115.
Values are sent between devices in bfloat16 or wider.
A program may use at most 768 MiB of HBM per device.

v0:
```python
import jax
import jax.numpy as jnp
from jax import lax
from jax.sharding import PartitionSpec as P

NORM_EPS = 1e-5
ROPE_BASE = 10000.0


def rms_norm(row_vals, gain_vec):
    values_f = row_vals.astype(jnp.float32)
    inv_rms = lax.rsqrt(jnp.mean(values_f * values_f, axis=-1, keepdims=True) + NORM_EPS)
    return (values_f * inv_rms * gain_vec.astype(jnp.float32)).astype(jnp.bfloat16)


def rope_tables(positions, head_dim):
    half_dim = head_dim // 2
    inv_freq = ROPE_BASE ** (-2.0 * jnp.arange(half_dim, dtype=jnp.float32) / head_dim)
    angles = positions.astype(jnp.float32)[:, None] * inv_freq[None, :]
    return jnp.cos(angles), jnp.sin(angles)


def rope_rotate(head_vecs, cos_tab, sin_tab):
    half_dim = head_vecs.shape[-1] // 2
    lead_shape = (cos_tab.shape[0],) + (1,) * (head_vecs.ndim - 2) + (half_dim,)
    cos_b = cos_tab.reshape(lead_shape)
    sin_b = sin_tab.reshape(lead_shape)
    front_half = head_vecs[..., :half_dim].astype(jnp.float32)
    back_half = head_vecs[..., half_dim:].astype(jnp.float32)
    rotated = jnp.concatenate([front_half * cos_b - back_half * sin_b, back_half * cos_b + front_half * sin_b], axis=-1)
    return rotated.astype(jnp.bfloat16)


def attend(queries, k_layer, v_layer, positions):
    head_dim = queries.shape[-1]
    scores = jnp.einsum('bgrd,bsgd->bgrs', queries, k_layer, preferred_element_type=jnp.float32) * (head_dim ** -0.5)
    allowed = jnp.arange(k_layer.shape[1])[None, :] <= positions[:, None]
    scores = jnp.where(allowed[:, None, None, :], scores, -1e30)
    attn_probs = jax.nn.softmax(scores, axis=-1).astype(jnp.bfloat16)
    mixed_out = jnp.einsum('bgrs,bsgd->bgrd', attn_probs, v_layer, preferred_element_type=jnp.float32)
    return mixed_out.astype(jnp.bfloat16).reshape(queries.shape[0], -1)


def solution(mesh):
    row_spec = P(('data', 'model'), None)
    cache_spec = P(None, 'data', None, 'model', None)
    col_spec = P(None, None, 'model')
    inner_spec = P(None, 'model', None)
    in_specs = (row_spec, P('data'), P(), P(), col_spec, col_spec, col_spec, inner_spec, col_spec, col_spec, inner_spec, cache_spec, cache_spec)
    out_specs = (row_spec, cache_spec, cache_spec)

    def device_step(hidden, positions, attn_gain, mlp_gain, w_query, w_key, w_value, w_out, w_gate, w_up, w_down, k_cache, v_cache):
        n_layers = w_query.shape[0]
        n_tokens = positions.shape[0]
        local_kv = k_cache.shape[3]
        head_dim = k_cache.shape[4]
        group_size = w_query.shape[2] // (local_kv * head_dim)
        row_ids = jnp.arange(n_tokens)
        cos_tab, sin_tab = rope_tables(positions, head_dim)
        for layer_idx in range(n_layers):
            normed = rms_norm(hidden, attn_gain[layer_idx])
            gathered = lax.all_gather(normed, 'model', axis=0, tiled=True)
            queries = jnp.dot(gathered, w_query[layer_idx], preferred_element_type=jnp.float32).astype(jnp.bfloat16)
            keys_new = jnp.dot(gathered, w_key[layer_idx], preferred_element_type=jnp.float32).astype(jnp.bfloat16)
            values_new = jnp.dot(gathered, w_value[layer_idx], preferred_element_type=jnp.float32).astype(jnp.bfloat16)
            queries = rope_rotate(queries.reshape(n_tokens, local_kv, group_size, head_dim), cos_tab, sin_tab)
            keys_new = rope_rotate(keys_new.reshape(n_tokens, local_kv, head_dim), cos_tab, sin_tab)
            values_new = values_new.reshape(n_tokens, local_kv, head_dim)
            k_cache = k_cache.at[layer_idx, row_ids, positions].set(keys_new)
            v_cache = v_cache.at[layer_idx, row_ids, positions].set(values_new)
            attn_rows = attend(queries, k_cache[layer_idx], v_cache[layer_idx], positions)
            partial = jnp.dot(attn_rows, w_out[layer_idx], preferred_element_type=jnp.float32).astype(jnp.bfloat16)
            summed = lax.psum_scatter(partial, 'model', scatter_dimension=0, tiled=True)
            hidden = (hidden.astype(jnp.float32) + summed.astype(jnp.float32)).astype(jnp.bfloat16)
            normed = rms_norm(hidden, mlp_gain[layer_idx])
            gathered = lax.all_gather(normed, 'model', axis=0, tiled=True)
            gate_proj = jnp.dot(gathered, w_gate[layer_idx], preferred_element_type=jnp.float32)
            up_proj = jnp.dot(gathered, w_up[layer_idx], preferred_element_type=jnp.float32)
            mlp_act = (jax.nn.silu(gate_proj) * up_proj).astype(jnp.bfloat16)
            partial = jnp.dot(mlp_act, w_down[layer_idx], preferred_element_type=jnp.float32).astype(jnp.bfloat16)
            summed = lax.psum_scatter(partial, 'model', scatter_dimension=0, tiled=True)
            hidden = (hidden.astype(jnp.float32) + summed.astype(jnp.float32)).astype(jnp.bfloat16)
        return hidden, k_cache, v_cache

    return jax.shard_map(device_step, mesh=mesh, in_specs=in_specs, out_specs=out_specs, check_vma=False)
```

profile of v0, /device:TPU:113, one launch (start us, length us, event | category | flops | bytes accessed | tf_op | source)
XLA Modules:
  0.0 221.4 jit_solution(9024469360022697994)
XLA Ops:
  7.3 8.1 %copy.41 = bf16[1,128,64,2,256]{4,3,2,1,0:T(2,128)(2,1)} copy(bf16[1,128,64,2,256]{4,3,2,1,0:T(2,128)(2,1)} %param.24) | data formatting | bytes 16777216
  15.4 0.8 copy-done.3
  16.2 4.0 %copy.42 = bf16[1,128,64,2,256]{4,3,2,1,0:T(2,128)(2,1)} copy(bf16[1,128,64,2,256]{4,3,2,1,0:T(2,128)(2,1)S(1)} %copy-done.3) | data formatting | bytes 16777216
  20.3 0.1 fusion.45
  20.6 20.5 %all_gather.6 = bf16[128,3072]{1,0:T(8,128)(2,1)S(1)} all-gather(bf16[16,3072]{1,0:T(8,128)(2,1)S(1)} %fusion.47), channel_id=1, replica_groups=mesh['data'=2,'model'=8] {'model'}, dimensions={0}, use_global_device_ids=true | all-gather | bytes 884736 | tf_op jit(solution)/shard_map/all_gather | solution.py:62
  41.0 0.9 copy-done.2
  41.9 0.6 fusion.31
  42.8 0.1 copy.27
  42.9 0.3 multiply_cosine_fusion
  43.4 0.1 copy.19
  43.5 3.4 %fusion.28 = bf16[128,512]{1,0:T(8,128)(2,1)} fusion(bf16[128,3072]{1,0:T(8,128)(2,1)} %copy-done.2, bf16[1,3072,512]{2,1,0:T(8,128)(2,1)} %param.17), kind=kOutput, calls=%fused_computation.25 | convolution fusion | flops 402718720 | bytes 4063232 | tf_op jit(solution)/shard_map/dot_general | solution.py:63
  46.9 1.6 reshape.190
  48.5 1.0 fusion.63
  49.5 0.8 maximum_bitcast_fusion
  50.3 16.4 %scatter_fusion = bf16[128,64,2,256]{3,2,1,0:T(2,128)(2,1)} fusion(bf16[128,64,2,256]{3,2,1,0:T(2,128)(2,1)} %bitcast.79, s32[128]{0:T(128)S(1)} %fusion.71, bf16[128,2,256]{2,1,0:T(2,128)(2,1)S(1)} %copy.19), kind=kCustom, calls=%fused_computation | custom fusion | bytes 394240 | tf_op jit(solution)/shard_map/scatter | solution.py:69
  66.7 5.7 %fusion.10 = f32[128,2,1,64]{3,2,1,0:T(1,128)S(1)} fusion(bf16[128,64,2,256]{3,2,1,0:T(2,128)(2,1)} %scatter_fusion, bf16[128,2,256,1]{2,1,0,3:T(2,128)(2,1)} %maximum_bitcast_fusion), kind=kOutput, calls=%fused_computation.12 | convolution fusion | flops 8388608 | bytes 8585216 | tf_op jit(solution)/shard_map/bgrd,bsgd->bgrs/dot_general | solution.py:36
  72.6 0.1 copy.23
  72.7 3.4 %fusion.34 = bf16[128,512]{1,0:T(8,128)(2,1)} fusion(bf16[128,3072]{1,0:T(8,128)(2,1)} %copy-done.2, bf16[1,3072,512]{2,1,0:T(8,128)(2,1)} %param.19), kind=kOutput, calls=%fused_computation.27 | convolution fusion | flops 402718720 | bytes 4063232 | tf_op jit(solution)/shard_map/dot_general | solution.py:65
  76.1 1.0 reshape.208
  77.1 16.4 %scatter_fusion.1 = bf16[128,64,2,256]{3,2,1,0:T(2,128)(2,1)} fusion(bf16[128,64,2,256]{3,2,1,0:T(2,128)(2,1)} %bitcast.77, s32[128]{0:T(128)S(1)} %fusion.71, bf16[128,2,256]{2,1,0:T(2,128)(2,1)S(1)} %reshape.208), kind=kCustom, calls=%fused_computation.1 | custom fusion | bytes 394240 | tf_op jit(solution)/shard_map/scatter | solution.py:70
  93.5 4.6 %fusion.8 = bf16[128,2,1,256]{3,2,1,0:T(2,128)(2,1)S(1)} fusion(bf16[128,2,64,1]{2,3,1,0:T(2,128)(2,1)S(1)} %copy.23, bf16[128,64,2,256]{3,2,1,0:T(2,128)(2,1)} %scatter_fusion.1), kind=kOutput, calls=%fused_computation.10 | convolution fusion | flops 8388608 | bytes 8552448 | tf_op jit(solution)/shard_map/bgrs,bsgd->bgrd/dot_general | solution.py:40
  98.0 0.1 copy.36
  98.2 1.5 convolution_convert_fusion
  99.9 30.1 %reduce-scatter.3.cloned.1.call-done = bf16[16,3072]{1,0:T(8,128)(2,1)} async-done(((bf16[128,3072]{1,0:T(8,128)(2,1)}), bf16[16,3072]{1,0:T(8,128)(2,1)}) %reduce-scatter.3.cloned.1.call-update) | async-done | bytes 98320 | tf_op jit(solution)/shard_map/reduce_scatter | solution.py:73
  129.9 1.0 fusion.49
  131.0 1.0 fusion.51
  132.0 21.2 %all_gather.7 = bf16[128,3072]{1,0:T(8,128)(2,1)S(1)} all-gather(bf16[16,3072]{1,0:T(8,128)(2,1)S(1)} %fusion.51), channel_id=1, replica_groups=mesh['data'=2,'model'=8] {'model'}, dimensions={0}, use_global_device_ids=true | all-gather | bytes 884736 | tf_op jit(solution)/shard_map/all_gather | solution.py:76
  153.1 0.9 copy-done.4
  154.0 10.1 %fusion.6 = f32[128,3072]{1,0:T(8,128)} fusion(bf16[128,3072]{1,0:T(8,128)(2,1)S(1)} %all_gather.7, bf16[1,3072,3072]{2,1,0:T(8,128)(2,1)} %param.21), kind=kOutput, calls=%fused_computation.8 | convolution fusion | flops 2415919104 | bytes 21233664 | tf_op jit(solution)/shard_map/dot_general | solution.py:77
  164.2 18.8 %fusion.15 = bf16[128,3072]{1,0:T(8,128)(2,1)} fusion(bf16[1,3072,3072]{2,1,0:T(8,128)(2,1)} %param.23, bf16[128,3072]{1,0:T(8,128)(2,1)} %copy-done.4, bf16[1,3072,3072]{2,1,0:T(8,128)(2,1)} %param.22, f32[128,3072]{1,0:T(8,128)} %fusion.6), kind=kOutput, calls=%fused_computation.15 | convolution fusion | flops 4834590720 | bytes 40894464 | tf_op jit(solution)/shard_map/dot_general | solution.py:80
  183.0 29.9 %reduce-scatter.5.cloned.1.call-done = bf16[16,3072]{1,0:T(8,128)(2,1)} async-done(((bf16[128,3072]{1,0:T(8,128)(2,1)}), bf16[16,3072]{1,0:T(8,128)(2,1)}) %reduce-scatter.5.cloned.1.call-update) | async-done | bytes 98320 | tf_op jit(solution)/shard_map/reduce_scatter | solution.py:81
  213.0 1.6 fusion.52
  (40 shorter events, 0.9 us)
Async XLA Ops:
  7.2 91.0 %copy-start = (bf16[1,512,3072]{2,1,0:T(8,128)(2,1)S(1)}, bf16[1,512,3072]{2,1,0:T(8,128)(2,1)}, u32[]{:S(2)}) copy-start(bf16[1,512,3072]{2,1,0:T(8,128)(2,1)} %param.20) | copy-start | bytes 9437188
  7.2 122.7 %reduce-scatter.3.cloned.1.call-start = ((), (), s32[]{:S(2)}) async-start(), calls=%async_computation.2 | async-start | bytes 884736 | tf_op jit(solution)/shard_map/reduce_scatter | solution.py:73
  7.3 9.0 %copy-start.3 = (bf16[1,128,64,2,256]{4,3,2,1,0:T(2,128)(2,1)S(1)}, bf16[1,128,64,2,256]{4,3,2,1,0:T(2,128)(2,1)}, u32[]{:S(2)}) copy-start(bf16[1,128,64,2,256]{4,3,2,1,0:T(2,128)(2,1)} %param.25) | copy-start | bytes 25165828
  16.2 4.0 %copy-start.10 = (s32[128]{0:T(128)S(1)}, s32[128]{0:T(128)}, u32[]{:S(2)}) copy-start(s32[128]{0:T(128)} %param.14) | copy-start | bytes 1540
  16.2 4.1 %copy-start.8 = (bf16[1,3072]{1,0:T(2,128)(2,1)S(1)}, bf16[1,3072]{1,0:T(2,128)(2,1)}, u32[]{:S(2)}) copy-start(bf16[1,3072]{1,0:T(2,128)(2,1)} %param.15) | copy-start | bytes 18436
  16.2 4.1 %copy-start.6 = (bf16[16,3072]{1,0:T(8,128)(2,1)S(1)}, bf16[16,3072]{1,0:T(8,128)(2,1)}, u32[]{:S(2)}) copy-start(bf16[16,3072]{1,0:T(8,128)(2,1)} %param.13) | copy-start | bytes 294916
  16.2 25.7 %copy-start.5 = (bf16[1,3072,512]{2,1,0:T(8,128)(2,1)S(1)}, bf16[1,3072,512]{2,1,0:T(8,128)(2,1)}, u32[]{:S(2)}) copy-start(bf16[1,3072,512]{2,1,0:T(8,128)(2,1)} %param.18) | copy-start | bytes 9437188
  41.0 0.9 copy-start.2
  76.1 23.7 %copy-start.9 = (bf16[1,3072]{1,0:T(2,128)(2,1)S(1)}, bf16[1,3072]{1,0:T(2,128)(2,1)}, u32[]{:S(2)}) copy-start(bf16[1,3072]{1,0:T(2,128)(2,1)} %param.16) | copy-start | bytes 18436
  99.8 113.2 %reduce-scatter.5.cloned.1.call-start = ((), (), s32[]{:S(2)}) async-start(), calls=%async_computation.3 | async-start | bytes 884736 | tf_op jit(solution)/shard_map/reduce_scatter | solution.py:81
  153.1 0.9 copy-start.4
  164.2 48.8 %copy-start.7 = (bf16[16,3072]{1,0:T(8,128)(2,1)S(1)}, bf16[16,3072]{1,0:T(8,128)(2,1)}, u32[]{:S(2)}) copy-start(bf16[16,3072]{1,0:T(8,128)(2,1)} %reduce-scatter.3.cloned.1.call-done) | copy-start | bytes 294916
  164.2 50.4 %copy-start.1 = (bf16[1,512,3072]{2,1,0:T(8,128)(2,1)S(1)}, bf16[1,512,3072]{2,1,0:T(8,128)(2,1)}, u32[]{:S(2)}) copy-start(bf16[1,512,3072]{2,1,0:T(8,128)(2,1)} %param.20) | copy-start | bytes 9437188
Sparse Core Ops, SparseCore 0:
  99.9 30.0 reduce-scatter.2
  183.1 29.7 reduce-scatter.4
where the time goes:
time: 225 us; the launch traced here: 221 us
  waiting for transfers between devices  60.1 us (27%)
  local copies, waits for them, and re-layouts  51 us (23%)
  matrix products  48.1 us (21%)
  blocking collectives  41.6 us (18%)
  between operations  14.3 us (6%)
  other arithmetic  6.19 us (3%)
    reduce_scatter x2, waiting for transfers between devices, device_step(): summed = lax.psum_scatter(partial, 'model', scatter_dimension=0, tiled=True)  60 us
    all_gather x2, blocking collectives, device_step(): gathered = lax.all_gather(normed, 'model', axis=0, tiled=True)  41.6 us
    dot_general x1, matrix products, device_step(): jnp.dot(mlp_act, w_down[layer_idx], preferred_element_type=jnp.float32)  18.8 us
    scatter x1, local copies, waits for them, and re-layouts, device_step(): v_cache = v_cache.at[layer_idx, row_ids, positions].set(values_new)  16.4 us
    scatter x1, local copies, waits for them, and re-layouts, device_step(): k_cache = k_cache.at[layer_idx, row_ids, positions].set(keys_new)  16.4 us
    unnamed x27, local copies, waits for them, and re-layouts  15 us
    dot_general x1, matrix products, device_step(): jnp.dot(gathered, w_gate[layer_idx], preferred_element_type=jnp.float32)  10.1 us
    dot_general x1, matrix products, attend(): jnp.einsum('bgrd,bsgd->bgrs', queries, k_layer, preferred_element_type=jn...  5.72 us
  transfers between devices with their start and end apart: 2, of which 2 were waited for; matrix products, arithmetic and copies ran while one was open for 0% of the time, Pallas kernels for 0%

commit v1 on v0

v1 whole, which is shorter than its diff:
```python
import functools
import math
import jax
import jax.numpy as jnp
from jax import lax
from jax.experimental import pallas as pl
from jax.experimental.pallas import tpu as pltpu
from jax.sharding import PartitionSpec as P

NORM_EPS = 1e-5
ROPE_BASE = 10000.0
BF16 = jnp.bfloat16
F32 = jnp.float32
VMEM = pl.BlockSpec(memory_space=pltpu.VMEM)
SMEM = pl.BlockSpec(memory_space=pltpu.SMEM)
HBM = pl.BlockSpec(memory_space=pltpu.HBM)
MLP_VMEM = 65800000
CHIPS = 4
MLP_CHUNK = 512


def places():
    me = lax.axis_index('model')
    core = lax.rem(me, 2)
    chip = lax.div(me, 2)
    other = me + 1 - 2 * core
    right = lax.rem(chip + 1, CHIPS) * 2 + core
    left = lax.rem(chip + CHIPS - 1, CHIPS) * 2 + core
    return me, core, chip, other, right, left


def enter(other, right, left):
    barrier = pltpu.get_barrier_semaphore()
    for peer in (other, right, left):
        pl.semaphore_signal(barrier, inc=1, device_id={'model': peer})
    pl.semaphore_wait(barrier, 3)


def remote(src, dst, send_sem, recv_sem, peer):
    return pltpu.make_async_remote_copy(src_ref=src, dst_ref=dst, send_sem=send_sem, recv_sem=recv_sem, device_id={'model': peer})


def norm_rows(x_f, gain_f):
    inv_rms = lax.rsqrt(jnp.mean(x_f * x_f, axis=-1, keepdims=True) + NORM_EPS)
    return (x_f * inv_rms * gain_f).astype(BF16)


def gather_rows(buf, send_sems, recv_sems):
    me, core, chip, other, right, left = places()
    width = buf.shape[2]
    half = width // 2
    lo, hi = pl.ds(0, half), pl.ds(half, half)
    far = lax.rem(chip + 2, CHIPS) * 2 + core
    full = pl.ds(0, width)

    def hop(blk, cols, idx, peer):
        view = buf.at[blk, :, cols]
        return remote(view, view, send_sems.at[idx], recv_sems.at[idx], peer)

    def arrive(blk, cols, idx):
        hop(blk, cols, idx, other).wait_recv()

    sends = [hop(me, lo, 0, right), hop(me, hi, 2, left), hop(me, hi, 1, right), hop(me, lo, 3, left), hop(me, full, 6, other)]
    for copy in sends:
        copy.start()

    def forward(blk, cols, idx, peer):
        copy = hop(blk, cols, idx, peer)
        copy.start()
        sends.append(copy)

    arrive(left, lo, 0)
    forward(left, lo, 4, right)
    forward(left, lo, 7, other)
    arrive(right, hi, 2)
    forward(right, hi, 5, left)
    forward(right, hi, 8, other)
    arrive(left, hi, 1)
    forward(left, hi, 9, other)
    arrive(right, lo, 3)
    forward(right, lo, 10, other)
    arrive(far, lo, 4)
    forward(far, lo, 11, other)
    arrive(far, hi, 5)
    forward(far, hi, 12, other)

    def across(blk):
        return blk + 1 - 2 * core

    arrive(other, full, 6)
    arrive(across(left), lo, 7)
    arrive(across(right), hi, 8)
    arrive(across(left), hi, 9)
    arrive(across(right), lo, 10)
    arrive(across(far), lo, 11)
    arrive(across(far), hi, 12)
    for copy in sends:
        copy.wait_send()


GATHER_SEMS = 13


def qkv_kernel(x_hbm, gain_hbm, pos_hbm, wq_hbm, wk_hbm, wv_hbm, q_ref, k_ref, v_ref, x_buf, gain_ref, pos_ref, h_buf, w_buf, load_sems, send_sems, recv_sems):
    me, core, chip, other, right, left = places()
    loads = [pltpu.make_async_copy(src, dst, load_sems.at[3 + i]) for i, (src, dst) in enumerate(((x_hbm, x_buf), (gain_hbm, gain_ref), (pos_hbm, pos_ref)))]
    for copy in loads:
        copy.start()
    w_copies = [pltpu.make_async_copy(w.at[0], w_buf.at[i], load_sems.at[i]) for i, w in enumerate((wq_hbm, wk_hbm, wv_hbm))]
    for copy in w_copies:
        copy.start()
    for copy in loads:
        copy.wait()
    h_buf[me] = norm_rows(x_buf[...].astype(F32), gain_ref[...].astype(F32))
    enter(other, right, left)
    gather_rows(h_buf, send_sems, recv_sems)

    n_tok = pos_ref.shape[1]
    half = 128
    head = 2 * half
    pos_row = jnp.broadcast_to(pos_ref[...].astype(F32), (n_tok, n_tok))
    diag = lax.broadcasted_iota(jnp.int32, (n_tok, n_tok), 0) == lax.broadcasted_iota(jnp.int32, (n_tok, n_tok), 1)
    pos_col = jnp.sum(jnp.where(diag, pos_row, 0.0), axis=1, keepdims=True)
    lane = lax.broadcasted_iota(jnp.int32, (n_tok, half), 1).astype(F32)
    angles = pos_col * jnp.exp(lane * (-2.0 * math.log(ROPE_BASE) / head))
    cos_tab, sin_tab = jnp.cos(angles), jnp.sin(angles)
    h_all = h_buf[...].reshape(n_tok, h_buf.shape[2])
    for i, out_ref in enumerate((q_ref, k_ref, v_ref)):
        w_copies[i].wait()
        proj = jnp.dot(h_all, w_buf[i], preferred_element_type=F32).astype(BF16)
        if i == 2:
            out_ref[...] = proj
            continue
        for h0 in range(0, proj.shape[1], head):
            front = proj[:, h0:h0 + half].astype(F32)
            back = proj[:, h0 + half:h0 + head].astype(F32)
            out_ref[:, h0:h0 + half] = (front * cos_tab - back * sin_tab).astype(BF16)
            out_ref[:, h0 + half:h0 + head] = (back * cos_tab + front * sin_tab).astype(BF16)


TOK_STEP = 16
TOK_SUB = 8


def attn_kernel(pos_smem, pos_ref, q_ref, k_ref, v_ref, wo_ref, kc_hbm, vc_hbm, part_ref, ko_hbm, vo_hbm,
                k_buf, v_buf, new_buf, q_buf, o_buf, pc_buf, in_sems, out_sems):
    _, n_tok, n_rows, n_heads, head = kc_hbm.shape
    lanes = 128
    steps = n_tok // TOK_STEP
    per_tok = n_rows * n_heads
    bufs = (k_buf, v_buf)

    def copies(t, hbm_pair, sems, outward):
        made = []
        for kv in range(2):
            flat = hbm_pair[kv].reshape(1, n_tok, per_tok, head)
            for c in range(2):
                far = flat.at[0, pl.ds(t * TOK_STEP, TOK_STEP), :, pl.ds(c * lanes, lanes)]
                near = bufs[kv].at[c, pl.ds(t * TOK_STEP, TOK_STEP)]
                src, dst = (near, far) if outward else (far, near)
                made.append(pltpu.make_async_copy(src, dst, sems.at[kv, c, t]))
        return made

    for t in range(steps):
        for copy in copies(t, (kc_hbm, vc_hbm), in_sems, False):
            copy.start()

    for h in range(n_heads):
        for c in range(2):
            cols = slice(h * head + c * lanes, h * head + (c + 1) * lanes)
            q_buf.at[c][pl.ds(h, n_tok, stride=2), :] = q_ref[:, cols].astype(F32)
            new_buf[0, h, c] = k_ref[:, cols].astype(F32)
            new_buf[1, h, c] = v_ref[:, cols].astype(F32)
    rows2 = n_tok * n_heads
    pos_row = jnp.broadcast_to(pos_ref[...].astype(F32), (rows2, n_tok))
    own = lax.broadcasted_iota(jnp.int32, (rows2, n_tok), 0) // 2 == lax.broadcasted_iota(jnp.int32, (rows2, n_tok), 1)
    pc_buf[...] = jnp.broadcast_to(jnp.sum(jnp.where(own, pos_row, 0.0), axis=1, keepdims=True), (rows2, n_tok))

    tile_row = lax.broadcasted_iota(jnp.int32, (16, lanes), 0)
    sub_rows = TOK_SUB * n_heads
    q_row = lax.broadcasted_iota(jnp.int32, (sub_rows, lanes), 0)
    key_col = lax.broadcasted_iota(jnp.int32, (sub_rows, lanes), 1)
    same_head = (q_row % 2) == (key_col % 2)
    key_pos = (key_col // 2).astype(F32)
    q_tok = q_row // 2

    def step(t, carry):
        for copy in copies(t, (kc_hbm, vc_hbm), in_sems, False):
            copy.wait()
        for i in range(TOK_STEP):
            b = t * TOK_STEP + i
            pos = pos_smem[0, b]
            tile = pl.ds(pl.multiple_of((pos >> 3) * 16, 16), 16)
            hit = (tile_row >> 1) == (pos & 7)
            for kv in range(2):
                for c in range(2):
                    old = bufs[kv][c, b, tile, :].astype(F32)
                    new = jnp.where((tile_row & 1) == 1, new_buf[kv, 1, c, pl.ds(b, 1), :], new_buf[kv, 0, c, pl.ds(b, 1), :])
                    bufs[kv][c, b, tile, :] = jnp.where(hit, new, old).astype(BF16)
        for sub in range(TOK_STEP // TOK_SUB):
            b0 = t * TOK_STEP + sub * TOK_SUB
            rows = pl.ds(pl.multiple_of(b0 * n_heads, 16), sub_rows)
            toks = pl.ds(b0, TOK_SUB)
            q = jnp.concatenate([q_buf[0, rows, :], q_buf[1, rows, :]], axis=1).astype(BF16)
            keys = jnp.concatenate([k_buf[c, toks].reshape(TOK_SUB * per_tok, lanes) for c in range(2)], axis=1)
            scores = lax.dot_general(q, keys, (((1,), (1,)), ((), ())), preferred_element_type=F32)
            mine = jnp.zeros((sub_rows, lanes), F32)
            for m in range(TOK_SUB):
                mine = jnp.where(q_tok == m, scores[:, m * lanes:(m + 1) * lanes], mine)
            mine = mine * (head ** -0.5)
            mine = jnp.where(same_head & (key_pos <= pc_buf[rows, :]), mine, -1e30)
            e = jnp.exp(mine - jnp.max(mine, axis=1, keepdims=True))
            probs = (e / jnp.sum(e, axis=1, keepdims=True)).astype(BF16).astype(F32)
            wide = jnp.concatenate([jnp.where(q_tok == m, probs, 0.0) for m in range(TOK_SUB)], axis=1).astype(BF16)
            vals = jnp.concatenate([v_buf[c, toks].reshape(TOK_SUB * per_tok, lanes) for c in range(2)], axis=1)
            out = jnp.dot(wide, vals, preferred_element_type=F32).astype(BF16).astype(F32)
            o_buf[0, rows, :] = out[:, :lanes]
            o_buf[1, rows, :] = out[:, lanes:]
        for copy in copies(t, (ko_hbm, vo_hbm), out_sems, True):
            copy.start()
        return carry

    lax.fori_loop(0, steps, step, 0)
    attn = jnp.concatenate([o_buf.at[c][pl.ds(h, n_tok, stride=2), :] for h in range(n_heads) for c in range(2)], axis=1).astype(BF16)
    width = part_ref.shape[1]
    for n0 in range(0, width, 768):
        part_ref[:, n0:n0 + 768] = jnp.dot(attn, wo_ref[0, :, n0:n0 + 768], preferred_element_type=F32).astype(BF16)
    for t in range(steps):
        for copy in copies(t, (ko_hbm, vo_hbm), out_sems, True):
            copy.wait()


class Reducer:
    def __init__(self, part, from_other, chip_sum, far_in, near_in, last_in, send_sems, recv_sems):
        self.part, self.from_other, self.chip_sum = part, from_other, chip_sum
        self.far_in, self.near_in, self.last_in = far_in, near_in, last_in
        self.send_sems, self.recv_sems = send_sems, recv_sems
        self.me, self.core, self.chip, self.other, self.right, self.left = places()
        self.sends = []

    def copy(self, kind, j, cols, way):
        nxt, prv = (self.right, self.left) if way > 0 else (self.left, self.right)
        ahead = lax.rem(self.chip + CHIPS + way, CHIPS)
        behind = lax.rem(self.chip + CHIPS - way, CHIPS)
        opposite = lax.rem(self.chip + 2, CHIPS)
        src, dst, peer = (
            (self.part.at[:, 1 - self.core, :, cols], self.from_other.at[:, :, cols], self.other),
            (self.chip_sum.at[opposite, :, cols], self.far_in.at[:, cols], nxt),
            (self.chip_sum.at[behind, :, cols], self.near_in.at[:, cols], prv),
            (self.chip_sum.at[ahead, :, cols], self.last_in.at[:, cols], nxt),
        )[kind]
        return remote(src, dst, self.send_sems.at[kind, j], self.recv_sems.at[kind, j], peer)

    def go(self, kind, j, cols, way):
        copy = self.copy(kind, j, cols, way)
        copy.start()
        self.sends.append(copy)

    def begin(self, j, cols, way):
        self.go(0, j, cols, way)

    def add_chip(self, k, cols):
        total = self.part[k, self.core, :, cols].astype(F32) + self.from_other[k, :, cols].astype(F32)
        self.chip_sum[k, :, cols] = total.astype(BF16)

    def second(self, j, cols, way):
        self.copy(0, j, cols, way).wait_recv()
        self.add_chip(lax.rem(self.chip + 2, CHIPS), cols)
        self.go(1, j, cols, way)
        self.add_chip(lax.rem(self.chip + CHIPS - way, CHIPS), cols)
        self.go(2, j, cols, way)

    def third(self, j, cols, way):
        ahead = lax.rem(self.chip + CHIPS + way, CHIPS)
        mine = self.part[ahead, self.core, :, cols].astype(F32) + self.from_other[ahead, :, cols].astype(F32)
        self.copy(1, j, cols, way).wait_recv()
        self.chip_sum[ahead, :, cols] = (mine + self.far_in[:, cols].astype(F32)).astype(BF16)
        self.go(3, j, cols, way)

    def last(self, j, cols, way):
        own = self.part[self.chip, self.core, :, cols].astype(F32) + self.from_other[self.chip, :, cols].astype(F32)
        self.copy(2, j, cols, way).wait_recv()
        own = own + self.near_in[:, cols].astype(F32)
        self.copy(3, j, cols, way).wait_recv()
        return own + self.last_in[:, cols].astype(F32)

    def finish(self):
        for copy in self.sends:
            copy.wait_send()


def mlp_kernel(part1, x_buf, gain_ref, w1_hbm, w3_hbm, w2_hbm, out_ref,
               other1, sum1, far1, near1, last1, part2, other2, sum2, far2, near2, last2,
               x1_buf, h_buf, act_buf, w1_buf, w3_buf, w2_buf,
               w_sems, rs1_send, rs1_recv, ag_send, ag_recv, rs2_send, rs2_recv):
    me, core, chip, other, right, left = places()
    width = x_buf.shape[1]
    n_chunks = w1_buf.shape[0]
    chunk = w1_buf.shape[2]

    def weight(kind, i):
        src = (w1_hbm, w3_hbm, w2_hbm)[kind]
        dst = (w1_buf, w3_buf, w2_buf)[kind]
        return pltpu.make_async_copy(src.at[0, :, pl.ds(pl.multiple_of(i * chunk, 128), chunk)], dst.at[i], w_sems.at[kind, i])

    for i in range(n_chunks):
        weight(0, i).start()
        weight(1, i).start()
    for i in range(n_chunks):
        weight(2, i).start()

    enter(other, right, left)
    half = width // 2
    plan1 = [(0, pl.ds(0, half), 1), (1, pl.ds(half, half), -1)]
    rs1 = Reducer(part1, other1, sum1, far1, near1, last1, rs1_send, rs1_recv)
    for stage in (rs1.begin, rs1.second, rs1.third):
        for item in plan1:
            stage(*item)
    for item in plan1:
        cols = item[1]
        x1_buf[:, cols] = (x_buf[:, cols].astype(F32) + rs1.last(*item)).astype(BF16)
    h_buf[me] = norm_rows(x1_buf[...].astype(F32), gain_ref[...].astype(F32))
    gather_rows(h_buf, ag_send, ag_recv)

    n_tok = act_buf.shape[0]

    def gate_up(i, carry):
        weight(0, i).wait()
        weight(1, i).wait()
        h_all = h_buf[...].reshape(n_tok, width)
        gate = jnp.dot(h_all, w1_buf[i], preferred_element_type=F32)
        up = jnp.dot(h_all, w3_buf[i], preferred_element_type=F32)
        act_buf[:, pl.ds(pl.multiple_of(i * chunk, 128), chunk)] = (gate * jax.nn.sigmoid(gate) * up).astype(BF16)
        return carry

    lax.fori_loop(0, n_chunks, gate_up, 0)

    rs2 = Reducer(part2, other2, sum2, far2, near2, last2, rs2_send, rs2_recv)
    plan2 = [(j, pl.ds(j * chunk, chunk), 1 if j % 2 == 0 else -1) for j in range(n_chunks)]

    def final(item):
        cols = item[1]
        out_ref[:, cols] = (x1_buf[:, cols].astype(F32) + rs2.last(*item)).astype(BF16)

    for j in range(n_chunks + 4):
        if j < n_chunks:
            weight(2, j).wait()
            down = jnp.dot(act_buf[...], w2_buf[j], preferred_element_type=F32).astype(BF16)
            part2[:, :, :, plan2[j][1]] = down.reshape(CHIPS, 2, n_tok // (2 * CHIPS), chunk)
            rs2.begin(*plan2[j])
        for lag, stage in ((1, rs2.second), (3, rs2.third), (4, final)):
            if 0 <= j - lag < n_chunks:
                stage(*plan2[j - lag]) if lag != 4 else final(plan2[j - lag])
    rs1.finish()
    rs2.finish()


def shape(dims, dtype=BF16):
    return jax.ShapeDtypeStruct(dims, dtype)


def run_qkv(x, gain, pos2, wq, wk, wv):
    n_tok = pos2.shape[1]
    rows, width = x.shape
    cols = wq.shape[2]
    blocks = n_tok // rows
    dma = pltpu.SemaphoreType.DMA
    return pl.pallas_call(
        qkv_kernel,
        out_shape=[shape((n_tok, cols))] * 3,
        in_specs=[HBM] * 6,
        out_specs=[VMEM] * 3,
        scratch_shapes=[
            pltpu.VMEM((rows, width), BF16), pltpu.VMEM(gain.shape, BF16), pltpu.VMEM(pos2.shape, pos2.dtype),
            pltpu.VMEM((blocks, rows, width), BF16), pltpu.VMEM((3, width, cols), BF16),
            dma((6,)), dma((GATHER_SEMS,)), dma((GATHER_SEMS,))],
        compiler_params=pltpu.CompilerParams(collective_id=0, has_side_effects=True, vmem_limit_bytes=32 << 20),
        name='gather_qkv',
    )(x, gain, pos2, wq, wk, wv)


def run_attn(pos2, q, k, v, wo, k_cache, v_cache):
    _, n_tok, n_rows, n_heads, head = k_cache.shape
    width = wo.shape[2]
    steps = n_tok // TOK_STEP
    dma = pltpu.SemaphoreType.DMA
    cache = pltpu.VMEM((2, n_tok, n_rows * n_heads, 128), BF16)
    wide = pltpu.VMEM((2, n_tok * n_heads, 128), F32)
    return pl.pallas_call(
        attn_kernel,
        out_shape=[shape((n_tok, width)), shape(k_cache.shape), shape(v_cache.shape)],
        in_specs=[SMEM, VMEM, VMEM, VMEM, VMEM, VMEM, HBM, HBM],
        out_specs=[VMEM, HBM, HBM],
        scratch_shapes=[
            cache, cache, pltpu.VMEM((2, n_heads, 2, n_tok, 128), F32), wide, wide, pltpu.VMEM((n_tok * n_heads, n_tok), F32),
            dma((2, 2, steps)), dma((2, 2, steps))],
        compiler_params=pltpu.CompilerParams(vmem_limit_bytes=48 << 20),
        name='attention',
    )(pos2, pos2, q, k, v, wo, k_cache, v_cache)


def run_mlp(part, x, gain, w1, w3, w2):
    rows, width = x.shape
    n_tok = part.shape[1] * part.shape[0] * part.shape[2]
    ffn = w1.shape[2]
    chunk = MLP_CHUNK
    n_chunks = ffn // chunk
    dma = pltpu.SemaphoreType.DMA
    block = pltpu.VMEM((rows, width), BF16)
    reduce_bufs = [pltpu.VMEM((CHIPS, 2, rows, width), BF16), pltpu.VMEM((CHIPS, rows, width), BF16), pltpu.VMEM((CHIPS, rows, width), BF16)] + [block] * 3
    return pl.pallas_call(
        mlp_kernel,
        out_shape=shape((rows, width)),
        in_specs=[VMEM, VMEM, VMEM, HBM, HBM, HBM],
        out_specs=VMEM,
        scratch_shapes=reduce_bufs[1:] + reduce_bufs + [
            block, pltpu.VMEM((n_tok // rows, rows, width), BF16), pltpu.VMEM((n_tok, ffn), BF16),
            pltpu.VMEM((n_chunks, width, chunk), BF16), pltpu.VMEM((n_chunks, width, chunk), BF16), pltpu.VMEM((width // chunk, ffn, chunk), BF16),
            dma((3, n_chunks)), dma((4, 2)), dma((4, 2)), dma((GATHER_SEMS,)), dma((GATHER_SEMS,)),
            dma((4, n_chunks)), dma((4, n_chunks))],
        compiler_params=pltpu.CompilerParams(collective_id=1, has_side_effects=True, vmem_limit_bytes=MLP_VMEM),
        name='reduce_mlp',
    )(part, x, gain, w1, w3, w2)


def solution(mesh):
    row_spec = P(('data', 'model'), None)
    cache_spec = P(None, 'data', None, 'model', None)
    col_spec = P(None, None, 'model')
    inner_spec = P(None, 'model', None)
    in_specs = (row_spec, P('data'), P(), P(), col_spec, col_spec, col_spec, inner_spec, col_spec, col_spec, inner_spec, cache_spec, cache_spec)
    out_specs = (row_spec, cache_spec, cache_spec)

    def device_step(hidden, positions, attn_gain, mlp_gain, w_query, w_key, w_value, w_out, w_gate, w_up, w_down, k_cache, v_cache):
        rows, width = hidden.shape
        n_tok = positions.shape[0]
        pos2 = positions.reshape(1, n_tok)
        q, k, v = run_qkv(hidden, attn_gain, pos2, w_query, w_key, w_value)
        part, k_out, v_out = run_attn(pos2, q, k, v, w_out, k_cache, v_cache)
        out = run_mlp(part.reshape(CHIPS, 2, rows, width), hidden, mlp_gain, w_gate, w_up, w_down)
        return out, k_out, v_out

    return jax.shard_map(device_step, mesh=mesh, in_specs=in_specs, out_specs=out_specs, check_vma=False)
```

time: 225 us -> 81.5 us (0.36); the launches traced: 221 us -> 80.9 us
  Pallas kernels: 0 us -> 69.9 us
  waiting for transfers between devices: 60.1 us -> 0 us
  matrix products: 48.1 us -> 0 us
  blocking collectives: 41.6 us -> 0 us
  local copies, waits for them, and re-layouts: 51 us -> 10.3 us
  between operations: 14.3 us -> 0.7 us
  other arithmetic: 6.19 us -> 0 us
    pallas_call x0 -> x3, Pallas kernels: none -> 69.9 us  [the longest x1 41.4 us: run_mlp(): pl.pallas_call(mlp_kernel, out_shape=shape((rows, width)), in_specs=[VMEM...]
    reduce_scatter x2 -> x0, waiting for transfers between devices: 60 us -> none  [device_step(): summed = lax.psum_scatter(partial, 'model', scatter_dimension=0, tiled=True)]
    dot_general x8 -> x0, matrix products: 48.1 us -> none  [the longest x1 18.8 us: device_step(): jnp.dot(mlp_act, w_down[layer_idx], preferred_element_type=jnp.float32)]
    all_gather x2 -> x0, blocking collectives: 41.6 us -> none  [device_step(): gathered = lax.all_gather(normed, 'model', axis=0, tiled=True)]
    scatter x2 -> x0, local copies, waits for them, and re-layouts: 32.8 us -> none  [the longest x1 16.4 us: device_step(): v_cache = v_cache.at[layer_idx, row_ids, positions].set(values_new)]
    unnamed x27 -> x19, local copies, waits for them, and re-layouts: 15 us -> 10.3 us
    convert_element_type x4 -> x0, other arithmetic: 2.66 us -> none  [the longest x1 1.57 us: device_step(): (hidden.astype(jnp.float32) + summed.astype(jnp.float32)).astype(jnp.bflo...]
    reshape x2 -> x0, local copies, waits for them, and re-layouts: 2.55 us -> none  [the longest x1 1.6 us: device_step(): queries.reshape(n_tokens, local_kv, group_size, head_dim)]
  transfers between devices with their start and end apart: 2 -> 0, of which waited for: 2 -> 0; matrix products, arithmetic and copies ran while one was open for 0% -> 0% of each run, Pallas kernels for 0% -> 0%
where the time goes in v1:
time: 81.5 us; the launch traced here: 80.9 us
  Pallas kernels  69.9 us (86%)
  local copies, waits for them, and re-layouts  10.3 us (13%)
    pallas_call x1, Pallas kernels, run_mlp(): pl.pallas_call(mlp_kernel, out_shape=shape((rows, width)), in_specs=[VMEM...  41.4 us
    pallas_call x1, Pallas kernels, run_qkv(): pl.pallas_call(qkv_kernel, out_shape=[shape((n_tok, cols))] * 3, in_specs...  14.9 us
    pallas_call x1, Pallas kernels, run_attn(): pl.pallas_call(attn_kernel, out_shape=[shape((n_tok, width)), shape(k_cac...  13.5 us
    unnamed x19, local copies, waits for them, and re-layouts  10.3 us

profile of v1, /device:TPU:113, one launch (start us, length us, event | category | flops | bytes accessed | tf_op | source)
XLA Modules:
  0.0 80.9 jit_solution(3157428079859340874)
XLA Ops:
  0.6 0.0 copy-start.8
  0.6 0.0 copy-start
  0.7 1.9 %copy-done = bf16[1,3072,512]{2,1,0:T(8,128)(2,1)S(1)} copy-done((bf16[1,3072,512]{2,1,0:T(8,128)(2,1)S(1)}, bf16[1,3072,512]{2,1,0:T(8,128)(2,1)}, u32[]{:S(2)}) %copy-start) | copy-done | bytes 3145752
  2.5 0.0 copy-start.1
  2.5 1.9 %copy-done.1 = bf16[1,3072,512]{2,1,0:T(8,128)(2,1)S(1)} copy-done((bf16[1,3072,512]{2,1,0:T(8,128)(2,1)S(1)}, bf16[1,3072,512]{2,1,0:T(8,128)(2,1)}, u32[]{:S(2)}) %copy-start.1) | copy-done | bytes 3145752
  4.4 0.0 copy-start.2
  4.4 1.9 %copy-done.2 = bf16[1,3072,512]{2,1,0:T(8,128)(2,1)S(1)} copy-done((bf16[1,3072,512]{2,1,0:T(8,128)(2,1)S(1)}, bf16[1,3072,512]{2,1,0:T(8,128)(2,1)}, u32[]{:S(2)}) %copy-start.2) | copy-done | bytes 3145752
  6.3 0.0 copy-start.5
  6.3 0.9 %copy-done.5 = bf16[16,3072]{1,0:T(8,128)(2,1)S(1)} copy-done((bf16[16,3072]{1,0:T(8,128)(2,1)S(1)}, bf16[16,3072]{1,0:T(8,128)(2,1)}, u32[]{:S(2)}) %copy-start.5) | copy-done | bytes 98328
  7.2 0.0 copy-start.6
  7.2 0.7 copy-done.6
  7.9 0.0 copy-start.7
  7.9 0.7 copy-done.7
  8.6 0.0 copy-start.3
  8.6 14.9 %gather_qkv.1 = (bf16[128,512]{1,0:T(8,128)(2,1)S(1)}, bf16[128,512]{1,0:T(8,128)(2,1)S(1)}, bf16[128,512]{1,0:T(8,128)(2,1)S(1)}) custom-call(bf16[16,3072]{1,0:T(8,128)(2,1)S(1)} %copy-done.5, bf16[1,3072]{1,0:T(2,128)(2,1)S(1)} %copy-done.6, s32[1,128]{1,0:T(1,128)S(1)} %bitcast.3, bf16[1,3072,512]{2,1,0:T(8,128)(2,1)S(1)} %copy-done, ...), custom_call_target="tpu_custom_call" | custom-call | tf_op jit(solution)/shard_map/gather_qkv/pallas_call | solution.py:368
  23.5 0.0 copy-done.8
  23.5 0.0 copy-done.3
  23.5 13.5 %attention.1 = (bf16[128,3072]{1,0:T(8,128)(2,1)S(1)}, bf16[1,128,64,2,256]{4,3,2,1,0:T(2,128)(2,1)}, bf16[1,128,64,2,256]{4,3,2,1,0:T(2,128)(2,1)}) custom-call(s32[1,128]{1,0:T(1,128)S(1)} %bitcast.4, s32[1,128]{1,0:T(1,128)S(1)} %bitcast.5, bf16[128,512]{1,0:T(8,128)(2,1)S(1)} %get-tuple-element.9.q_ref, bf16[128,512]{1,0:T(8,128)(2,1)S(1)} %get-tuple-element.10.k_ref, ...), custom_call_target="tpu_custom_call" | custom-call | tf_op jit(solution)/shard_map/attention/pallas_call | solution.py:389
  37.0 0.0 copy-start.4
  37.1 0.9 %copy-done.4 = bf16[128,3072]{1,0:T(8,128)(2,1)} copy-done((bf16[128,3072]{1,0:T(8,128)(2,1)}, bf16[128,3072]{1,0:T(8,128)(2,1)S(1)}, u32[]{:S(2)}) %copy-start.4) | copy-done | bytes 786456
  37.9 41.4 %reduce_mlp.1 = bf16[16,3072]{1,0:T(8,128)(2,1)} custom-call(bf16[4,2,16,3072]{3,2,1,0:T(8,128)(2,1)} %bitcast.2, bf16[16,3072]{1,0:T(8,128)(2,1)} %x_buf.1, bf16[1,3072]{1,0:T(2,128)(2,1)} %gain_ref.1, bf16[1,3072,3072]{2,1,0:T(8,128)(2,1)} %w1_hbm.1, bf16[1,3072,3072]{2,1,0:T(8,128)(2,1)} %w3_hbm.1, bf16[1,3072,3072]{2,1,0:T(8,128)(2,1)} %w2_hbm.1), custom_call_target="tpu_custom_call" | custom-call | tf_op jit(solution)/shard_map/reduce_mlp/pallas_call | solution.py:411
  79.4 1.5 %copy.17 = bf16[16,3072]{1,0:T(8,128)(2,1)} copy(bf16[16,3072]{1,0:T(8,128)(2,1)} %reduce_mlp.1) | data formatting | bytes 196608
Async XLA Ops:
  0.6 22.9 %copy-start.8 = (s32[128]{0:T(128)S(1)}, s32[128]{0:T(128)}, u32[]{:S(2)}) copy-start(s32[128]{0:T(128)} %param.14) | copy-start | bytes 1540
  0.6 1.9 %copy-start = (bf16[1,3072,512]{2,1,0:T(8,128)(2,1)S(1)}, bf16[1,3072,512]{2,1,0:T(8,128)(2,1)}, u32[]{:S(2)}) copy-start(bf16[1,3072,512]{2,1,0:T(8,128)(2,1)} %wq_hbm.1) | copy-start | bytes 9437188
  2.5 1.9 %copy-start.1 = (bf16[1,3072,512]{2,1,0:T(8,128)(2,1)S(1)}, bf16[1,3072,512]{2,1,0:T(8,128)(2,1)}, u32[]{:S(2)}) copy-start(bf16[1,3072,512]{2,1,0:T(8,128)(2,1)} %wk_hbm.1) | copy-start | bytes 9437188
  4.4 1.9 %copy-start.2 = (bf16[1,3072,512]{2,1,0:T(8,128)(2,1)S(1)}, bf16[1,3072,512]{2,1,0:T(8,128)(2,1)}, u32[]{:S(2)}) copy-start(bf16[1,3072,512]{2,1,0:T(8,128)(2,1)} %wv_hbm.1) | copy-start | bytes 9437188
  6.3 0.9 %copy-start.5 = (bf16[16,3072]{1,0:T(8,128)(2,1)S(1)}, bf16[16,3072]{1,0:T(8,128)(2,1)}, u32[]{:S(2)}) copy-start(bf16[16,3072]{1,0:T(8,128)(2,1)} %x_buf.1) | copy-start | bytes 294916
  7.2 0.7 copy-start.6
  7.9 0.7 copy-start.7
  8.6 15.0 %copy-start.3 = (bf16[1,512,3072]{2,1,0:T(8,128)(2,1)S(1)}, bf16[1,512,3072]{2,1,0:T(8,128)(2,1)}, u32[]{:S(2)}) copy-start(bf16[1,512,3072]{2,1,0:T(8,128)(2,1)} %wo_ref.1) | copy-start | bytes 9437188
  37.0 0.9 %copy-start.4 = (bf16[128,3072]{1,0:T(8,128)(2,1)}, bf16[128,3072]{1,0:T(8,128)(2,1)S(1)}, u32[]{:S(2)}) copy-start(bf16[128,3072]{1,0:T(8,128)(2,1)S(1)} %get-tuple-element.12) | copy-start | bytes 2359300

commit v2 on v1

v2 whole, which is shorter than its diff:
```python
import functools
import math
import jax
import jax.numpy as jnp
from jax import lax
from jax.experimental import pallas as pl
from jax.experimental.pallas import tpu as pltpu
from jax.sharding import PartitionSpec as P

NORM_EPS = 1e-5
ROPE_BASE = 10000.0
BF16 = jnp.bfloat16
F32 = jnp.float32
VMEM = pl.BlockSpec(memory_space=pltpu.VMEM)
SMEM = pl.BlockSpec(memory_space=pltpu.SMEM)
HBM = pl.BlockSpec(memory_space=pltpu.HBM)
MLP_VMEM = 63400000
CHIPS = 4
MLP_CHUNK = 512
RS1_PIECES = 4
RS2_LAG = 3
GATHER_SEMS = 21


def places():
    me = lax.axis_index('model')
    core = lax.rem(me, 2)
    chip = lax.div(me, 2)
    other = me + 1 - 2 * core
    right = lax.rem(chip + 1, CHIPS) * 2 + core
    left = lax.rem(chip + CHIPS - 1, CHIPS) * 2 + core
    return me, core, chip, other, right, left


def knock(other, right, left):
    barrier = pltpu.get_barrier_semaphore()
    for peer in (other, right, left):
        pl.semaphore_signal(barrier, inc=1, device_id={'model': peer})


def enter():
    pl.semaphore_wait(pltpu.get_barrier_semaphore(), 3)


def remote(src, dst, send_sem, recv_sem, peer):
    return pltpu.make_async_remote_copy(src_ref=src, dst_ref=dst, send_sem=send_sem, recv_sem=recv_sem, device_id={'model': peer})


def norm_rows(x_f, gain_f):
    inv_rms = lax.rsqrt(jnp.mean(x_f * x_f, axis=-1, keepdims=True) + NORM_EPS)
    return (x_f * inv_rms * gain_f).astype(BF16)


def gather_rows(buf, send_sems, recv_sems):
    me, core, chip, other, right, left = places()
    width = buf.shape[2]
    quarter = width // 4
    q0, q1, q2, q3 = (pl.ds(i * quarter, quarter) for i in range(4))
    lo, hi, full = pl.ds(0, 2 * quarter), pl.ds(2 * quarter, 2 * quarter), pl.ds(0, width)
    far = lax.rem(chip + 2, CHIPS) * 2 + core
    sends = []

    def hop(blk, cols, idx, peer):
        view = buf.at[blk, :, cols]
        return remote(view, view, send_sems.at[idx], recv_sems.at[idx], peer)

    def arrive(blk, cols, idx):
        hop(blk, cols, idx, other).wait_recv()

    def send(blk, cols, idx, peer):
        copy = hop(blk, cols, idx, peer)
        copy.start()
        sends.append(copy)

    for cols, idx, peer in ((q0, 0, right), (q2, 1, left), (q1, 2, right), (q3, 3, left), (hi, 4, right), (lo, 5, left), (full, 6, other)):
        send(me, cols, idx, peer)
    across = []
    for blk, cols, idx, onward, peer in (
            (left, q0, 0, 7, right), (right, q2, 1, 8, left), (left, q1, 2, 9, right), (right, q3, 3, 10, left),
            (left, hi, 4, None, None), (right, lo, 5, None, None),
            (far, q0, 7, None, None), (far, q2, 8, None, None), (far, q1, 9, None, None), (far, q3, 10, None, None)):
        arrive(blk, cols, idx)
        if onward is not None:
            send(blk, cols, onward, peer)
        send(blk, cols, 11 + len(across), other)
        across.append((blk + 1 - 2 * core, cols, 11 + len(across)))
    arrive(other, full, 6)
    for item in across:
        arrive(*item)
    for copy in sends:
        copy.wait_send()


LANES = 128


def cache_copies(hbm, buf, sems, start, size, outward=False):
    _, n_tok, n_rows, n_heads, head = hbm.shape
    flat = hbm.reshape(1, n_tok, n_rows * n_heads, head)
    made = []
    for c in range(2):
        far = flat.at[0, pl.ds(start, size), :, pl.ds(c * LANES, LANES)]
        near = buf.at[c, pl.ds(start, size)]
        src, dst = (near, far) if outward else (far, near)
        made.append(pltpu.make_async_copy(src, dst, sems.at[c]))
    return made


def qkv_kernel(x_hbm, gain_hbm, pos_hbm, wq_hbm, wk_hbm, wv_hbm, kc_hbm, vc_hbm, q_ref, k_ref, v_ref, kb_ref, vb_ref,
               x_buf, gain_ref, pos_ref, h_buf, w_buf, load_sems, cache_sems, send_sems, recv_sems):
    me, core, chip, other, right, left = places()
    knock(other, right, left)
    loads = [pltpu.make_async_copy(src, dst, load_sems.at[3 + i]) for i, (src, dst) in enumerate(((x_hbm, x_buf), (gain_hbm, gain_ref), (pos_hbm, pos_ref)))]
    w_copies = [pltpu.make_async_copy(w.at[0], w_buf.at[i], load_sems.at[i]) for i, w in enumerate((wq_hbm, wk_hbm, wv_hbm))]
    piece = kb_ref.shape[1] // 2
    cache_in = []
    for kv, (hbm, buf) in enumerate(((kc_hbm, kb_ref), (vc_hbm, vb_ref))):
        for p in range(2):
            for c in range(2):
                src = hbm.at[0, pl.ds(p * piece, piece), :, :, pl.ds(c * LANES, LANES)]
                cache_in.append(pltpu.make_async_copy(src, buf.at[c, pl.ds(p * piece, piece)], cache_sems.at[kv, p, c]))
    for copy in loads + w_copies + cache_in:
        copy.start()
    for copy in loads:
        copy.wait()
    h_buf[me] = norm_rows(x_buf[...].astype(F32), gain_ref[...].astype(F32))
    enter()
    gather_rows(h_buf, send_sems, recv_sems)

    n_tok = pos_ref.shape[1]
    half = 128
    head = 2 * half
    pos_row = jnp.broadcast_to(pos_ref[...].astype(F32), (n_tok, n_tok))
    diag = lax.broadcasted_iota(jnp.int32, (n_tok, n_tok), 0) == lax.broadcasted_iota(jnp.int32, (n_tok, n_tok), 1)
    pos_col = jnp.sum(jnp.where(diag, pos_row, 0.0), axis=1, keepdims=True)
    lane = lax.broadcasted_iota(jnp.int32, (n_tok, half), 1).astype(F32)
    angles = pos_col * jnp.exp(lane * (-2.0 * math.log(ROPE_BASE) / head))
    cos_tab, sin_tab = jnp.cos(angles), jnp.sin(angles)
    h_all = h_buf[...].reshape(n_tok, h_buf.shape[2])
    for i, out_ref in enumerate((q_ref, k_ref, v_ref)):
        w_copies[i].wait()
        proj = jnp.dot(h_all, w_buf[i], preferred_element_type=F32).astype(BF16)
        if i == 2:
            out_ref[...] = proj
            continue
        for h0 in range(0, proj.shape[1], head):
            front = proj[:, h0:h0 + half].astype(F32)
            back = proj[:, h0 + half:h0 + head].astype(F32)
            out_ref[:, h0:h0 + half] = (front * cos_tab - back * sin_tab).astype(BF16)
            out_ref[:, h0 + half:h0 + head] = (back * cos_tab + front * sin_tab).astype(BF16)
    for copy in cache_in:
        copy.wait()


TOK_STEP = 16
TOK_SUB = 8


def attn_kernel(pos_smem, pos_ref, q_ref, k_ref, v_ref, kb_in, vb_in, attn_ref, k_buf, v_buf, ko_hbm, vo_hbm,
                new_buf, q_buf, o_buf, pc_buf, out_sems):
    _, n_tok, n_rows, n_heads, head = ko_hbm.shape
    lanes = LANES
    steps = n_tok // TOK_STEP
    per_tok = n_rows * n_heads
    bufs = (k_buf, v_buf)

    def write_out(t):
        made = []
        for kv, hbm in enumerate((ko_hbm, vo_hbm)):
            made += cache_copies(hbm, bufs[kv], out_sems.at[kv, t], t * TOK_STEP, TOK_STEP, True)
        return made

    for h in range(n_heads):
        for c in range(2):
            cols = slice(h * head + c * lanes, h * head + (c + 1) * lanes)
            q_buf.at[c][pl.ds(h, n_tok, stride=2), :] = q_ref[:, cols].astype(F32)
            new_buf[0, h, c] = k_ref[:, cols].astype(F32)
            new_buf[1, h, c] = v_ref[:, cols].astype(F32)
    rows2 = n_tok * n_heads
    pos_row = jnp.broadcast_to(pos_ref[...].astype(F32), (rows2, n_tok))
    own = lax.broadcasted_iota(jnp.int32, (rows2, n_tok), 0) // 2 == lax.broadcasted_iota(jnp.int32, (rows2, n_tok), 1)
    pc_buf[...] = jnp.broadcast_to(jnp.sum(jnp.where(own, pos_row, 0.0), axis=1, keepdims=True), (rows2, n_tok))

    tile_row = lax.broadcasted_iota(jnp.int32, (16, lanes), 0)
    sub_rows = TOK_SUB * n_heads
    q_row = lax.broadcasted_iota(jnp.int32, (sub_rows, lanes), 0)
    key_col = lax.broadcasted_iota(jnp.int32, (sub_rows, lanes), 1)
    same_head = (q_row % 2) == (key_col % 2)
    key_pos = (key_col // 2).astype(F32)
    q_tok = q_row // 2

    def step(t, carry):
        for i in range(TOK_STEP):
            b = t * TOK_STEP + i
            pos = pos_smem[0, b]
            tile = pl.ds(pl.multiple_of((pos >> 3) * 16, 16), 16)
            hit = (tile_row >> 1) == (pos & 7)
            for kv in range(2):
                for c in range(2):
                    old = bufs[kv][c, b, tile, :].astype(F32)
                    new = jnp.where((tile_row & 1) == 1, new_buf[kv, 1, c, pl.ds(b, 1), :], new_buf[kv, 0, c, pl.ds(b, 1), :])
                    bufs[kv][c, b, tile, :] = jnp.where(hit, new, old).astype(BF16)
        for sub in range(TOK_STEP // TOK_SUB):
            b0 = t * TOK_STEP + sub * TOK_SUB
            rows = pl.ds(pl.multiple_of(b0 * n_heads, 16), sub_rows)
            toks = pl.ds(b0, TOK_SUB)
            q = jnp.concatenate([q_buf[0, rows, :], q_buf[1, rows, :]], axis=1).astype(BF16)
            keys = jnp.concatenate([k_buf[c, toks].reshape(TOK_SUB * per_tok, lanes) for c in range(2)], axis=1)
            scores = lax.dot_general(q, keys, (((1,), (1,)), ((), ())), preferred_element_type=F32)
            mine = jnp.zeros((sub_rows, lanes), F32)
            for m in range(TOK_SUB):
                mine = jnp.where(q_tok == m, scores[:, m * lanes:(m + 1) * lanes], mine)
            mine = mine * (head ** -0.5)
            mine = jnp.where(same_head & (key_pos <= pc_buf[rows, :]), mine, -1e30)
            e = jnp.exp(mine - jnp.max(mine, axis=1, keepdims=True))
            probs = (e / jnp.sum(e, axis=1, keepdims=True)).astype(BF16).astype(F32)
            wide = jnp.concatenate([jnp.where(q_tok == m, probs, 0.0) for m in range(TOK_SUB)], axis=1).astype(BF16)
            vals = jnp.concatenate([v_buf[c, toks].reshape(TOK_SUB * per_tok, lanes) for c in range(2)], axis=1)
            out = jnp.dot(wide, vals, preferred_element_type=F32).astype(BF16).astype(F32)
            o_buf[0, rows, :] = out[:, :lanes]
            o_buf[1, rows, :] = out[:, lanes:]
        for copy in write_out(t):
            copy.start()
        return carry

    lax.fori_loop(0, steps, step, 0)
    attn_ref[...] = jnp.concatenate([o_buf.at[c][pl.ds(h, n_tok, stride=2), :] for h in range(n_heads) for c in range(2)], axis=1).astype(BF16)
    for t in range(steps):
        for copy in write_out(t):
            copy.wait()


class Reducer:
    def __init__(self, part, from_other, chip_sum, far_in, near_in, last_in, send_sems, recv_sems):
        self.part, self.from_other, self.chip_sum = part, from_other, chip_sum
        self.far_in, self.near_in, self.last_in = far_in, near_in, last_in
        self.send_sems, self.recv_sems = send_sems, recv_sems
        self.me, self.core, self.chip, self.other, self.right, self.left = places()
        self.sends = []

    def copy(self, kind, j, cols, way):
        nxt, prv = (self.right, self.left) if way > 0 else (self.left, self.right)
        ahead = lax.rem(self.chip + CHIPS + way, CHIPS)
        behind = lax.rem(self.chip + CHIPS - way, CHIPS)
        opposite = lax.rem(self.chip + 2, CHIPS)
        if kind < 4:
            k = (opposite, behind, ahead, self.chip)[kind]
            src, dst, peer = self.part.at[k, 1 - self.core, :, cols], self.from_other.at[k, :, cols], self.other
        else:
            src, dst, peer = (
                (self.chip_sum.at[opposite, :, cols], self.far_in.at[:, cols], nxt),
                (self.chip_sum.at[behind, :, cols], self.near_in.at[:, cols], prv),
                (self.chip_sum.at[ahead, :, cols], self.last_in.at[:, cols], nxt),
            )[kind - 4]
        return remote(src, dst, self.send_sems.at[kind, j], self.recv_sems.at[kind, j], peer)

    def go(self, kind, j, cols, way):
        copy = self.copy(kind, j, cols, way)
        copy.start()
        self.sends.append(copy)

    def begin(self, j, cols, way):
        for kind in range(4):
            self.go(kind, j, cols, way)

    def pair(self, kind, k, j, cols, way):
        self.copy(kind, j, cols, way).wait_recv()
        return self.part[k, self.core, :, cols].astype(F32) + self.from_other[k, :, cols].astype(F32)

    def far(self, j, cols, way):
        opposite = lax.rem(self.chip + 2, CHIPS)
        self.chip_sum[opposite, :, cols] = self.pair(0, opposite, j, cols, way).astype(BF16)
        self.go(4, j, cols, way)

    def near(self, j, cols, way):
        behind = lax.rem(self.chip + CHIPS - way, CHIPS)
        self.chip_sum[behind, :, cols] = self.pair(1, behind, j, cols, way).astype(BF16)
        self.go(5, j, cols, way)

    def third(self, j, cols, way):
        ahead = lax.rem(self.chip + CHIPS + way, CHIPS)
        mine = self.pair(2, ahead, j, cols, way)
        self.copy(4, j, cols, way).wait_recv()
        self.chip_sum[ahead, :, cols] = (mine + self.far_in[:, cols].astype(F32)).astype(BF16)
        self.go(6, j, cols, way)

    def last(self, j, cols, way):
        own = self.pair(3, self.chip, j, cols, way)
        self.copy(5, j, cols, way).wait_recv()
        own = own + self.near_in[:, cols].astype(F32)
        self.copy(6, j, cols, way).wait_recv()
        return own + self.last_in[:, cols].astype(F32)

    def finish(self):
        for copy in self.sends:
            copy.wait_send()


def mlp_kernel(attn_ref, x_buf, gain_ref, wo_ref, w1_hbm, w3_hbm, w2_hbm, out_ref,
               part, other_in, chip_sum, far_in, near_in, last_in,
               x1_buf, h_buf, act_buf, w1_buf, w3_buf, w2_buf,
               w_sems, rs1_send, rs1_recv, ag_send, ag_recv, rs2_send, rs2_recv):
    me, core, chip, other, right, left = places()
    knock(other, right, left)
    width = x_buf.shape[1]
    n_tok = act_buf.shape[0]
    n_chunks = w1_buf.shape[0]
    chunk = w1_buf.shape[2]

    def weight(kind, i):
        src = (w1_hbm, w3_hbm, w2_hbm)[kind]
        dst = (w1_buf, w3_buf, w2_buf)[kind]
        return pltpu.make_async_copy(src.at[0, :, pl.ds(pl.multiple_of(i * chunk, 128), chunk)], dst.at[i], w_sems.at[kind, i])

    for i in range(n_chunks):
        weight(0, i).start()
        weight(1, i).start()
    for i in range(n_chunks):
        weight(2, i).start()

    def plan(pieces):
        size = width // pieces
        return [(j, pl.ds(j * size, size), 1 if j % 2 == 0 else -1) for j in range(pieces)]

    def put_part(cols, value):
        part[:, :, :, cols] = value.astype(BF16).reshape(CHIPS, 2, n_tok // (2 * CHIPS), value.shape[1])

    plan1 = plan(RS1_PIECES)
    rs1 = Reducer(part, other_in, chip_sum, far_in, near_in, last_in, rs1_send, rs1_recv)
    attn = attn_ref[...]
    for item in plan1:
        put_part(item[1], jnp.dot(attn, wo_ref[0, :, item[1]], preferred_element_type=F32))
        if item[0] == 0:
            enter()
        rs1.begin(*item)
    for stage in (rs1.far, rs1.near, rs1.third):
        for item in plan1:
            stage(*item)
    for item in plan1:
        cols = item[1]
        x1_buf[:, cols] = (x_buf[:, cols].astype(F32) + rs1.last(*item)).astype(BF16)
    rs1.finish()
    h_buf[me] = norm_rows(x1_buf[...].astype(F32), gain_ref[...].astype(F32))
    gather_rows(h_buf, ag_send, ag_recv)

    def gate_up(i, carry):
        weight(0, i).wait()
        weight(1, i).wait()
        h_all = h_buf[...].reshape(n_tok, width)
        gate = jnp.dot(h_all, w1_buf[i], preferred_element_type=F32)
        up = jnp.dot(h_all, w3_buf[i], preferred_element_type=F32)
        act_buf[:, pl.ds(pl.multiple_of(i * chunk, 128), chunk)] = (gate * jax.nn.sigmoid(gate) * up).astype(BF16)
        return carry

    lax.fori_loop(0, n_chunks, gate_up, 0)

    rs2 = Reducer(part, other_in, chip_sum, far_in, near_in, last_in, rs2_send, rs2_recv)
    plan2 = plan(n_chunks)
    for j in range(n_chunks + RS2_LAG):
        if j < n_chunks:
            weight(2, j).wait()
            put_part(plan2[j][1], jnp.dot(act_buf[...], w2_buf[j], preferred_element_type=F32))
            rs2.begin(*plan2[j])
        if j >= RS2_LAG:
            rs2.far(*plan2[j - RS2_LAG])
            rs2.near(*plan2[j - RS2_LAG])
    for item in plan2:
        rs2.third(*item)
    for item in plan2:
        cols = item[1]
        out_ref[:, cols] = (x1_buf[:, cols].astype(F32) + rs2.last(*item)).astype(BF16)
    rs2.finish()


def shape(dims, dtype=BF16):
    return jax.ShapeDtypeStruct(dims, dtype)


def run_qkv(x, gain, pos2, wq, wk, wv, k_cache, v_cache):
    _, n_tok, n_rows, n_heads, head = k_cache.shape
    rows, width = x.shape
    cols = wq.shape[2]
    blocks = n_tok // rows
    dma = pltpu.SemaphoreType.DMA
    args = (x, gain, pos2, wq, wk, wv, k_cache, v_cache)
    return pl.pallas_call(
        qkv_kernel,
        out_shape=[shape((n_tok, cols))] * 3 + [shape((2, n_tok, n_rows, n_heads, LANES))] * 2,
        in_specs=[HBM] * len(args),
        out_specs=[VMEM] * 5,
        scratch_shapes=[
            pltpu.VMEM((rows, width), BF16), pltpu.VMEM(gain.shape, BF16), pltpu.VMEM(pos2.shape, pos2.dtype),
            pltpu.VMEM((blocks, rows, width), BF16), pltpu.VMEM((3, width, cols), BF16),
            dma((6,)), dma((2, 2, 2)), dma((GATHER_SEMS,)), dma((GATHER_SEMS,))],
        compiler_params=pltpu.CompilerParams(collective_id=0, has_side_effects=True, vmem_limit_bytes=36 << 20),
        name='gather_qkv',
    )(*(pltpu.with_memory_space_constraint(a, pltpu.HBM) for a in args))


def run_attn(pos2, q, k, v, k_tiles, v_tiles, k_cache, v_cache):
    _, n_tok, n_rows, n_heads, head = k_cache.shape
    steps = n_tok // TOK_STEP
    dma = pltpu.SemaphoreType.DMA
    wide = pltpu.VMEM((2, n_tok * n_heads, LANES), F32)
    k_tiles, v_tiles = (a.reshape(2, n_tok, n_rows * n_heads, LANES) for a in (k_tiles, v_tiles))
    tiles = shape(k_tiles.shape)
    attn, _, _, k_out, v_out = pl.pallas_call(
        attn_kernel,
        out_shape=[shape(q.shape), tiles, tiles, shape(k_cache.shape), shape(v_cache.shape)],
        in_specs=[SMEM, VMEM, VMEM, VMEM, VMEM, VMEM, VMEM],
        out_specs=[VMEM, VMEM, VMEM, HBM, HBM],
        scratch_shapes=[
            pltpu.VMEM((2, n_heads, 2, n_tok, LANES), F32), wide, wide, pltpu.VMEM((n_tok * n_heads, n_tok), F32),
            dma((2, steps, 2))],
        input_output_aliases={5: 1, 6: 2},
        compiler_params=pltpu.CompilerParams(vmem_limit_bytes=24 << 20),
        name='attention',
    )(pos2, pos2, q, k, v, k_tiles, v_tiles)
    return attn, k_out, v_out


def run_mlp(attn, x, gain, wo, w1, w3, w2):
    rows, width = x.shape
    n_tok = attn.shape[0]
    ffn = w1.shape[2]
    chunk = MLP_CHUNK
    n_chunks = ffn // chunk
    dma = pltpu.SemaphoreType.DMA
    block = pltpu.VMEM((rows, width), BF16)
    chips = pltpu.VMEM((CHIPS, rows, width), BF16)
    return pl.pallas_call(
        mlp_kernel,
        out_shape=shape((rows, width)),
        in_specs=[VMEM, VMEM, VMEM, VMEM, HBM, HBM, HBM],
        out_specs=VMEM,
        scratch_shapes=[
            pltpu.VMEM((CHIPS, 2, rows, width), BF16), chips, chips, block, block, block,
            block, pltpu.VMEM((n_tok // rows, rows, width), BF16), pltpu.VMEM((n_tok, ffn), BF16),
            pltpu.VMEM((n_chunks, width, chunk), BF16), pltpu.VMEM((n_chunks, width, chunk), BF16), pltpu.VMEM((width // chunk, ffn, chunk), BF16),
            dma((3, n_chunks)), dma((7, RS1_PIECES)), dma((7, RS1_PIECES)), dma((GATHER_SEMS,)), dma((GATHER_SEMS,)),
            dma((7, n_chunks)), dma((7, n_chunks))],
        compiler_params=pltpu.CompilerParams(collective_id=1, has_side_effects=True, vmem_limit_bytes=MLP_VMEM),
        name='reduce_mlp',
    )(*(pltpu.with_memory_space_constraint(a, pltpu.VMEM) for a in (attn, x, gain, wo)), w1, w3, w2)


def solution(mesh):
    row_spec = P(('data', 'model'), None)
    cache_spec = P(None, 'data', None, 'model', None)
    col_spec = P(None, None, 'model')
    inner_spec = P(None, 'model', None)
    in_specs = (row_spec, P('data'), P(), P(), col_spec, col_spec, col_spec, inner_spec, col_spec, col_spec, inner_spec, cache_spec, cache_spec)
    out_specs = (row_spec, cache_spec, cache_spec)

    def device_step(hidden, positions, attn_gain, mlp_gain, w_query, w_key, w_value, w_out, w_gate, w_up, w_down, k_cache, v_cache):
        n_tok = positions.shape[0]
        pos2 = positions.reshape(1, n_tok)
        q, k, v, k_tiles, v_tiles = run_qkv(hidden, attn_gain, pos2, w_query, w_key, w_value, k_cache, v_cache)
        attn, k_out, v_out = run_attn(pos2, q, k, v, k_tiles, v_tiles, k_cache, v_cache)
        out = run_mlp(attn, hidden, mlp_gain, w_out, w_gate, w_up, w_down)
        return out, k_out, v_out

    return jax.shard_map(device_step, mesh=mesh, in_specs=in_specs, out_specs=out_specs, check_vma=False)
```

time: 81.5 us -> 69.9 us (0.86)
  local copies, waits for them, and re-layouts: 10.3 us -> 1.56 us
  Pallas kernels: 69.9 us -> 66.8 us
    unnamed x19 -> x9, local copies, waits for them, and re-layouts: 10.3 us -> 1.56 us
    pallas_call x1, Pallas kernels: 41.4 us -> 36.6 us  [run_mlp(): pl.pallas_call(mlp_kernel, out_shape=shape((rows, width)), in_specs=[VMEM...]
    pallas_call x2, Pallas kernels: 28.4 us -> 30.2 us  [the longest x1 18.7 us: run_qkv(): pl.pallas_call(qkv_kernel, out_shape=[shape((n_tok, cols))] * 3 + [shape(...]
where the time goes in v2:
time: 69.9 us; the launch traced here: 69 us
  Pallas kernels  66.8 us (96%)
  local copies, waits for them, and re-layouts  1.56 us (2%)
  between operations  0.72 us (1%)
    pallas_call x1, Pallas kernels, run_mlp(): pl.pallas_call(mlp_kernel, out_shape=shape((rows, width)), in_specs=[VMEM...  36.6 us
    pallas_call x1, Pallas kernels, run_qkv(): pl.pallas_call(qkv_kernel, out_shape=[shape((n_tok, cols))] * 3 + [shape(...  18.7 us
    pallas_call x1, Pallas kernels, run_attn(): pl.pallas_call(attn_kernel, out_shape=[shape(q.shape), tiles, tiles, shap...  11.5 us
    unnamed x9, local copies, waits for them, and re-layouts  1.56 us

profile of v2, /device:TPU:113, one launch (start us, length us, event | category | flops | bytes accessed | tf_op | source)
XLA Modules:
  0.0 69.0 jit_solution(13819433001308245513)
XLA Ops:
  0.6 0.0 copy-start.3
  0.6 18.7 %gather_qkv.1 = (bf16[128,512]{1,0:T(8,128)(2,1)S(1)}, bf16[128,512]{1,0:T(8,128)(2,1)S(1)}, bf16[128,512]{1,0:T(8,128)(2,1)S(1)}, bf16[2,128,64,2,128]{4,3,2,1,...) custom-call(bf16[16,3072]{1,0:T(8,128)(2,1)} %x_buf.1, bf16[1,3072]{1,0:T(2,128)(2,1)} %gain_hbm.1, s32[1,128]{1,0:T(1,128)} %bitcast.5, ...), custom_call_target="tpu_custom_call" | custom-call | tf_op jit(solution)/shard_map/gather_qkv/pallas_call | solution.py:386
  19.3 0.0 copy-done.3
  19.3 0.0 copy-start
  19.3 0.0 copy-start.1
  19.4 0.0 copy-start.2
  19.4 11.5 %attention.1 = (bf16[128,512]{1,0:T(8,128)(2,1)S(1)}, bf16[2,128,128,128]{3,2,1,0:T(8,128)(2,1)S(1)}, bf16[2,128,128,128]{3,2,1,0:T(8,128)(2,1)S(1)}, bf16[1,128...) custom-call(s32[1,128]{1,0:T(1,128)S(1)} %bitcast.6, ...), custom_call_target="tpu_custom_call", output_to_operand_aliasing={{1}: (5, {}), {2}: (6, {})} | custom-call | tf_op jit(solution)/shard_map/attention/pallas_call | solution.py:407
  30.9 0.0 copy-done
  30.9 0.0 copy-done.1
  30.9 0.0 copy-done.2
  30.9 36.6 %reduce_mlp.1 = bf16[16,3072]{1,0:T(8,128)(2,1)} custom-call(bf16[128,512]{1,0:T(8,128)(2,1)S(1)} %get-tuple-element.16.attn_ref, bf16[16,3072]{1,0:T(8,128)(2,1)S(1)} %copy-done.1, bf16[1,3072]{1,0:T(2,128)(2,1)S(1)} %copy-done.2, bf16[1,512,3072]{2,1,0:T(8,128)(2,1)S(1)} %copy-done, bf16[1,3072,3072]{2,1,0:T(8,128)(2,1)} %w1_hbm.1, ...), custom_call_target="tpu_custom_call" | custom-call | tf_op jit(solution)/shard_map/reduce_mlp/pallas_call | solution.py:431
  67.5 1.5 %copy.21 = bf16[16,3072]{1,0:T(8,128)(2,1)} copy(bf16[16,3072]{1,0:T(8,128)(2,1)} %reduce_mlp.1) | data formatting | bytes 196608
Async XLA Ops:
  0.6 18.7 %copy-start.3 = (s32[128]{0:T(128)S(1)}, s32[128]{0:T(128)}, u32[]{:S(2)}) copy-start(s32[128]{0:T(128)} %param.14) | copy-start | bytes 1540
  19.3 11.5 %copy-start = (bf16[1,512,3072]{2,1,0:T(8,128)(2,1)S(1)}, bf16[1,512,3072]{2,1,0:T(8,128)(2,1)}, u32[]{:S(2)}) copy-start(bf16[1,512,3072]{2,1,0:T(8,128)(2,1)} %wo_ref.1) | copy-start | bytes 9437188
  19.3 11.5 %copy-start.1 = (bf16[16,3072]{1,0:T(8,128)(2,1)S(1)}, bf16[16,3072]{1,0:T(8,128)(2,1)}, u32[]{:S(2)}) copy-start(bf16[16,3072]{1,0:T(8,128)(2,1)} %x_buf.1) | copy-start | bytes 294916
  19.4 11.5 %copy-start.2 = (bf16[1,3072]{1,0:T(2,128)(2,1)S(1)}, bf16[1,3072]{1,0:T(2,128)(2,1)}, u32[]{:S(2)}) copy-start(bf16[1,3072]{1,0:T(2,128)(2,1)} %gain_ref.1) | copy-start | bytes 18436

commit v3 on v2

--- a/solution.py
+++ b/solution.py
@@ -94,31 +94,19 @@
 LANES = 128
 
 
-def cache_copies(hbm, buf, sems, start, size, outward=False):
-    _, n_tok, n_rows, n_heads, head = hbm.shape
-    flat = hbm.reshape(1, n_tok, n_rows * n_heads, head)
-    made = []
-    for c in range(2):
-        far = flat.at[0, pl.ds(start, size), :, pl.ds(c * LANES, LANES)]
-        near = buf.at[c, pl.ds(start, size)]
-        src, dst = (near, far) if outward else (far, near)
-        made.append(pltpu.make_async_copy(src, dst, sems.at[c]))
-    return made
-
-
 def qkv_kernel(x_hbm, gain_hbm, pos_hbm, wq_hbm, wk_hbm, wv_hbm, kc_hbm, vc_hbm, q_ref, k_ref, v_ref, kb_ref, vb_ref,
                x_buf, gain_ref, pos_ref, h_buf, w_buf, load_sems, cache_sems, send_sems, recv_sems):
     me, core, chip, other, right, left = places()
     knock(other, right, left)
     loads = [pltpu.make_async_copy(src, dst, load_sems.at[3 + i]) for i, (src, dst) in enumerate(((x_hbm, x_buf), (gain_hbm, gain_ref), (pos_hbm, pos_ref)))]
     w_copies = [pltpu.make_async_copy(w.at[0], w_buf.at[i], load_sems.at[i]) for i, w in enumerate((wq_hbm, wk_hbm, wv_hbm))]
-    piece = kb_ref.shape[1] // 2
+    pieces = cache_sems.shape[1]
+    piece = kb_ref.shape[0] // pieces
     cache_in = []
     for kv, (hbm, buf) in enumerate(((kc_hbm, kb_ref), (vc_hbm, vb_ref))):
-        for p in range(2):
-            for c in range(2):
-                src = hbm.at[0, pl.ds(p * piece, piece), :, :, pl.ds(c * LANES, LANES)]
-                cache_in.append(pltpu.make_async_copy(src, buf.at[c, pl.ds(p * piece, piece)], cache_sems.at[kv, p, c]))
+        for p in range(pieces):
+            toks = pl.ds(p * piece, piece)
+            cache_in.append(pltpu.make_async_copy(hbm.at[toks], buf.at[toks], cache_sems.at[kv, p]))
     for copy in loads + w_copies + cache_in:
         copy.start()
     for copy in loads:
@@ -158,67 +146,79 @@
 
 def attn_kernel(pos_smem, pos_ref, q_ref, k_ref, v_ref, kb_in, vb_in, attn_ref, k_buf, v_buf, ko_hbm, vo_hbm,
                 new_buf, q_buf, o_buf, pc_buf, out_sems):
-    _, n_tok, n_rows, n_heads, head = ko_hbm.shape
-    lanes = LANES
+    n_tok, per_tok, lanes = k_buf.shape
+    n_heads = 2
+    head = q_ref.shape[1] // n_heads
     steps = n_tok // TOK_STEP
-    per_tok = n_rows * n_heads
     bufs = (k_buf, v_buf)
 
     def write_out(t):
-        made = []
-        for kv, hbm in enumerate((ko_hbm, vo_hbm)):
-            made += cache_copies(hbm, bufs[kv], out_sems.at[kv, t], t * TOK_STEP, TOK_STEP, True)
-        return made
+        toks = pl.ds(t * TOK_STEP, TOK_STEP)
+        return [pltpu.make_async_copy(buf.at[toks], hbm.at[toks], out_sems.at[kv, t]) for kv, (buf, hbm) in enumerate(zip(bufs, (ko_hbm, vo_hbm)))]
 
     for h in range(n_heads):
         for c in range(2):
             cols = slice(h * head + c * lanes, h * head + (c + 1) * lanes)
             q_buf.at[c][pl.ds(h, n_tok, stride=2), :] = q_ref[:, cols].astype(F32)
-            new_buf[0, h, c] = k_ref[:, cols].astype(F32)
-            new_buf[1, h, c] = v_ref[:, cols].astype(F32)
+            for kv, ref in enumerate((k_ref, v_ref)):
+                new = ref[:, cols].astype(F32)
+                for again in range(2):
+                    new_buf.at[kv][pl.ds(4 * again + 2 * c + h, n_tok, stride=8), :] = new
     rows2 = n_tok * n_heads
     pos_row = jnp.broadcast_to(pos_ref[...].astype(F32), (rows2, n_tok))
     own = lax.broadcasted_iota(jnp.int32, (rows2, n_tok), 0) // 2 == lax.broadcasted_iota(jnp.int32, (rows2, n_tok), 1)
     pc_buf[...] = jnp.broadcast_to(jnp.sum(jnp.where(own, pos_row, 0.0), axis=1, keepdims=True), (rows2, n_tok))
 
     tile_row = lax.broadcasted_iota(jnp.int32, (16, lanes), 0)
-    sub_rows = TOK_SUB * n_heads
-    q_row = lax.broadcasted_iota(jnp.int32, (sub_rows, lanes), 0)
-    key_col = lax.broadcasted_iota(jnp.int32, (sub_rows, lanes), 1)
-    same_head = (q_row % 2) == (key_col % 2)
-    key_pos = (key_col // 2).astype(F32)
-    q_tok = q_row // 2
+    sub = TOK_SUB * n_heads
+    tok_of = (lax.broadcasted_iota(jnp.int32, (4 * sub, per_tok), 0) % sub) // 2
+    row = lax.broadcasted_iota(jnp.int32, (2 * sub, per_tok), 0)
+    col = lax.broadcasted_iota(jnp.int32, (2 * sub, per_tok), 1)
+    counts = ((col & 2) == 0) & ((col & 1) == (row & 1))
+    key_pos = (col >> 2).astype(F32)
+
+    def shift(x, by):
+        return jnp.concatenate([pltpu.roll(x[:, i:i + lanes], by % lanes, 1) for i in range(0, per_tok, lanes)], axis=1)
 
     def step(t, carry):
+        b0 = t * TOK_STEP
         for i in range(TOK_STEP):
-            b = t * TOK_STEP + i
+            b = b0 + i
             pos = pos_smem[0, b]
-            tile = pl.ds(pl.multiple_of((pos >> 3) * 16, 16), 16)
-            hit = (tile_row >> 1) == (pos & 7)
+            tile = pl.ds(pl.multiple_of((pos >> 2) * 16, 16), 16)
+            hit = (tile_row >> 2) == (pos & 3)
             for kv in range(2):
-                for c in range(2):
-                    old = bufs[kv][c, b, tile, :].astype(F32)
-                    new = jnp.where((tile_row & 1) == 1, new_buf[kv, 1, c, pl.ds(b, 1), :], new_buf[kv, 0, c, pl.ds(b, 1), :])
-                    bufs[kv][c, b, tile, :] = jnp.where(hit, new, old).astype(BF16)
-        for sub in range(TOK_STEP // TOK_SUB):
-            b0 = t * TOK_STEP + sub * TOK_SUB
-            rows = pl.ds(pl.multiple_of(b0 * n_heads, 16), sub_rows)
-            toks = pl.ds(b0, TOK_SUB)
-            q = jnp.concatenate([q_buf[0, rows, :], q_buf[1, rows, :]], axis=1).astype(BF16)
-            keys = jnp.concatenate([k_buf[c, toks].reshape(TOK_SUB * per_tok, lanes) for c in range(2)], axis=1)
-            scores = lax.dot_general(q, keys, (((1,), (1,)), ((), ())), preferred_element_type=F32)
-            mine = jnp.zeros((sub_rows, lanes), F32)
-            for m in range(TOK_SUB):
-                mine = jnp.where(q_tok == m, scores[:, m * lanes:(m + 1) * lanes], mine)
-            mine = mine * (head ** -0.5)
-            mine = jnp.where(same_head & (key_pos <= pc_buf[rows, :]), mine, -1e30)
-            e = jnp.exp(mine - jnp.max(mine, axis=1, keepdims=True))
-            probs = (e / jnp.sum(e, axis=1, keepdims=True)).astype(BF16).astype(F32)
-            wide = jnp.concatenate([jnp.where(q_tok == m, probs, 0.0) for m in range(TOK_SUB)], axis=1).astype(BF16)
-            vals = jnp.concatenate([v_buf[c, toks].reshape(TOK_SUB * per_tok, lanes) for c in range(2)], axis=1)
-            out = jnp.dot(wide, vals, preferred_element_type=F32).astype(BF16).astype(F32)
-            o_buf[0, rows, :] = out[:, :lanes]
-            o_buf[1, rows, :] = out[:, lanes:]
+                new = new_buf[kv, pl.ds(pl.multiple_of(b * 8, 8), 8), :]
+                old = bufs[kv][b, tile, :].astype(F32)
+                bufs[kv][b, tile, :] = jnp.where(hit, jnp.concatenate([new, new], axis=0), old).astype(BF16)
+
+        def pair(buf):
+            return jnp.concatenate([buf[pl.ds(b0 + g * TOK_SUB, TOK_SUB)].reshape(TOK_SUB * per_tok, lanes) for g in range(2)], axis=1)
+
+        rows = [pl.ds(pl.multiple_of(b0 * n_heads + g * sub, sub), sub) for g in range(2)]
+        none = jnp.zeros((sub, lanes), F32)
+        q = jnp.concatenate(
+            [jnp.concatenate([q_buf[c, rows[0], :], none], axis=1) for c in range(2)] +
+            [jnp.concatenate([none, q_buf[c, rows[1], :]], axis=1) for c in range(2)], axis=0).astype(BF16)
+        scores = lax.dot_general(q, pair(k_buf), (((1,), (1,)), ((), ())), preferred_element_type=F32)
+        mine = scores[:, :per_tok]
+        for m in range(1, TOK_SUB):
+            mine = jnp.where(tok_of == m, scores[:, m * per_tok:(m + 1) * per_tok], mine)
+        first = jnp.concatenate([mine[:sub], mine[2 * sub:3 * sub]], axis=0)
+        second = jnp.concatenate([mine[sub:2 * sub], mine[3 * sub:]], axis=0)
+        total = (first + shift(second, -2)) * (head ** -0.5)
+        pos_of = pc_buf[pl.ds(pl.multiple_of(b0 * n_heads, 2 * sub), 2 * sub), :]
+        total = jnp.where(counts & (key_pos <= jnp.concatenate([pos_of] * (per_tok // lanes), axis=1)), total, -1e30)
+        e = jnp.exp(total - jnp.max(total, axis=1, keepdims=True))
+        probs = (e / jnp.sum(e, axis=1, keepdims=True)).astype(BF16).astype(F32)
+        moved = shift(probs, 2)
+        probs = jnp.concatenate([probs[:sub], moved[:sub], probs[sub:], moved[sub:]], axis=0)
+        wide = jnp.concatenate([jnp.where(tok_of == m, probs, 0.0) for m in range(TOK_SUB)], axis=1).astype(BF16)
+        out = jnp.dot(wide, pair(v_buf), preferred_element_type=F32).astype(BF16).astype(F32)
+        for g in range(2):
+            for c in range(2):
+                at = (2 * g + c) * sub
+                o_buf[c, rows[g], :] = out[at:at + sub, g * lanes:(g + 1) * lanes]
         for copy in write_out(t):
             copy.start()
         return carry
@@ -376,42 +376,53 @@
     return jax.ShapeDtypeStruct(dims, dtype)
 
 
-def run_qkv(x, gain, pos2, wq, wk, wv, k_cache, v_cache):
-    _, n_tok, n_rows, n_heads, head = k_cache.shape
+def to_tiles(cache):
+    _, n_tok, n_rows, n_heads, head = cache.shape
+    halves = head // LANES
+    return cache.reshape(n_tok, n_rows, n_heads, halves, LANES).transpose(0, 1, 3, 2, 4).reshape(n_tok, n_rows * halves * n_heads, LANES)
+
+
+def from_tiles(tiles, like):
+    _, n_tok, n_rows, n_heads, head = like.shape
+    halves = head // LANES
+    return tiles.reshape(n_tok, n_rows, halves, n_heads, LANES).transpose(0, 1, 3, 2, 4).reshape(like.shape)
+
+
+def run_qkv(x, gain, pos2, wq, wk, wv, k_tiles, v_tiles):
+    n_tok = k_tiles.shape[0]
     rows, width = x.shape
     cols = wq.shape[2]
     blocks = n_tok // rows
     dma = pltpu.SemaphoreType.DMA
-    args = (x, gain, pos2, wq, wk, wv, k_cache, v_cache)
+    args = (x, gain, pos2, wq, wk, wv, k_tiles, v_tiles)
     return pl.pallas_call(
         qkv_kernel,
-        out_shape=[shape((n_tok, cols))] * 3 + [shape((2, n_tok, n_rows, n_heads, LANES))] * 2,
+        out_shape=[shape((n_tok, cols))] * 3 + [shape(k_tiles.shape)] * 2,
         in_specs=[HBM] * len(args),
         out_specs=[VMEM] * 5,
         scratch_shapes=[
             pltpu.VMEM((rows, width), BF16), pltpu.VMEM(gain.shape, BF16), pltpu.VMEM(pos2.shape, pos2.dtype),
             pltpu.VMEM((blocks, rows, width), BF16), pltpu.VMEM((3, width, cols), BF16),
-            dma((6,)), dma((2, 2, 2)), dma((GATHER_SEMS,)), dma((GATHER_SEMS,))],
+            dma((6,)), dma((2, 4)), dma((GATHER_SEMS,)), dma((GATHER_SEMS,))],
         compiler_params=pltpu.CompilerParams(collective_id=0, has_side_effects=True, vmem_limit_bytes=36 << 20),
         name='gather_qkv',
     )(*(pltpu.with_memory_space_constraint(a, pltpu.HBM) for a in args))
 
 
-def run_attn(pos2, q, k, v, k_tiles, v_tiles, k_cache, v_cache):
-    _, n_tok, n_rows, n_heads, head = k_cache.shape
-    steps = n_tok // TOK_STEP
+def run_attn(pos2, q, k, v, k_tiles, v_tiles):
+    n_tok = k_tiles.shape[0]
+    rows2 = q.shape[1] // (2 * LANES) * n_tok
     dma = pltpu.SemaphoreType.DMA
-    wide = pltpu.VMEM((2, n_tok * n_heads, LANES), F32)
-    k_tiles, v_tiles = (a.reshape(2, n_tok, n_rows * n_heads, LANES) for a in (k_tiles, v_tiles))
+    wide = pltpu.VMEM((2, rows2, LANES), F32)
     tiles = shape(k_tiles.shape)
     attn, _, _, k_out, v_out = pl.pallas_call(
         attn_kernel,
-        out_shape=[shape(q.shape), tiles, tiles, shape(k_cache.shape), shape(v_cache.shape)],
+        out_shape=[shape(q.shape), tiles, tiles, tiles, tiles],
         in_specs=[SMEM, VMEM, VMEM, VMEM, VMEM, VMEM, VMEM],
         out_specs=[VMEM, VMEM, VMEM, HBM, HBM],
         scratch_shapes=[
-            pltpu.VMEM((2, n_heads, 2, n_tok, LANES), F32), wide, wide, pltpu.VMEM((n_tok * n_heads, n_tok), F32),
-            dma((2, steps, 2))],
+            pltpu.VMEM((2, n_tok * 8, LANES), F32), wide, wide, pltpu.VMEM((rows2, n_tok), F32),
+            dma((2, n_tok // TOK_STEP))],
         input_output_aliases={5: 1, 6: 2},
         compiler_params=pltpu.CompilerParams(vmem_limit_bytes=24 << 20),
         name='attention',
@@ -455,9 +466,9 @@
     def device_step(hidden, positions, attn_gain, mlp_gain, w_query, w_key, w_value, w_out, w_gate, w_up, w_down, k_cache, v_cache):
         n_tok = positions.shape[0]
         pos2 = positions.reshape(1, n_tok)
-        q, k, v, k_tiles, v_tiles = run_qkv(hidden, attn_gain, pos2, w_query, w_key, w_value, k_cache, v_cache)
-        attn, k_out, v_out = run_attn(pos2, q, k, v, k_tiles, v_tiles, k_cache, v_cache)
+        q, k, v, k_tiles, v_tiles = run_qkv(hidden, attn_gain, pos2, w_query, w_key, w_value, to_tiles(k_cache), to_tiles(v_cache))
+        attn, k_out, v_out = run_attn(pos2, q, k, v, k_tiles, v_tiles)
         out = run_mlp(attn, hidden, mlp_gain, w_out, w_gate, w_up, w_down)
-        return out, k_out, v_out
+        return out, from_tiles(k_out, k_cache), from_tiles(v_out, v_cache)
 
     return jax.shard_map(device_step, mesh=mesh, in_specs=in_specs, out_specs=out_specs, check_vma=False)

time: 69.9 us -> 70.6 us (1.010)
  no operation moved by 1% of the time
where the time goes in v3:
time: 70.6 us; the launch traced here: 69.7 us
  Pallas kernels  67.4 us (95%)
  local copies, waits for them, and re-layouts  1.56 us (2%)
  between operations  0.72 us (1%)
    pallas_call x1, Pallas kernels, run_mlp(): pl.pallas_call(mlp_kernel, out_shape=shape((rows, width)), in_specs=[VMEM...  36.6 us
    pallas_call x1, Pallas kernels, run_qkv(): pl.pallas_call(qkv_kernel, out_shape=[shape((n_tok, cols))] * 3 + [shape(...  18.7 us
    pallas_call x1, Pallas kernels, run_attn(): pl.pallas_call(attn_kernel, out_shape=[shape(q.shape), tiles, tiles, tile...  12.1 us
    unnamed x9, local copies, waits for them, and re-layouts  1.56 us

profile of v3, /device:TPU:113, one launch (start us, length us, event | category | flops | bytes accessed | tf_op | source)
XLA Modules:
  0.0 69.7 jit_solution(10352322526486908960)
XLA Ops:
  0.6 0.0 copy-start.3
  0.6 18.7 %gather_qkv.1 = (bf16[128,512]{1,0:T(8,128)(2,1)S(1)}, bf16[128,512]{1,0:T(8,128)(2,1)S(1)}, bf16[128,512]{1,0:T(8,128)(2,1)S(1)}, bf16[128,256,128]{2,1,0:T(8,128)(2,1)S(1)}, bf16[128,256,128]{2,1,0:T(8,128)(2,1)S(1)}) custom-call(bf16[16,3072]{1,0:T(8,128)(2,1)} %x_buf.1, bf16[1,3072]{1,0:T(2,128)(2,1)} %gain_hbm.1, s32[1,128]{1,0:T(1,128)} %bitcast.21, ...), custom_call_target="tpu_custom_call" | custom-call | tf_op jit(solution)/shard_map/gather_qkv/pallas_call | solution.py:398
  19.3 0.0 copy-done.3
  19.3 0.0 copy-start
  19.4 0.0 copy-start.1
  19.4 0.0 copy-start.2
  19.4 12.1 %attention.1 = (bf16[128,512]{1,0:T(8,128)(2,1)S(1)}, bf16[128,256,128]{2,1,0:T(8,128)(2,1)S(1)}, bf16[128,256,128]{2,1,0:T(8,128)(2,1)S(1)}, bf16[128,256,128]{2,1,0:T(8,128)(2,1)}, bf16[128,256,128]{2,1,0:T(8,128)(2,1)}) custom-call(s32[1,128]{1,0:T(1,128)S(1)} %bitcast.22, s32[1,128]{1,0:T(1,128)S(1)} %bitcast.23, ...), custom_call_target="tpu_custom_call", output_to_operand_aliasing={{1}: (5, {}), {2}: (6, {})} | custom-call | tf_op jit(solution)/shard_map/attention/pallas_call | solution.py:418
  31.5 0.0 copy-done
  31.5 0.0 copy-done.1
  31.6 0.0 copy-done.2
  31.6 36.6 %reduce_mlp.1 = bf16[16,3072]{1,0:T(8,128)(2,1)} custom-call(bf16[128,512]{1,0:T(8,128)(2,1)S(1)} %get-tuple-element.16.attn_ref, bf16[16,3072]{1,0:T(8,128)(2,1)S(1)} %copy-done.1, bf16[1,3072]{1,0:T(2,128)(2,1)S(1)} %copy-done.2, bf16[1,512,3072]{2,1,0:T(8,128)(2,1)S(1)} %copy-done, bf16[1,3072,3072]{2,1,0:T(8,128)(2,1)} %w1_hbm.1, ...), custom_call_target="tpu_custom_call" | custom-call | tf_op jit(solution)/shard_map/reduce_mlp/pallas_call | solution.py:442
  68.2 1.5 %copy.25 = bf16[16,3072]{1,0:T(8,128)(2,1)} copy(bf16[16,3072]{1,0:T(8,128)(2,1)} %reduce_mlp.1) | data formatting | bytes 196608
Async XLA Ops:
  0.6 18.7 %copy-start.3 = (s32[128]{0:T(128)S(1)}, s32[128]{0:T(128)}, u32[]{:S(2)}) copy-start(s32[128]{0:T(128)} %param.14) | copy-start | bytes 1540
  19.3 12.2 %copy-start = (bf16[1,512,3072]{2,1,0:T(8,128)(2,1)S(1)}, bf16[1,512,3072]{2,1,0:T(8,128)(2,1)}, u32[]{:S(2)}) copy-start(bf16[1,512,3072]{2,1,0:T(8,128)(2,1)} %wo_ref.1) | copy-start | bytes 9437188
  19.4 12.2 %copy-start.1 = (bf16[16,3072]{1,0:T(8,128)(2,1)S(1)}, bf16[16,3072]{1,0:T(8,128)(2,1)}, u32[]{:S(2)}) copy-start(bf16[16,3072]{1,0:T(8,128)(2,1)} %x_buf.1) | copy-start | bytes 294916
  19.4 12.2 %copy-start.2 = (bf16[1,3072]{1,0:T(2,128)(2,1)S(1)}, bf16[1,3072]{1,0:T(2,128)(2,1)}, u32[]{:S(2)}) copy-start(bf16[1,3072]{1,0:T(2,128)(2,1)} %gain_ref.1) | copy-start | bytes 18436

commit v4 on v3

--- a/solution.py
+++ b/solution.py
@@ -19,6 +19,7 @@
 MLP_CHUNK = 512
 RS1_PIECES = 4
 RS2_LAG = 3
+RS2_STRAIGHT = 2
 GATHER_SEMS = 21
 
 
@@ -32,14 +33,14 @@
     return me, core, chip, other, right, left
 
 
-def knock(other, right, left):
+def knock(*peers):
     barrier = pltpu.get_barrier_semaphore()
-    for peer in (other, right, left):
+    for peer in peers:
         pl.semaphore_signal(barrier, inc=1, device_id={'model': peer})
 
 
-def enter():
-    pl.semaphore_wait(pltpu.get_barrier_semaphore(), 3)
+def enter(peers):
+    pl.semaphore_wait(pltpu.get_barrier_semaphore(), peers)
 
 
 def remote(src, dst, send_sem, recv_sem, peer):
@@ -107,12 +108,14 @@
         for p in range(pieces):
             toks = pl.ds(p * piece, piece)
             cache_in.append(pltpu.make_async_copy(hbm.at[toks], buf.at[toks], cache_sems.at[kv, p]))
-    for copy in loads + w_copies + cache_in:
+    for copy in loads:
+        copy.start()
+    for copy in w_copies + cache_in:
         copy.start()
     for copy in loads:
         copy.wait()
     h_buf[me] = norm_rows(x_buf[...].astype(F32), gain_ref[...].astype(F32))
-    enter()
+    enter(3)
     gather_rows(h_buf, send_sems, recv_sems)
 
     n_tok = pos_ref.shape[1]
@@ -142,6 +145,7 @@
 
 TOK_STEP = 16
 TOK_SUB = 8
+TURN = 16
 
 
 def attn_kernel(pos_smem, pos_ref, q_ref, k_ref, v_ref, kb_in, vb_in, attn_ref, k_buf, v_buf, ko_hbm, vo_hbm,
@@ -175,7 +179,7 @@
     row = lax.broadcasted_iota(jnp.int32, (2 * sub, per_tok), 0)
     col = lax.broadcasted_iota(jnp.int32, (2 * sub, per_tok), 1)
     counts = ((col & 2) == 0) & ((col & 1) == (row & 1))
-    key_pos = (col >> 2).astype(F32)
+    key_pos = (((col + jnp.where(row >= sub, TURN, 0)) % per_tok) >> 2).astype(F32)
 
     def shift(x, by):
         return jnp.concatenate([pltpu.roll(x[:, i:i + lanes], by % lanes, 1) for i in range(0, per_tok, lanes)], axis=1)
@@ -193,7 +197,9 @@
                 bufs[kv][b, tile, :] = jnp.where(hit, jnp.concatenate([new, new], axis=0), old).astype(BF16)
 
         def pair(buf):
-            return jnp.concatenate([buf[pl.ds(b0 + g * TOK_SUB, TOK_SUB)].reshape(TOK_SUB * per_tok, lanes) for g in range(2)], axis=1)
+            one, two = (buf[pl.ds(b0 + g * TOK_SUB, TOK_SUB)] for g in range(2))
+            two = jnp.concatenate([two[:, TURN:], two[:, :TURN]], axis=1)
+            return jnp.concatenate([x.reshape(TOK_SUB * per_tok, lanes) for x in (one, two)], axis=1)
 
         rows = [pl.ds(pl.multiple_of(b0 * n_heads + g * sub, sub), sub) for g in range(2)]
         none = jnp.zeros((sub, lanes), F32)
@@ -238,7 +244,7 @@
         self.me, self.core, self.chip, self.other, self.right, self.left = places()
         self.sends = []
 
-    def copy(self, kind, j, cols, way):
+    def copy(self, kind, j, cols, way, direct):
         nxt, prv = (self.right, self.left) if way > 0 else (self.left, self.right)
         ahead = lax.rem(self.chip + CHIPS + way, CHIPS)
         behind = lax.rem(self.chip + CHIPS - way, CHIPS)
@@ -248,47 +254,52 @@
             src, dst, peer = self.part.at[k, 1 - self.core, :, cols], self.from_other.at[k, :, cols], self.other
         else:
             src, dst, peer = (
-                (self.chip_sum.at[opposite, :, cols], self.far_in.at[:, cols], nxt),
+                (self.chip_sum.at[opposite, :, cols], self.far_in.at[:, cols], opposite * 2 + self.core if direct else nxt),
                 (self.chip_sum.at[behind, :, cols], self.near_in.at[:, cols], prv),
                 (self.chip_sum.at[ahead, :, cols], self.last_in.at[:, cols], nxt),
             )[kind - 4]
         return remote(src, dst, self.send_sems.at[kind, j], self.recv_sems.at[kind, j], peer)
 
-    def go(self, kind, j, cols, way):
-        copy = self.copy(kind, j, cols, way)
+    def go(self, kind, j, cols, way, direct):
+        copy = self.copy(kind, j, cols, way, direct)
         copy.start()
         self.sends.append(copy)
 
-    def begin(self, j, cols, way):
+    def begin(self, j, cols, way, direct):
         for kind in range(4):
-            self.go(kind, j, cols, way)
-
-    def pair(self, kind, k, j, cols, way):
-        self.copy(kind, j, cols, way).wait_recv()
+            self.go(kind, j, cols, way, direct)
+
+    def pair(self, kind, k, j, cols, way, direct):
+        self.copy(kind, j, cols, way, direct).wait_recv()
         return self.part[k, self.core, :, cols].astype(F32) + self.from_other[k, :, cols].astype(F32)
 
-    def far(self, j, cols, way):
+    def far(self, j, cols, way, direct):
         opposite = lax.rem(self.chip + 2, CHIPS)
-        self.chip_sum[opposite, :, cols] = self.pair(0, opposite, j, cols, way).astype(BF16)
-        self.go(4, j, cols, way)
-
-    def near(self, j, cols, way):
+        self.chip_sum[opposite, :, cols] = self.pair(0, opposite, j, cols, way, direct).astype(BF16)
+        self.go(4, j, cols, way, direct)
+
+    def near(self, j, cols, way, direct):
         behind = lax.rem(self.chip + CHIPS - way, CHIPS)
-        self.chip_sum[behind, :, cols] = self.pair(1, behind, j, cols, way).astype(BF16)
-        self.go(5, j, cols, way)
-
-    def third(self, j, cols, way):
+        self.chip_sum[behind, :, cols] = self.pair(1, behind, j, cols, way, direct).astype(BF16)
+        self.go(5, j, cols, way, direct)
+
+    def third(self, j, cols, way, direct):
         ahead = lax.rem(self.chip + CHIPS + way, CHIPS)
-        mine = self.pair(2, ahead, j, cols, way)
-        self.copy(4, j, cols, way).wait_recv()
-        self.chip_sum[ahead, :, cols] = (mine + self.far_in[:, cols].astype(F32)).astype(BF16)
-        self.go(6, j, cols, way)
-
-    def last(self, j, cols, way):
-        own = self.pair(3, self.chip, j, cols, way)
-        self.copy(5, j, cols, way).wait_recv()
+        mine = self.pair(2, ahead, j, cols, way, direct)
+        if not direct:
+            self.copy(4, j, cols, way, direct).wait_recv()
+            mine = mine + self.far_in[:, cols].astype(F32)
+        self.chip_sum[ahead, :, cols] = mine.astype(BF16)
+        self.go(6, j, cols, way, direct)
+
+    def last(self, j, cols, way, direct):
+        own = self.pair(3, self.chip, j, cols, way, direct)
+        self.copy(5, j, cols, way, direct).wait_recv()
         own = own + self.near_in[:, cols].astype(F32)
-        self.copy(6, j, cols, way).wait_recv()
+        if direct:
+            self.copy(4, j, cols, way, direct).wait_recv()
+            own = own + self.far_in[:, cols].astype(F32)
+        self.copy(6, j, cols, way, direct).wait_recv()
         return own + self.last_in[:, cols].astype(F32)
 
     def finish(self):
@@ -301,7 +312,7 @@
                x1_buf, h_buf, act_buf, w1_buf, w3_buf, w2_buf,
                w_sems, rs1_send, rs1_recv, ag_send, ag_recv, rs2_send, rs2_recv):
     me, core, chip, other, right, left = places()
-    knock(other, right, left)
+    knock(other, right, left, lax.rem(chip + 2, CHIPS) * 2 + core)
     width = x_buf.shape[1]
     n_tok = act_buf.shape[0]
     n_chunks = w1_buf.shape[0]
@@ -318,9 +329,9 @@
     for i in range(n_chunks):
         weight(2, i).start()
 
-    def plan(pieces):
+    def plan(pieces, straight=0):
         size = width // pieces
-        return [(j, pl.ds(j * size, size), 1 if j % 2 == 0 else -1) for j in range(pieces)]
+        return [(j, pl.ds(j * size, size), 1 if j % 2 == 0 else -1, j >= pieces - straight) for j in range(pieces)]
 
     def put_part(cols, value):
         part[:, :, :, cols] = value.astype(BF16).reshape(CHIPS, 2, n_tok // (2 * CHIPS), value.shape[1])
@@ -331,7 +342,7 @@
     for item in plan1:
         put_part(item[1], jnp.dot(attn, wo_ref[0, :, item[1]], preferred_element_type=F32))
         if item[0] == 0:
-            enter()
+            enter(4)
         rs1.begin(*item)
     for stage in (rs1.far, rs1.near, rs1.third):
         for item in plan1:
@@ -355,7 +366,7 @@
     lax.fori_loop(0, n_chunks, gate_up, 0)
 
     rs2 = Reducer(part, other_in, chip_sum, far_in, near_in, last_in, rs2_send, rs2_recv)
-    plan2 = plan(n_chunks)
+    plan2 = plan(n_chunks, RS2_STRAIGHT)
     for j in range(n_chunks + RS2_LAG):
         if j < n_chunks:
             weight(2, j).wait()
@@ -364,8 +375,11 @@
         if j >= RS2_LAG:
             rs2.far(*plan2[j - RS2_LAG])
             rs2.near(*plan2[j - RS2_LAG])
+            if plan2[j - RS2_LAG][3]:
+                rs2.third(*plan2[j - RS2_LAG])
     for item in plan2:
-        rs2.third(*item)
+        if not item[3]:
+            rs2.third(*item)
     for item in plan2:
         cols = item[1]
         out_ref[:, cols] = (x1_buf[:, cols].astype(F32) + rs2.last(*item)).astype(BF16)

time: 70.6 us -> 69.9 us (0.990); the launches traced: 69.7 us -> 69.8 us
  no operation moved by 1% of the time
where the time goes in v4:
time: 69.9 us; the launch traced here: 69.8 us
  Pallas kernels  67.5 us (97%)
  local copies, waits for them, and re-layouts  1.56 us (2%)
  between operations  0.72 us (1%)
    pallas_call x1, Pallas kernels, run_mlp(): pl.pallas_call(mlp_kernel, out_shape=shape((rows, width)), in_specs=[VMEM...  36.7 us
    pallas_call x1, Pallas kernels, run_qkv(): pl.pallas_call(qkv_kernel, out_shape=[shape((n_tok, cols))] * 3 + [shape(...  18.7 us
    pallas_call x1, Pallas kernels, run_attn(): pl.pallas_call(attn_kernel, out_shape=[shape(q.shape), tiles, tiles, tile...  12.2 us
    unnamed x9, local copies, waits for them, and re-layouts  1.56 us

profile of v4, /device:TPU:113, one launch (start us, length us, event | category | flops | bytes accessed | tf_op | source)
XLA Modules:
  0.0 69.8 jit_solution(13484694997129375395)
XLA Ops:
  0.6 0.0 copy-start.3
  0.6 18.7 %gather_qkv.1 = (bf16[128,512]{1,0:T(8,128)(2,1)S(1)}, bf16[128,512]{1,0:T(8,128)(2,1)S(1)}, bf16[128,512]{1,0:T(8,128)(2,1)S(1)}, bf16[128,256,128]{2,1,0:T(8,128)(2,1)S(1)}, bf16[128,256,128]{2,1,0:T(8,128)(2,1)S(1)}) custom-call(bf16[16,3072]{1,0:T(8,128)(2,1)} %x_buf.1, bf16[1,3072]{1,0:T(2,128)(2,1)} %gain_hbm.1, s32[1,128]{1,0:T(1,128)} %bitcast.21, ...), custom_call_target="tpu_custom_call" | custom-call | tf_op jit(solution)/shard_map/gather_qkv/pallas_call | solution.py:412
  19.3 0.0 copy-done.3
  19.3 0.0 copy-start
  19.4 0.0 copy-start.1
  19.4 0.0 copy-start.2
  19.4 12.2 %attention.1 = (bf16[128,512]{1,0:T(8,128)(2,1)S(1)}, bf16[128,256,128]{2,1,0:T(8,128)(2,1)S(1)}, bf16[128,256,128]{2,1,0:T(8,128)(2,1)S(1)}, bf16[128,256,128]{2,1,0:T(8,128)(2,1)}, bf16[128,256,128]{2,1,0:T(8,128)(2,1)}) custom-call(s32[1,128]{1,0:T(1,128)S(1)} %bitcast.22, s32[1,128]{1,0:T(1,128)S(1)} %bitcast.23, ...), custom_call_target="tpu_custom_call", output_to_operand_aliasing={{1}: (5, {}), {2}: (6, {})} | custom-call | tf_op jit(solution)/shard_map/attention/pallas_call | solution.py:432
  31.5 0.0 copy-done
  31.5 0.0 copy-done.1
  31.6 0.0 copy-done.2
  31.6 36.7 %reduce_mlp.1 = bf16[16,3072]{1,0:T(8,128)(2,1)} custom-call(bf16[128,512]{1,0:T(8,128)(2,1)S(1)} %get-tuple-element.16.attn_ref, bf16[16,3072]{1,0:T(8,128)(2,1)S(1)} %copy-done.1, bf16[1,3072]{1,0:T(2,128)(2,1)S(1)} %copy-done.2, bf16[1,512,3072]{2,1,0:T(8,128)(2,1)S(1)} %copy-done, bf16[1,3072,3072]{2,1,0:T(8,128)(2,1)} %w1_hbm.1, ...), custom_call_target="tpu_custom_call" | custom-call | tf_op jit(solution)/shard_map/reduce_mlp/pallas_call | solution.py:456
  68.2 1.5 %copy.25 = bf16[16,3072]{1,0:T(8,128)(2,1)} copy(bf16[16,3072]{1,0:T(8,128)(2,1)} %reduce_mlp.1) | data formatting | bytes 196608
Async XLA Ops:
  0.6 18.7 %copy-start.3 = (s32[128]{0:T(128)S(1)}, s32[128]{0:T(128)}, u32[]{:S(2)}) copy-start(s32[128]{0:T(128)} %param.14) | copy-start | bytes 1540
  19.3 12.2 %copy-start = (bf16[1,512,3072]{2,1,0:T(8,128)(2,1)S(1)}, bf16[1,512,3072]{2,1,0:T(8,128)(2,1)}, u32[]{:S(2)}) copy-start(bf16[1,512,3072]{2,1,0:T(8,128)(2,1)} %wo_ref.1) | copy-start | bytes 9437188
  19.4 12.2 %copy-start.1 = (bf16[16,3072]{1,0:T(8,128)(2,1)S(1)}, bf16[16,3072]{1,0:T(8,128)(2,1)}, u32[]{:S(2)}) copy-start(bf16[16,3072]{1,0:T(8,128)(2,1)} %x_buf.1) | copy-start | bytes 294916
  19.4 12.2 %copy-start.2 = (bf16[1,3072]{1,0:T(2,128)(2,1)S(1)}, bf16[1,3072]{1,0:T(2,128)(2,1)}, u32[]{:S(2)}) copy-start(bf16[1,3072]{1,0:T(2,128)(2,1)} %gain_ref.1) | copy-start | bytes 18436

commit v5 on v4

--- a/solution.py
+++ b/solution.py
@@ -12,7 +12,6 @@
 BF16 = jnp.bfloat16
 F32 = jnp.float32
 VMEM = pl.BlockSpec(memory_space=pltpu.VMEM)
-SMEM = pl.BlockSpec(memory_space=pltpu.SMEM)
 HBM = pl.BlockSpec(memory_space=pltpu.HBM)
 MLP_VMEM = 63400000
 CHIPS = 4
@@ -52,7 +51,7 @@
     return (x_f * inv_rms * gain_f).astype(BF16)
 
 
-def gather_rows(buf, send_sems, recv_sems):
+def gather_rows(buf, send_sems, recv_sems, behind=()):
     me, core, chip, other, right, left = places()
     width = buf.shape[2]
     quarter = width // 4
@@ -76,6 +75,11 @@
     for cols, idx, peer in ((q0, 0, right), (q2, 1, left), (q1, 2, right), (q3, 3, left), (hi, 4, right), (lo, 5, left), (full, 6, other)):
         send(me, cols, idx, peer)
     across = []
+    behind = list(behind)
+    share = -(-len(behind) // 8)
+    for copy in behind[:2 * share]:
+        copy.start()
+    behind = behind[2 * share:]
     for blk, cols, idx, onward, peer in (
             (left, q0, 0, 7, right), (right, q2, 1, 8, left), (left, q1, 2, 9, right), (right, q3, 3, 10, left),
             (left, hi, 4, None, None), (right, lo, 5, None, None),
@@ -85,6 +89,9 @@
             send(blk, cols, onward, peer)
         send(blk, cols, 11 + len(across), other)
         across.append((blk + 1 - 2 * core, cols, 11 + len(across)))
+        for copy in behind[:share]:
+            copy.start()
+        behind = behind[share:]
     arrive(other, full, 6)
     for item in across:
         arrive(*item)
@@ -110,13 +117,13 @@
             cache_in.append(pltpu.make_async_copy(hbm.at[toks], buf.at[toks], cache_sems.at[kv, p]))
     for copy in loads:
         copy.start()
-    for copy in w_copies + cache_in:
+    for copy in w_copies:
         copy.start()
     for copy in loads:
         copy.wait()
     h_buf[me] = norm_rows(x_buf[...].astype(F32), gain_ref[...].astype(F32))
     enter(3)
-    gather_rows(h_buf, send_sems, recv_sems)
+    gather_rows(h_buf, send_sems, recv_sems, cache_in)
 
     n_tok = pos_ref.shape[1]
     half = 128
@@ -145,16 +152,17 @@
 
 TOK_STEP = 16
 TOK_SUB = 8
-TURN = 16
-
-
-def attn_kernel(pos_smem, pos_ref, q_ref, k_ref, v_ref, kb_in, vb_in, attn_ref, k_buf, v_buf, ko_hbm, vo_hbm,
-                new_buf, q_buf, o_buf, pc_buf, out_sems):
+
+
+def attn_kernel(pos_hbm, pos_ref, q_ref, k_ref, v_ref, kb_in, vb_in, attn_ref, k_buf, v_buf, ko_hbm, vo_hbm,
+                pos_smem, new_buf, q_buf, o_buf, pc_buf, score_buf, prob_buf, pos_sem, out_sems):
     n_tok, per_tok, lanes = k_buf.shape
     n_heads = 2
     head = q_ref.shape[1] // n_heads
     steps = n_tok // TOK_STEP
     bufs = (k_buf, v_buf)
+    pos_copy = pltpu.make_async_copy(pos_hbm, pos_smem, pos_sem)
+    pos_copy.start()
 
     def write_out(t):
         toks = pl.ds(t * TOK_STEP, TOK_STEP)
@@ -179,12 +187,37 @@
     row = lax.broadcasted_iota(jnp.int32, (2 * sub, per_tok), 0)
     col = lax.broadcasted_iota(jnp.int32, (2 * sub, per_tok), 1)
     counts = ((col & 2) == 0) & ((col & 1) == (row & 1))
-    key_pos = (((col + jnp.where(row >= sub, TURN, 0)) % per_tok) >> 2).astype(F32)
+    key_pos = (col >> 2).astype(F32)
 
     def shift(x, by):
         return jnp.concatenate([pltpu.roll(x[:, i:i + lanes], by % lanes, 1) for i in range(0, per_tok, lanes)], axis=1)
 
-    def step(t, carry):
+    def pair(buf, b0):
+        one, two = (buf[pl.ds(b0 + g * TOK_SUB, TOK_SUB)] for g in range(2))
+        return jnp.concatenate([x.reshape(TOK_SUB * per_tok, lanes) for x in (one, two)], axis=1)
+
+    def out_rows(b0):
+        return [pl.ds(pl.multiple_of(b0 * n_heads + g * sub, sub), sub) for g in range(2)]
+
+    def mix(t):
+        b0 = t * TOK_STEP
+        probs = prob_buf[...]
+        wide = jnp.concatenate([jnp.where(tok_of == m, probs, 0.0) for m in range(TOK_SUB)], axis=1).astype(BF16)
+        out = jnp.dot(wide, pair(v_buf, b0), preferred_element_type=F32).astype(BF16).astype(F32)
+        rows = out_rows(b0)
+        for g in range(2):
+            for c in range(2):
+                at = (2 * g + c) * sub
+                o_buf[c, rows[g], :] = out[at:at + sub, g * lanes:(g + 1) * lanes]
+
+    def soften():
+        total = score_buf[...]
+        e = jnp.exp(total - jnp.max(total, axis=1, keepdims=True))
+        probs = (e / jnp.sum(e, axis=1, keepdims=True)).astype(BF16).astype(F32)
+        moved = shift(probs, 2)
+        prob_buf[...] = jnp.concatenate([probs[:sub], moved[:sub], probs[sub:], moved[sub:]], axis=0)
+
+    def score(t):
         b0 = t * TOK_STEP
         for i in range(TOK_STEP):
             b = b0 + i
@@ -195,18 +228,12 @@
                 new = new_buf[kv, pl.ds(pl.multiple_of(b * 8, 8), 8), :]
                 old = bufs[kv][b, tile, :].astype(F32)
                 bufs[kv][b, tile, :] = jnp.where(hit, jnp.concatenate([new, new], axis=0), old).astype(BF16)
-
-        def pair(buf):
-            one, two = (buf[pl.ds(b0 + g * TOK_SUB, TOK_SUB)] for g in range(2))
-            two = jnp.concatenate([two[:, TURN:], two[:, :TURN]], axis=1)
-            return jnp.concatenate([x.reshape(TOK_SUB * per_tok, lanes) for x in (one, two)], axis=1)
-
-        rows = [pl.ds(pl.multiple_of(b0 * n_heads + g * sub, sub), sub) for g in range(2)]
+        rows = out_rows(b0)
         none = jnp.zeros((sub, lanes), F32)
         q = jnp.concatenate(
             [jnp.concatenate([q_buf[c, rows[0], :], none], axis=1) for c in range(2)] +
             [jnp.concatenate([none, q_buf[c, rows[1], :]], axis=1) for c in range(2)], axis=0).astype(BF16)
-        scores = lax.dot_general(q, pair(k_buf), (((1,), (1,)), ((), ())), preferred_element_type=F32)
+        scores = lax.dot_general(q, pair(k_buf, b0), (((1,), (1,)), ((), ())), preferred_element_type=F32)
         mine = scores[:, :per_tok]
         for m in range(1, TOK_SUB):
             mine = jnp.where(tok_of == m, scores[:, m * per_tok:(m + 1) * per_tok], mine)
@@ -214,22 +241,30 @@
         second = jnp.concatenate([mine[sub:2 * sub], mine[3 * sub:]], axis=0)
         total = (first + shift(second, -2)) * (head ** -0.5)
         pos_of = pc_buf[pl.ds(pl.multiple_of(b0 * n_heads, 2 * sub), 2 * sub), :]
-        total = jnp.where(counts & (key_pos <= jnp.concatenate([pos_of] * (per_tok // lanes), axis=1)), total, -1e30)
-        e = jnp.exp(total - jnp.max(total, axis=1, keepdims=True))
-        probs = (e / jnp.sum(e, axis=1, keepdims=True)).astype(BF16).astype(F32)
-        moved = shift(probs, 2)
-        probs = jnp.concatenate([probs[:sub], moved[:sub], probs[sub:], moved[sub:]], axis=0)
-        wide = jnp.concatenate([jnp.where(tok_of == m, probs, 0.0) for m in range(TOK_SUB)], axis=1).astype(BF16)
-        out = jnp.dot(wide, pair(v_buf), preferred_element_type=F32).astype(BF16).astype(F32)
-        for g in range(2):
-            for c in range(2):
-                at = (2 * g + c) * sub
-                o_buf[c, rows[g], :] = out[at:at + sub, g * lanes:(g + 1) * lanes]
+        score_buf[...] = jnp.where(counts & (key_pos <= jnp.concatenate([pos_of] * (per_tok // lanes), axis=1)), total, -1e30)
+
+    def send(t):
         for copy in write_out(t):
             copy.start()
+
+    pos_copy.wait()
+    score(0)
+    send(0)
+    soften()
+    score(1)
+    send(1)
+
+    def step(t, carry):
+        mix(t - 2)
+        soften()
+        score(t)
+        send(t)
         return carry
 
-    lax.fori_loop(0, steps, step, 0)
+    lax.fori_loop(2, steps, step, 0)
+    mix(steps - 2)
+    soften()
+    mix(steps - 1)
     attn_ref[...] = jnp.concatenate([o_buf.at[c][pl.ds(h, n_tok, stride=2), :] for h in range(n_heads) for c in range(2)], axis=1).astype(BF16)
     for t in range(steps):
         for copy in write_out(t):
@@ -326,8 +361,6 @@
     for i in range(n_chunks):
         weight(0, i).start()
         weight(1, i).start()
-    for i in range(n_chunks):
-        weight(2, i).start()
 
     def plan(pieces, straight=0):
         size = width // pieces
@@ -353,6 +386,8 @@
     rs1.finish()
     h_buf[me] = norm_rows(x1_buf[...].astype(F32), gain_ref[...].astype(F32))
     gather_rows(h_buf, ag_send, ag_recv)
+    for i in range(n_chunks):
+        weight(2, i).start()
 
     def gate_up(i, carry):
         weight(0, i).wait()
@@ -417,7 +452,7 @@
         scratch_shapes=[
             pltpu.VMEM((rows, width), BF16), pltpu.VMEM(gain.shape, BF16), pltpu.VMEM(pos2.shape, pos2.dtype),
             pltpu.VMEM((blocks, rows, width), BF16), pltpu.VMEM((3, width, cols), BF16),
-            dma((6,)), dma((2, 4)), dma((GATHER_SEMS,)), dma((GATHER_SEMS,))],
+            dma((6,)), dma((2, 8)), dma((GATHER_SEMS,)), dma((GATHER_SEMS,))],
         compiler_params=pltpu.CompilerParams(collective_id=0, has_side_effects=True, vmem_limit_bytes=36 << 20),
         name='gather_qkv',
     )(*(pltpu.with_memory_space_constraint(a, pltpu.HBM) for a in args))
@@ -432,15 +467,16 @@
     attn, _, _, k_out, v_out = pl.pallas_call(
         attn_kernel,
         out_shape=[shape(q.shape), tiles, tiles, tiles, tiles],
-        in_specs=[SMEM, VMEM, VMEM, VMEM, VMEM, VMEM, VMEM],
+        in_specs=[HBM, VMEM, VMEM, VMEM, VMEM, VMEM, VMEM],
         out_specs=[VMEM, VMEM, VMEM, HBM, HBM],
         scratch_shapes=[
-            pltpu.VMEM((2, n_tok * 8, LANES), F32), wide, wide, pltpu.VMEM((rows2, n_tok), F32),
-            dma((2, n_tok // TOK_STEP))],
+            pltpu.SMEM(pos2.shape, pos2.dtype), pltpu.VMEM((2, n_tok * 8, LANES), F32), wide, wide, pltpu.VMEM((rows2, n_tok), F32),
+            pltpu.VMEM((4 * TOK_SUB, k_tiles.shape[1]), F32), pltpu.VMEM((8 * TOK_SUB, k_tiles.shape[1]), F32),
+            dma, dma((2, n_tok // TOK_STEP))],
         input_output_aliases={5: 1, 6: 2},
         compiler_params=pltpu.CompilerParams(vmem_limit_bytes=24 << 20),
         name='attention',
-    )(pos2, pos2, q, k, v, k_tiles, v_tiles)
+    )(pltpu.with_memory_space_constraint(pos2, pltpu.HBM), pos2, q, k, v, k_tiles, v_tiles)
     return attn, k_out, v_out
 
 

time: 69.9 us -> 62.4 us (0.89)
  Pallas kernels: 67.5 us -> 60 us
    pallas_call x1, Pallas kernels: 18.7 us -> 15 us  [run_qkv(): pl.pallas_call(qkv_kernel, out_shape=[shape((n_tok, cols))] * 3 + [shape(...]
    pallas_call x1, Pallas kernels: 12.2 us -> 8.63 us  [run_attn(): pl.pallas_call(attn_kernel, out_shape=[shape(q.shape), tiles, tiles, tile...]
    unnamed x9 -> x7, local copies, waits for them, and re-layouts: 1.56 us -> 1.56 us
where the time goes in v5:
time: 62.4 us; the launch traced here: 62.3 us
  Pallas kernels  60 us (96%)
  local copies, waits for them, and re-layouts  1.56 us (2%)
  between operations  0.7 us (1%)
    pallas_call x1, Pallas kernels, run_mlp(): pl.pallas_call(mlp_kernel, out_shape=shape((rows, width)), in_specs=[VMEM...  36.4 us
    pallas_call x1, Pallas kernels, run_qkv(): pl.pallas_call(qkv_kernel, out_shape=[shape((n_tok, cols))] * 3 + [shape(...  15 us
    pallas_call x1, Pallas kernels, run_attn(): pl.pallas_call(attn_kernel, out_shape=[shape(q.shape), tiles, tiles, tile...  8.63 us
    unnamed x7, local copies, waits for them, and re-layouts  1.56 us

profile of v5, /device:TPU:113, one launch (start us, length us, event | category | flops | bytes accessed | tf_op | source)
XLA Modules:
  0.0 62.3 jit_solution(18357242642733164102)
XLA Ops:
  0.6 15.0 %gather_qkv.1 = (bf16[128,512]{1,0:T(8,128)(2,1)S(1)}, bf16[128,512]{1,0:T(8,128)(2,1)S(1)}, bf16[128,512]{1,0:T(8,128)(2,1)S(1)}, bf16[128,256,128]{2,1,0:T(8,128)(2,1)S(1)}, bf16[128,256,128]{2,1,0:T(8,128)(2,1)S(1)}) custom-call(bf16[16,3072]{1,0:T(8,128)(2,1)} %x_buf.1, bf16[1,3072]{1,0:T(2,128)(2,1)} %gain_hbm.1, s32[1,128]{1,0:T(1,128)} %bitcast.23, ...), custom_call_target="tpu_custom_call" | custom-call | tf_op jit(solution)/shard_map/gather_qkv/pallas_call | solution.py:447
  15.6 0.0 copy-start
  15.7 0.0 copy-start.1
  15.7 0.0 copy-start.2
  15.7 8.6 %attention.1 = (bf16[128,512]{1,0:T(8,128)(2,1)S(1)}, bf16[128,256,128]{2,1,0:T(8,128)(2,1)S(1)}, bf16[128,256,128]{2,1,0:T(8,128)(2,1)S(1)}, bf16[128,256,128]{2,1,0:T(8,128)(2,1)}, bf16[128,256,128]{2,1,0:T(8,128)(2,1)}) custom-call(s32[1,128]{1,0:T(1,128)} %bitcast.24, s32[1,128]{1,0:T(1,128)} %bitcast.25, ...), custom_call_target="tpu_custom_call", output_to_operand_aliasing={{1}: (5, {}), {2}: (6, {})} | custom-call | tf_op jit(solution)/shard_map/attention/pallas_call | solution.py:467
  24.3 0.0 copy-done
  24.3 0.0 copy-done.1
  24.3 0.0 copy-done.2
  24.3 36.4 %reduce_mlp.1 = bf16[16,3072]{1,0:T(8,128)(2,1)} custom-call(bf16[128,512]{1,0:T(8,128)(2,1)S(1)} %get-tuple-element.16.attn_ref, bf16[16,3072]{1,0:T(8,128)(2,1)S(1)} %copy-done.1, bf16[1,3072]{1,0:T(2,128)(2,1)S(1)} %copy-done.2, bf16[1,512,3072]{2,1,0:T(8,128)(2,1)S(1)} %copy-done, bf16[1,3072,3072]{2,1,0:T(8,128)(2,1)} %w1_hbm.1, ...), custom_call_target="tpu_custom_call" | custom-call | tf_op jit(solution)/shard_map/reduce_mlp/pallas_call | solution.py:492
  60.7 1.5 %copy.25 = bf16[16,3072]{1,0:T(8,128)(2,1)} copy(bf16[16,3072]{1,0:T(8,128)(2,1)} %reduce_mlp.1) | data formatting | bytes 196608
Async XLA Ops:
  15.6 8.7 %copy-start = (bf16[1,512,3072]{2,1,0:T(8,128)(2,1)S(1)}, bf16[1,512,3072]{2,1,0:T(8,128)(2,1)}, u32[]{:S(2)}) copy-start(bf16[1,512,3072]{2,1,0:T(8,128)(2,1)} %wo_ref.1) | copy-start | bytes 9437188
  15.7 8.7 %copy-start.1 = (bf16[16,3072]{1,0:T(8,128)(2,1)S(1)}, bf16[16,3072]{1,0:T(8,128)(2,1)}, u32[]{:S(2)}) copy-start(bf16[16,3072]{1,0:T(8,128)(2,1)} %x_buf.1) | copy-start | bytes 294916
  15.7 8.7 %copy-start.2 = (bf16[1,3072]{1,0:T(2,128)(2,1)S(1)}, bf16[1,3072]{1,0:T(2,128)(2,1)}, u32[]{:S(2)}) copy-start(bf16[1,3072]{1,0:T(2,128)(2,1)} %gain_ref.1) | copy-start | bytes 18436

commit v6 on v5

--- a/solution.py
+++ b/solution.py
@@ -51,7 +51,7 @@
     return (x_f * inv_rms * gain_f).astype(BF16)
 
 
-def gather_rows(buf, send_sems, recv_sems, behind=()):
+def gather_rows(buf, send_sems, recv_sems, behind=(), meanwhile=None):
     me, core, chip, other, right, left = places()
     width = buf.shape[2]
     quarter = width // 4
@@ -80,6 +80,8 @@
     for copy in behind[:2 * share]:
         copy.start()
     behind = behind[2 * share:]
+    if meanwhile is not None:
+        meanwhile()
     for blk, cols, idx, onward, peer in (
             (left, q0, 0, 7, right), (right, q2, 1, 8, left), (left, q1, 2, 9, right), (right, q3, 3, 10, left),
             (left, hi, 4, None, None), (right, lo, 5, None, None),
@@ -102,8 +104,8 @@
 LANES = 128
 
 
-def qkv_kernel(x_hbm, gain_hbm, pos_hbm, wq_hbm, wk_hbm, wv_hbm, kc_hbm, vc_hbm, q_ref, k_ref, v_ref, kb_ref, vb_ref,
-               x_buf, gain_ref, pos_ref, h_buf, w_buf, load_sems, cache_sems, send_sems, recv_sems):
+def qkv_kernel(x_hbm, gain_hbm, pos_hbm, wq_hbm, wk_hbm, wv_hbm, kc_hbm, vc_hbm, q_ref, k_ref, v_ref, kb_ref, vb_ref, pc_ref,
+               trig_buf, x_buf, gain_ref, pos_ref, h_buf, w_buf, load_sems, cache_sems, send_sems, recv_sems):
     me, core, chip, other, right, left = places()
     knock(other, right, left)
     loads = [pltpu.make_async_copy(src, dst, load_sems.at[3 + i]) for i, (src, dst) in enumerate(((x_hbm, x_buf), (gain_hbm, gain_ref), (pos_hbm, pos_ref)))]
@@ -117,23 +119,29 @@
             cache_in.append(pltpu.make_async_copy(hbm.at[toks], buf.at[toks], cache_sems.at[kv, p]))
     for copy in loads:
         copy.start()
-    for copy in w_copies:
-        copy.start()
     for copy in loads:
         copy.wait()
     h_buf[me] = norm_rows(x_buf[...].astype(F32), gain_ref[...].astype(F32))
     enter(3)
-    gather_rows(h_buf, send_sems, recv_sems, cache_in)
-
     n_tok = pos_ref.shape[1]
-    half = 128
+    half = LANES
     head = 2 * half
-    pos_row = jnp.broadcast_to(pos_ref[...].astype(F32), (n_tok, n_tok))
-    diag = lax.broadcasted_iota(jnp.int32, (n_tok, n_tok), 0) == lax.broadcasted_iota(jnp.int32, (n_tok, n_tok), 1)
-    pos_col = jnp.sum(jnp.where(diag, pos_row, 0.0), axis=1, keepdims=True)
-    lane = lax.broadcasted_iota(jnp.int32, (n_tok, half), 1).astype(F32)
-    angles = pos_col * jnp.exp(lane * (-2.0 * math.log(ROPE_BASE) / head))
-    cos_tab, sin_tab = jnp.cos(angles), jnp.sin(angles)
+    pos_f = pos_ref[...].astype(F32)
+
+    def pick(rows, per):
+        own = lax.broadcasted_iota(jnp.int32, (rows, n_tok), 0) // per == lax.broadcasted_iota(jnp.int32, (rows, n_tok), 1)
+        return jnp.sum(jnp.where(own, jnp.broadcast_to(pos_f, (rows, n_tok)), 0.0), axis=1, keepdims=True)
+
+    def tables():
+        lane = lax.broadcasted_iota(jnp.int32, (n_tok, half), 1).astype(F32)
+        angles = pick(n_tok, 1) * jnp.exp(lane * (-2.0 * math.log(ROPE_BASE) / head))
+        trig_buf[0] = jnp.cos(angles)
+        trig_buf[1] = jnp.sin(angles)
+        rows2 = pc_ref.shape[0]
+        pc_ref[...] = jnp.broadcast_to(pick(rows2, rows2 // n_tok), pc_ref.shape)
+
+    gather_rows(h_buf, send_sems, recv_sems, w_copies + cache_in, tables)
+    cos_tab, sin_tab = trig_buf[0], trig_buf[1]
     h_all = h_buf[...].reshape(n_tok, h_buf.shape[2])
     for i, out_ref in enumerate((q_ref, k_ref, v_ref)):
         w_copies[i].wait()
@@ -151,11 +159,12 @@
 
 
 TOK_STEP = 16
-TOK_SUB = 8
-
-
-def attn_kernel(pos_hbm, pos_ref, q_ref, k_ref, v_ref, kb_in, vb_in, attn_ref, k_buf, v_buf, ko_hbm, vo_hbm,
-                pos_smem, new_buf, q_buf, o_buf, pc_buf, score_buf, prob_buf, pos_sem, out_sems):
+TOK_UNIT = 8
+TOK_SUB = 4
+
+
+def attn_kernel(pos_hbm, pc_buf, q_ref, k_ref, v_ref, kb_in, vb_in, attn_ref, k_buf, v_buf, ko_hbm, vo_hbm,
+                pos_smem, new_buf, q_buf, o_buf, score_buf, prob_buf, pos_sem, out_sems):
     n_tok, per_tok, lanes = k_buf.shape
     n_heads = 2
     head = q_ref.shape[1] // n_heads
@@ -176,11 +185,6 @@
                 new = ref[:, cols].astype(F32)
                 for again in range(2):
                     new_buf.at[kv][pl.ds(4 * again + 2 * c + h, n_tok, stride=8), :] = new
-    rows2 = n_tok * n_heads
-    pos_row = jnp.broadcast_to(pos_ref[...].astype(F32), (rows2, n_tok))
-    own = lax.broadcasted_iota(jnp.int32, (rows2, n_tok), 0) // 2 == lax.broadcasted_iota(jnp.int32, (rows2, n_tok), 1)
-    pc_buf[...] = jnp.broadcast_to(jnp.sum(jnp.where(own, pos_row, 0.0), axis=1, keepdims=True), (rows2, n_tok))
-
     tile_row = lax.broadcasted_iota(jnp.int32, (16, lanes), 0)
     sub = TOK_SUB * n_heads
     tok_of = (lax.broadcasted_iota(jnp.int32, (4 * sub, per_tok), 0) % sub) // 2
@@ -199,9 +203,11 @@
     def out_rows(b0):
         return [pl.ds(pl.multiple_of(b0 * n_heads + g * sub, sub), sub) for g in range(2)]
 
-    def mix(t):
-        b0 = t * TOK_STEP
-        probs = prob_buf[...]
+    units = TOK_STEP // TOK_UNIT
+
+    def mix(t, u):
+        b0 = t * TOK_STEP + u * TOK_UNIT
+        probs = prob_buf[u]
         wide = jnp.concatenate([jnp.where(tok_of == m, probs, 0.0) for m in range(TOK_SUB)], axis=1).astype(BF16)
         out = jnp.dot(wide, pair(v_buf, b0), preferred_element_type=F32).astype(BF16).astype(F32)
         rows = out_rows(b0)
@@ -210,16 +216,16 @@
                 at = (2 * g + c) * sub
                 o_buf[c, rows[g], :] = out[at:at + sub, g * lanes:(g + 1) * lanes]
 
-    def soften():
-        total = score_buf[...]
+    def soften(u):
+        total = score_buf[u]
         e = jnp.exp(total - jnp.max(total, axis=1, keepdims=True))
         probs = (e / jnp.sum(e, axis=1, keepdims=True)).astype(BF16).astype(F32)
         moved = shift(probs, 2)
-        prob_buf[...] = jnp.concatenate([probs[:sub], moved[:sub], probs[sub:], moved[sub:]], axis=0)
-
-    def score(t):
-        b0 = t * TOK_STEP
-        for i in range(TOK_STEP):
+        prob_buf[u] = jnp.concatenate([probs[:sub], moved[:sub], probs[sub:], moved[sub:]], axis=0)
+
+    def score(t, u):
+        b0 = t * TOK_STEP + u * TOK_UNIT
+        for i in range(TOK_UNIT):
             b = b0 + i
             pos = pos_smem[0, b]
             tile = pl.ds(pl.multiple_of((pos >> 2) * 16, 16), 16)
@@ -241,30 +247,34 @@
         second = jnp.concatenate([mine[sub:2 * sub], mine[3 * sub:]], axis=0)
         total = (first + shift(second, -2)) * (head ** -0.5)
         pos_of = pc_buf[pl.ds(pl.multiple_of(b0 * n_heads, 2 * sub), 2 * sub), :]
-        score_buf[...] = jnp.where(counts & (key_pos <= jnp.concatenate([pos_of] * (per_tok // lanes), axis=1)), total, -1e30)
+        score_buf[u] = jnp.where(counts & (key_pos <= jnp.concatenate([pos_of] * (per_tok // lanes), axis=1)), total, -1e30)
 
     def send(t):
         for copy in write_out(t):
             copy.start()
 
+    def each(stage, *args):
+        for u in range(units):
+            stage(*args, u)
+
     pos_copy.wait()
-    score(0)
+    each(score, 0)
     send(0)
-    soften()
-    score(1)
+    each(soften)
+    each(score, 1)
     send(1)
 
     def step(t, carry):
-        mix(t - 2)
-        soften()
-        score(t)
+        each(mix, t - 2)
+        each(soften)
+        each(score, t)
         send(t)
         return carry
 
     lax.fori_loop(2, steps, step, 0)
-    mix(steps - 2)
-    soften()
-    mix(steps - 1)
+    each(mix, steps - 2)
+    each(soften)
+    each(mix, steps - 1)
     attn_ref[...] = jnp.concatenate([o_buf.at[c][pl.ds(h, n_tok, stride=2), :] for h in range(n_heads) for c in range(2)], axis=1).astype(BF16)
     for t in range(steps):
         for copy in write_out(t):
@@ -358,9 +368,14 @@
         dst = (w1_buf, w3_buf, w2_buf)[kind]
         return pltpu.make_async_copy(src.at[0, :, pl.ds(pl.multiple_of(i * chunk, 128), chunk)], dst.at[i], w_sems.at[kind, i])
 
-    for i in range(n_chunks):
-        weight(0, i).start()
-        weight(1, i).start()
+    queue = [weight(kind, i) for i in range(n_chunks) for kind in range(2)] + [weight(2, i) for i in range(n_chunks)]
+
+    def feed(n):
+        for copy in queue[:n]:
+            copy.start()
+        del queue[:n]
+
+    feed(2)
 
     def plan(pieces, straight=0):
         size = width // pieces
@@ -377,17 +392,17 @@
         if item[0] == 0:
             enter(4)
         rs1.begin(*item)
-    for stage in (rs1.far, rs1.near, rs1.third):
+    feed(1)
+    for stage, n in ((rs1.far, 0), (rs1.near, 4), (rs1.third, 3)):
         for item in plan1:
             stage(*item)
+        feed(n)
     for item in plan1:
         cols = item[1]
         x1_buf[:, cols] = (x_buf[:, cols].astype(F32) + rs1.last(*item)).astype(BF16)
     rs1.finish()
     h_buf[me] = norm_rows(x1_buf[...].astype(F32), gain_ref[...].astype(F32))
-    gather_rows(h_buf, ag_send, ag_recv)
-    for i in range(n_chunks):
-        weight(2, i).start()
+    gather_rows(h_buf, ag_send, ag_recv, queue)
 
     def gate_up(i, carry):
         weight(0, i).wait()
@@ -446,11 +461,11 @@
     args = (x, gain, pos2, wq, wk, wv, k_tiles, v_tiles)
     return pl.pallas_call(
         qkv_kernel,
-        out_shape=[shape((n_tok, cols))] * 3 + [shape(k_tiles.shape)] * 2,
+        out_shape=[shape((n_tok, cols))] * 3 + [shape(k_tiles.shape)] * 2 + [shape((cols // (2 * LANES) * n_tok, LANES), F32)],
         in_specs=[HBM] * len(args),
-        out_specs=[VMEM] * 5,
+        out_specs=[VMEM] * 6,
         scratch_shapes=[
-            pltpu.VMEM((rows, width), BF16), pltpu.VMEM(gain.shape, BF16), pltpu.VMEM(pos2.shape, pos2.dtype),
+            pltpu.VMEM((2, n_tok, LANES), F32), pltpu.VMEM((rows, width), BF16), pltpu.VMEM(gain.shape, BF16), pltpu.VMEM(pos2.shape, pos2.dtype),
             pltpu.VMEM((blocks, rows, width), BF16), pltpu.VMEM((3, width, cols), BF16),
             dma((6,)), dma((2, 8)), dma((GATHER_SEMS,)), dma((GATHER_SEMS,))],
         compiler_params=pltpu.CompilerParams(collective_id=0, has_side_effects=True, vmem_limit_bytes=36 << 20),
@@ -458,7 +473,7 @@
     )(*(pltpu.with_memory_space_constraint(a, pltpu.HBM) for a in args))
 
 
-def run_attn(pos2, q, k, v, k_tiles, v_tiles):
+def run_attn(pos2, pos_rows, q, k, v, k_tiles, v_tiles):
     n_tok = k_tiles.shape[0]
     rows2 = q.shape[1] // (2 * LANES) * n_tok
     dma = pltpu.SemaphoreType.DMA
@@ -470,13 +485,13 @@
         in_specs=[HBM, VMEM, VMEM, VMEM, VMEM, VMEM, VMEM],
         out_specs=[VMEM, VMEM, VMEM, HBM, HBM],
         scratch_shapes=[
-            pltpu.SMEM(pos2.shape, pos2.dtype), pltpu.VMEM((2, n_tok * 8, LANES), F32), wide, wide, pltpu.VMEM((rows2, n_tok), F32),
-            pltpu.VMEM((4 * TOK_SUB, k_tiles.shape[1]), F32), pltpu.VMEM((8 * TOK_SUB, k_tiles.shape[1]), F32),
+            pltpu.SMEM(pos2.shape, pos2.dtype), pltpu.VMEM((2, n_tok * 8, LANES), F32), wide, wide,
+            pltpu.VMEM((TOK_STEP // TOK_UNIT, 4 * TOK_SUB, k_tiles.shape[1]), F32), pltpu.VMEM((TOK_STEP // TOK_UNIT, 8 * TOK_SUB, k_tiles.shape[1]), F32),
             dma, dma((2, n_tok // TOK_STEP))],
         input_output_aliases={5: 1, 6: 2},
         compiler_params=pltpu.CompilerParams(vmem_limit_bytes=24 << 20),
         name='attention',
-    )(pltpu.with_memory_space_constraint(pos2, pltpu.HBM), pos2, q, k, v, k_tiles, v_tiles)
+    )(pltpu.with_memory_space_constraint(pos2, pltpu.HBM), pos_rows, q, k, v, k_tiles, v_tiles)
     return attn, k_out, v_out
 
 
@@ -491,7 +506,7 @@
     chips = pltpu.VMEM((CHIPS, rows, width), BF16)
     return pl.pallas_call(
         mlp_kernel,
-        out_shape=shape((rows, width)),
+        out_shape=pltpu.VMEM((rows, width), BF16),
         in_specs=[VMEM, VMEM, VMEM, VMEM, HBM, HBM, HBM],
         out_specs=VMEM,
         scratch_shapes=[
@@ -516,8 +531,8 @@
     def device_step(hidden, positions, attn_gain, mlp_gain, w_query, w_key, w_value, w_out, w_gate, w_up, w_down, k_cache, v_cache):
         n_tok = positions.shape[0]
         pos2 = positions.reshape(1, n_tok)
-        q, k, v, k_tiles, v_tiles = run_qkv(hidden, attn_gain, pos2, w_query, w_key, w_value, to_tiles(k_cache), to_tiles(v_cache))
-        attn, k_out, v_out = run_attn(pos2, q, k, v, k_tiles, v_tiles)
+        q, k, v, k_tiles, v_tiles, pos_rows = run_qkv(hidden, attn_gain, pos2, w_query, w_key, w_value, to_tiles(k_cache), to_tiles(v_cache))
+        attn, k_out, v_out = run_attn(pos2, pos_rows, q, k, v, k_tiles, v_tiles)
         out = run_mlp(attn, hidden, mlp_gain, w_out, w_gate, w_up, w_down)
         return out, from_tiles(k_out, k_cache), from_tiles(v_out, v_cache)
 

time: 62.4 us -> 60.4 us (0.968)
  Pallas kernels: 60 us -> 57.4 us
  local copies, waits for them, and re-layouts: 1.56 us -> 2.2 us
    pallas_call x1, Pallas kernels: 8.63 us -> 7.11 us  [run_attn(): pl.pallas_call(attn_kernel, out_shape=[shape(q.shape), tiles, tiles, tile...]
    pallas_call x1, Pallas kernels: 36.4 us -> 35.6 us  [run_mlp(): pl.pallas_call(mlp_kernel, out_shape=pltpu.VMEM((rows, width), BF16), in_...]
    unnamed x7 -> x11, local copies, waits for them, and re-layouts: 1.56 us -> 2.2 us
where the time goes in v6:
time: 60.4 us; the launch traced here: 60.3 us
  Pallas kernels  57.4 us (95%)
  local copies, waits for them, and re-layouts  2.2 us (4%)
  between operations  0.69 us (1%)
    pallas_call x1, Pallas kernels, run_mlp(): pl.pallas_call(mlp_kernel, out_shape=pltpu.VMEM((rows, width), BF16), in_...  35.6 us
    pallas_call x1, Pallas kernels, run_qkv(): pl.pallas_call(qkv_kernel, out_shape=[shape((n_tok, cols))] * 3 + [shape(...  14.7 us
    pallas_call x1, Pallas kernels, run_attn(): pl.pallas_call(attn_kernel, out_shape=[shape(q.shape), tiles, tiles, tile...  7.11 us
    unnamed x11, local copies, waits for them, and re-layouts  2.2 us

profile of v6, /device:TPU:113, one launch (start us, length us, event | category | flops | bytes accessed | tf_op | source)
XLA Modules:
  0.0 60.3 jit_solution(10139974444415234090)
XLA Ops:
  0.6 14.7 %gather_qkv.1 = (bf16[128,512]{1,0:T(8,128)(2,1)S(1)}, bf16[128,512]{1,0:T(8,128)(2,1)S(1)}, bf16[128,512]{1,0:T(8,128)(2,1)S(1)}, bf16[128,256,128]{2,1,0:T(8,1...) custom-call(bf16[16,3072]{1,0:T(8,128)(2,1)} %x_buf.1, bf16[1,3072]{1,0:T(2,128)(2,1)} %gain_hbm.1, ...), custom_call_target="tpu_custom_call" | custom-call | tf_op jit(solution)/shard_map/gather_qkv/pallas_call | solution.py:462
  15.3 0.0 copy-start
  15.3 0.0 copy-start.1
  15.4 0.0 copy-start.4
  15.4 7.1 %attention.1 = (bf16[128,512]{1,0:T(8,128)(2,1)S(1)}, bf16[128,256,128]{2,1,0:T(8,128)(2,1)S(1)}, bf16[128,256,128]{2,1,0:T(8,128)(2,1)S(1)}, bf16[128,256,128]{2,1,0:T(8,128)(2,1)}, bf16[128,256,128]{2,1,0:T(8,128)(2,1)}) custom-call(s32[1,128]{1,0:T(1,128)} %bitcast.24, ...), custom_call_target="tpu_custom_call", output_to_operand_aliasing={{1}: (5, {}), {2}: (6, {})} | custom-call | tf_op jit(solution)/shard_map/attention/pallas_call | solution.py:482
  22.5 0.0 copy-start.2
  22.5 0.6 %copy-done.2 = bf16[128,512]{1,0:T(8,128)(2,1)} copy-done((bf16[128,512]{1,0:T(8,128)(2,1)}, bf16[128,512]{1,0:T(8,128)(2,1)S(1)}, u32[]{:S(2)}) %copy-start.2) | copy-done | bytes 131096
  23.1 0.0 copy-done
  23.1 0.0 copy-done.1
  23.1 0.0 copy-done.4
  23.1 0.0 copy-start.3
  23.2 0.9 %copy-done.3 = bf16[128,512]{1,0:T(8,128)(2,1)S(1)} copy-done((bf16[128,512]{1,0:T(8,128)(2,1)S(1)}, bf16[128,512]{1,0:T(8,128)(2,1)}, u32[]{:S(2)}) %copy-start.3) | copy-done | bytes 131096
  24.1 35.6 %reduce_mlp.1 = bf16[16,3072]{1,0:T(8,128)(2,1)S(1)} custom-call(bf16[128,512]{1,0:T(8,128)(2,1)S(1)} %copy-done.3, bf16[16,3072]{1,0:T(8,128)(2,1)S(1)} %copy-done.1, bf16[1,3072]{1,0:T(2,128)(2,1)S(1)} %copy-done.4, bf16[1,512,3072]{2,1,0:T(8,128)(2,1)S(1)} %copy-done, bf16[1,3072,3072]{2,1,0:T(8,128)(2,1)} %w1_hbm.1, bf16[1,3072,3072]{2,1,0:T(8,128)(2,1)} %w3_hbm.1, ...), custom_call_target="tpu_custom_call" | custom-call | tf_op jit(solution)/shard_map/reduce_mlp/pallas_call | solution.py:507
  59.7 0.6 %copy.25 = bf16[16,3072]{1,0:T(8,128)(2,1)} copy(bf16[16,3072]{1,0:T(8,128)(2,1)S(1)} %reduce_mlp.1) | data formatting | bytes 196608
Async XLA Ops:
  15.3 7.8 %copy-start = (bf16[1,512,3072]{2,1,0:T(8,128)(2,1)S(1)}, bf16[1,512,3072]{2,1,0:T(8,128)(2,1)}, u32[]{:S(2)}) copy-start(bf16[1,512,3072]{2,1,0:T(8,128)(2,1)} %wo_ref.1) | copy-start | bytes 9437188
  15.3 7.8 %copy-start.1 = (bf16[16,3072]{1,0:T(8,128)(2,1)S(1)}, bf16[16,3072]{1,0:T(8,128)(2,1)}, u32[]{:S(2)}) copy-start(bf16[16,3072]{1,0:T(8,128)(2,1)} %x_buf.1) | copy-start | bytes 294916
  15.4 7.8 %copy-start.4 = (bf16[1,3072]{1,0:T(2,128)(2,1)S(1)}, bf16[1,3072]{1,0:T(2,128)(2,1)}, u32[]{:S(2)}) copy-start(bf16[1,3072]{1,0:T(2,128)(2,1)} %gain_ref.1) | copy-start | bytes 18436
  22.5 0.6 %copy-start.2 = (bf16[128,512]{1,0:T(8,128)(2,1)}, bf16[128,512]{1,0:T(8,128)(2,1)S(1)}, u32[]{:S(2)}) copy-start(bf16[128,512]{1,0:T(8,128)(2,1)S(1)} %get-tuple-element.18.attn_ref) | copy-start | bytes 393220
  23.1 0.9 %copy-start.3 = (bf16[128,512]{1,0:T(8,128)(2,1)S(1)}, bf16[128,512]{1,0:T(8,128)(2,1)}, u32[]{:S(2)}) copy-start(bf16[128,512]{1,0:T(8,128)(2,1)} %copy-done.2) | copy-start | bytes 393220

commit v7 on v6

--- a/solution.py
+++ b/solution.py
@@ -13,12 +13,12 @@
 F32 = jnp.float32
 VMEM = pl.BlockSpec(memory_space=pltpu.VMEM)
 HBM = pl.BlockSpec(memory_space=pltpu.HBM)
-MLP_VMEM = 63400000
+MLP_VMEM = 61600000
 CHIPS = 4
 MLP_CHUNK = 512
 RS1_PIECES = 4
-RS2_LAG = 3
-RS2_STRAIGHT = 2
+RS2_LAG = 2
+RS2_STRAIGHT = 3
 GATHER_SEMS = 21
 
 
@@ -223,10 +223,9 @@
         moved = shift(probs, 2)
         prob_buf[u] = jnp.concatenate([probs[:sub], moved[:sub], probs[sub:], moved[sub:]], axis=0)
 
-    def score(t, u):
-        b0 = t * TOK_STEP + u * TOK_UNIT
-        for i in range(TOK_UNIT):
-            b = b0 + i
+    def insert(t):
+        for i in range(TOK_STEP):
+            b = t * TOK_STEP + i
             pos = pos_smem[0, b]
             tile = pl.ds(pl.multiple_of((pos >> 2) * 16, 16), 16)
             hit = (tile_row >> 2) == (pos & 3)
@@ -234,6 +233,9 @@
                 new = new_buf[kv, pl.ds(pl.multiple_of(b * 8, 8), 8), :]
                 old = bufs[kv][b, tile, :].astype(F32)
                 bufs[kv][b, tile, :] = jnp.where(hit, jnp.concatenate([new, new], axis=0), old).astype(BF16)
+
+    def score(t, u):
+        b0 = t * TOK_STEP + u * TOK_UNIT
         rows = out_rows(b0)
         none = jnp.zeros((sub, lanes), F32)
         q = jnp.concatenate(
@@ -258,17 +260,23 @@
             stage(*args, u)
 
     pos_copy.wait()
+    insert(0)
+
+    def place(t, carry):
+        insert(t)
+        send(t - 1)
+        return carry
+
+    lax.fori_loop(1, steps, place, 0)
     each(score, 0)
-    send(0)
+    send(steps - 1)
     each(soften)
     each(score, 1)
-    send(1)
 
     def step(t, carry):
         each(mix, t - 2)
         each(soften)
         each(score, t)
-        send(t)
         return carry
 
     lax.fori_loop(2, steps, step, 0)

time: 60.4 us -> 60.7 us (level)
    unnamed x11 -> x7, local copies, waits for them, and re-layouts: 2.2 us -> 2.54 us
where the time goes in v7:
time: 60.7 us; the launch traced here: 60.5 us
  Pallas kernels  57.3 us (94%)
  local copies, waits for them, and re-layouts  2.54 us (4%)
  between operations  0.7 us (1%)
    pallas_call x1, Pallas kernels, run_mlp(): pl.pallas_call(mlp_kernel, out_shape=pltpu.VMEM((rows, width), BF16), in_...  35.3 us
    pallas_call x1, Pallas kernels, run_qkv(): pl.pallas_call(qkv_kernel, out_shape=[shape((n_tok, cols))] * 3 + [shape(...  14.7 us
    pallas_call x1, Pallas kernels, run_attn(): pl.pallas_call(attn_kernel, out_shape=[shape(q.shape), tiles, tiles, tile...  7.23 us
    unnamed x7, local copies, waits for them, and re-layouts  2.54 us

profile of v7, /device:TPU:113, one launch (start us, length us, event | category | flops | bytes accessed | tf_op | source)
XLA Modules:
  0.0 60.5 jit_solution(3867336084535653324)
XLA Ops:
  0.6 14.7 %gather_qkv.1 = (bf16[128,512]{1,0:T(8,128)(2,1)S(1)}, bf16[128,512]{1,0:T(8,128)(2,1)S(1)}, bf16[128,512]{1,0:T(8,128)(2,1)S(1)}, bf16[128,256,128]{2,1,0:T(8,1...) custom-call(bf16[16,3072]{1,0:T(8,128)(2,1)} %x_buf.1, bf16[1,3072]{1,0:T(2,128)(2,1)} %gain_hbm.1, ...), custom_call_target="tpu_custom_call" | custom-call | tf_op jit(solution)/shard_map/gather_qkv/pallas_call | solution.py:470
  15.3 0.0 copy-start.1
  15.3 0.0 copy-start.2
  15.4 7.2 %attention.1 = (bf16[128,512]{1,0:T(8,128)(2,1)S(1)}, bf16[128,256,128]{2,1,0:T(8,128)(2,1)S(1)}, bf16[128,256,128]{2,1,0:T(8,128)(2,1)S(1)}, bf16[128,256,128]{2,1,0:T(8,128)(2,1)}, bf16[128,256,128]{2,1,0:T(8,128)(2,1)}) custom-call(s32[1,128]{1,0:T(1,128)} %bitcast.24, ...), custom_call_target="tpu_custom_call", output_to_operand_aliasing={{1}: (5, {}), {2}: (6, {})} | custom-call | tf_op jit(solution)/shard_map/attention/pallas_call | solution.py:490
  22.6 0.0 copy-done.1
  22.6 0.0 copy-done.2
  22.6 0.0 copy-start
  22.6 1.9 %copy-done = bf16[1,512,3072]{2,1,0:T(8,128)(2,1)S(1)} copy-done((bf16[1,512,3072]{2,1,0:T(8,128)(2,1)S(1)}, bf16[1,512,3072]{2,1,0:T(8,128)(2,1)}, u32[]{:S(2)}) %copy-start) | copy-done | bytes 3145752
  24.5 35.3 %reduce_mlp.1 = bf16[16,3072]{1,0:T(8,128)(2,1)S(1)} custom-call(bf16[128,512]{1,0:T(8,128)(2,1)S(1)} %get-tuple-element.18.attn_ref, bf16[16,3072]{1,0:T(8,128)(2,1)S(1)} %copy-done.1, bf16[1,3072]{1,0:T(2,128)(2,1)S(1)} %copy-done.2, bf16[1,512,3072]{2,1,0:T(8,128)(2,1)S(1)} %copy-done, bf16[1,3072,3072]{2,1,0:T(8,128)(2,1)} %w1_hbm.1, ...), custom_call_target="tpu_custom_call" | custom-call | tf_op jit(solution)/shard_map/reduce_mlp/pallas_call | solution.py:515
  59.9 0.6 %copy.25 = bf16[16,3072]{1,0:T(8,128)(2,1)} copy(bf16[16,3072]{1,0:T(8,128)(2,1)S(1)} %reduce_mlp.1) | data formatting | bytes 196608
Async XLA Ops:
  15.3 7.3 %copy-start.1 = (bf16[16,3072]{1,0:T(8,128)(2,1)S(1)}, bf16[16,3072]{1,0:T(8,128)(2,1)}, u32[]{:S(2)}) copy-start(bf16[16,3072]{1,0:T(8,128)(2,1)} %x_buf.1) | copy-start | bytes 294916
  15.3 7.3 %copy-start.2 = (bf16[1,3072]{1,0:T(2,128)(2,1)S(1)}, bf16[1,3072]{1,0:T(2,128)(2,1)}, u32[]{:S(2)}) copy-start(bf16[1,3072]{1,0:T(2,128)(2,1)} %gain_ref.1) | copy-start | bytes 18436
  22.6 1.9 %copy-start = (bf16[1,512,3072]{2,1,0:T(8,128)(2,1)S(1)}, bf16[1,512,3072]{2,1,0:T(8,128)(2,1)}, u32[]{:S(2)}) copy-start(bf16[1,512,3072]{2,1,0:T(8,128)(2,1)} %wo_ref.1) | copy-start | bytes 9437188

commit v8 on v7

--- a/solution.py
+++ b/solution.py
@@ -18,7 +18,7 @@
 MLP_CHUNK = 512
 RS1_PIECES = 4
 RS2_LAG = 2
-RS2_STRAIGHT = 3
+RS2_STRAIGHT = 4
 GATHER_SEMS = 21
 
 
@@ -72,7 +72,9 @@
         copy.start()
         sends.append(copy)
 
-    for cols, idx, peer in ((q0, 0, right), (q2, 1, left), (q1, 2, right), (q3, 3, left), (hi, 4, right), (lo, 5, left), (full, 6, other)):
+    for cols, idx, peer in (
+            (q0, 0, right), (q2, 1, left), (q1, 9, far), (q3, 10, far), (q1, 2, right), (q3, 3, left), (hi, 4, right), (lo, 5, left),
+            (full, 6, other)):
         send(me, cols, idx, peer)
     across = []
     behind = list(behind)
@@ -83,9 +85,9 @@
     if meanwhile is not None:
         meanwhile()
     for blk, cols, idx, onward, peer in (
-            (left, q0, 0, 7, right), (right, q2, 1, 8, left), (left, q1, 2, 9, right), (right, q3, 3, 10, left),
+            (left, q0, 0, 7, right), (right, q2, 1, 8, left), (left, q1, 2, None, None), (right, q3, 3, None, None),
             (left, hi, 4, None, None), (right, lo, 5, None, None),
-            (far, q0, 7, None, None), (far, q2, 8, None, None), (far, q1, 9, None, None), (far, q3, 10, None, None)):
+            (far, q1, 9, None, None), (far, q3, 10, None, None), (far, q0, 7, None, None), (far, q2, 8, None, None)):
         arrive(blk, cols, idx)
         if onward is not None:
             send(blk, cols, onward, peer)
@@ -107,7 +109,7 @@
 def qkv_kernel(x_hbm, gain_hbm, pos_hbm, wq_hbm, wk_hbm, wv_hbm, kc_hbm, vc_hbm, q_ref, k_ref, v_ref, kb_ref, vb_ref, pc_ref,
                trig_buf, x_buf, gain_ref, pos_ref, h_buf, w_buf, load_sems, cache_sems, send_sems, recv_sems):
     me, core, chip, other, right, left = places()
-    knock(other, right, left)
+    knock(other, right, left, lax.rem(chip + 2, CHIPS) * 2 + core)
     loads = [pltpu.make_async_copy(src, dst, load_sems.at[3 + i]) for i, (src, dst) in enumerate(((x_hbm, x_buf), (gain_hbm, gain_ref), (pos_hbm, pos_ref)))]
     w_copies = [pltpu.make_async_copy(w.at[0], w_buf.at[i], load_sems.at[i]) for i, w in enumerate((wq_hbm, wk_hbm, wv_hbm))]
     pieces = cache_sems.shape[1]
@@ -122,7 +124,7 @@
     for copy in loads:
         copy.wait()
     h_buf[me] = norm_rows(x_buf[...].astype(F32), gain_ref[...].astype(F32))
-    enter(3)
+    enter(4)
     n_tok = pos_ref.shape[1]
     half = LANES
     head = 2 * half
@@ -476,7 +478,7 @@
             pltpu.VMEM((2, n_tok, LANES), F32), pltpu.VMEM((rows, width), BF16), pltpu.VMEM(gain.shape, BF16), pltpu.VMEM(pos2.shape, pos2.dtype),
             pltpu.VMEM((blocks, rows, width), BF16), pltpu.VMEM((3, width, cols), BF16),
             dma((6,)), dma((2, 8)), dma((GATHER_SEMS,)), dma((GATHER_SEMS,))],
-        compiler_params=pltpu.CompilerParams(collective_id=0, has_side_effects=True, vmem_limit_bytes=36 << 20),
+        compiler_params=pltpu.CompilerParams(collective_id=0, has_side_effects=True, vmem_limit_bytes=16 << 20),
         name='gather_qkv',
     )(*(pltpu.with_memory_space_constraint(a, pltpu.HBM) for a in args))
 
@@ -497,7 +499,7 @@
             pltpu.VMEM((TOK_STEP // TOK_UNIT, 4 * TOK_SUB, k_tiles.shape[1]), F32), pltpu.VMEM((TOK_STEP // TOK_UNIT, 8 * TOK_SUB, k_tiles.shape[1]), F32),
             dma, dma((2, n_tok // TOK_STEP))],
         input_output_aliases={5: 1, 6: 2},
-        compiler_params=pltpu.CompilerParams(vmem_limit_bytes=24 << 20),
+        compiler_params=pltpu.CompilerParams(vmem_limit_bytes=8 << 20),
         name='attention',
     )(pltpu.with_memory_space_constraint(pos2, pltpu.HBM), pos_rows, q, k, v, k_tiles, v_tiles)
     return attn, k_out, v_out

time: 60.7 us -> 58.3 us (0.960)
  local copies, waits for them, and re-layouts: 2.54 us -> 0.66 us
    unnamed x7, local copies, waits for them, and re-layouts: 2.54 us -> 0.66 us
    pallas_call x1, Pallas kernels: 14.7 us -> 13.9 us  [run_qkv(): pl.pallas_call(qkv_kernel, out_shape=[shape((n_tok, cols))] * 3 + [shape(...]
where the time goes in v8:
time: 58.3 us; the launch traced here: 58.2 us
  Pallas kernels  56.8 us (97%)
  between operations  0.7 us (1%)
  local copies, waits for them, and re-layouts  0.66 us (1%)
    pallas_call x1, Pallas kernels, run_mlp(): pl.pallas_call(mlp_kernel, out_shape=pltpu.VMEM((rows, width), BF16), in_...  35.7 us
    pallas_call x1, Pallas kernels, run_qkv(): pl.pallas_call(qkv_kernel, out_shape=[shape((n_tok, cols))] * 3 + [shape(...  13.9 us
    pallas_call x1, Pallas kernels, run_attn(): pl.pallas_call(attn_kernel, out_shape=[shape(q.shape), tiles, tiles, tile...  7.23 us

profile of v8, /device:TPU:113, one launch (start us, length us, event | category | flops | bytes accessed | tf_op | source)
XLA Modules:
  0.0 58.2 jit_solution(15520671267730632765)
XLA Ops:
  0.6 13.9 %gather_qkv.1 = (bf16[128,512]{1,0:T(8,128)(2,1)S(1)}, bf16[128,512]{1,0:T(8,128)(2,1)S(1)}, bf16[128,512]{1,0:T(8,128)(2,1)S(1)}, bf16[128,256,128]{2,1,0:T(8,1...) custom-call(bf16[16,3072]{1,0:T(8,128)(2,1)} %x_buf.1, bf16[1,3072]{1,0:T(2,128)(2,1)} %gain_hbm.1, ...), custom_call_target="tpu_custom_call" | custom-call | tf_op jit(solution)/shard_map/gather_qkv/pallas_call | solution.py:472
  14.5 0.0 copy-start
  14.5 0.0 copy-start.1
  14.5 0.0 copy-start.2
  14.6 7.2 %attention.1 = (bf16[128,512]{1,0:T(8,128)(2,1)S(1)}, bf16[128,256,128]{2,1,0:T(8,128)(2,1)S(1)}, bf16[128,256,128]{2,1,0:T(8,128)(2,1)S(1)}, bf16[128,256,128]{2,1,0:T(8,128)(2,1)}, bf16[128,256,128]{2,1,0:T(8,128)(2,1)}) custom-call(s32[1,128]{1,0:T(1,128)} %bitcast.24, ...), custom_call_target="tpu_custom_call", output_to_operand_aliasing={{1}: (5, {}), {2}: (6, {})} | custom-call | tf_op jit(solution)/shard_map/attention/pallas_call | solution.py:492
  21.8 0.0 copy-done
  21.8 0.0 copy-done.1
  21.8 0.0 copy-done.2
  21.8 35.7 %reduce_mlp.1 = bf16[16,3072]{1,0:T(8,128)(2,1)S(1)} custom-call(bf16[128,512]{1,0:T(8,128)(2,1)S(1)} %get-tuple-element.18.attn_ref, bf16[16,3072]{1,0:T(8,128)(2,1)S(1)} %copy-done.1, bf16[1,3072]{1,0:T(2,128)(2,1)S(1)} %copy-done.2, bf16[1,512,3072]{2,1,0:T(8,128)(2,1)S(1)} %copy-done, bf16[1,3072,3072]{2,1,0:T(8,128)(2,1)} %w1_hbm.1, ...), custom_call_target="tpu_custom_call" | custom-call | tf_op jit(solution)/shard_map/reduce_mlp/pallas_call | solution.py:517
  57.5 0.6 %copy.25 = bf16[16,3072]{1,0:T(8,128)(2,1)} copy(bf16[16,3072]{1,0:T(8,128)(2,1)S(1)} %reduce_mlp.1) | data formatting | bytes 196608
Async XLA Ops:
  14.5 7.3 %copy-start = (bf16[1,512,3072]{2,1,0:T(8,128)(2,1)S(1)}, bf16[1,512,3072]{2,1,0:T(8,128)(2,1)}, u32[]{:S(2)}) copy-start(bf16[1,512,3072]{2,1,0:T(8,128)(2,1)} %wo_ref.1) | copy-start | bytes 9437188
  14.5 7.3 %copy-start.1 = (bf16[16,3072]{1,0:T(8,128)(2,1)S(1)}, bf16[16,3072]{1,0:T(8,128)(2,1)}, u32[]{:S(2)}) copy-start(bf16[16,3072]{1,0:T(8,128)(2,1)} %x_buf.1) | copy-start | bytes 294916
  14.5 7.3 %copy-start.2 = (bf16[1,3072]{1,0:T(2,128)(2,1)S(1)}, bf16[1,3072]{1,0:T(2,128)(2,1)}, u32[]{:S(2)}) copy-start(bf16[1,3072]{1,0:T(2,128)(2,1)} %gain_ref.1) | copy-start | bytes 18436

commit v9 on v8

--- a/solution.py
+++ b/solution.py
@@ -262,26 +262,28 @@
             stage(*args, u)
 
     pos_copy.wait()
-    insert(0)
-
-    def place(t, carry):
+    for t in range(3):
         insert(t)
-        send(t - 1)
-        return carry
-
-    lax.fori_loop(1, steps, place, 0)
+    send(0)
     each(score, 0)
-    send(steps - 1)
+    send(1)
+    send(2)
     each(soften)
     each(score, 1)
 
-    def step(t, carry):
+    def stages(t):
         each(mix, t - 2)
         each(soften)
         each(score, t)
+
+    def step(t, carry):
+        insert(t + 1)
+        stages(t)
+        send(t + 1)
         return carry
 
-    lax.fori_loop(2, steps, step, 0)
+    lax.fori_loop(2, steps - 1, step, 0)
+    stages(steps - 1)
     each(mix, steps - 2)
     each(soften)
     each(mix, steps - 1)
@@ -399,9 +401,10 @@
     attn = attn_ref[...]
     for item in plan1:
         put_part(item[1], jnp.dot(attn, wo_ref[0, :, item[1]], preferred_element_type=F32))
-        if item[0] == 0:
-            enter(4)
-        rs1.begin(*item)
+    enter(4)
+    for kind in range(4):
+        for item in plan1:
+            rs1.go(kind, *item)
     feed(1)
     for stage, n in ((rs1.far, 0), (rs1.near, 4), (rs1.third, 3)):
         for item in plan1:

time: 58.3 us -> 58.4 us (level)
  no operation moved by 1% of the time
where the time goes in v9:
time: 58.4 us; the launch traced here: 58.3 us
  Pallas kernels  57 us (98%)
  between operations  0.7 us (1%)
  local copies, waits for them, and re-layouts  0.66 us (1%)
    pallas_call x1, Pallas kernels, run_mlp(): pl.pallas_call(mlp_kernel, out_shape=pltpu.VMEM((rows, width), BF16), in_...  35.7 us
    pallas_call x1, Pallas kernels, run_qkv(): pl.pallas_call(qkv_kernel, out_shape=[shape((n_tok, cols))] * 3 + [shape(...  13.9 us
    pallas_call x1, Pallas kernels, run_attn(): pl.pallas_call(attn_kernel, out_shape=[shape(q.shape), tiles, tiles, tile...  7.4 us

profile of v9, /device:TPU:113, one launch (start us, length us, event | category | flops | bytes accessed | tf_op | source)
XLA Modules:
  0.0 58.3 jit_solution(10831222135918217703)
XLA Ops:
  0.6 13.9 %gather_qkv.1 = (bf16[128,512]{1,0:T(8,128)(2,1)S(1)}, bf16[128,512]{1,0:T(8,128)(2,1)S(1)}, bf16[128,512]{1,0:T(8,128)(2,1)S(1)}, bf16[128,256,128]{2,1,0:T(8,1...) custom-call(bf16[16,3072]{1,0:T(8,128)(2,1)} %x_buf.1, bf16[1,3072]{1,0:T(2,128)(2,1)} %gain_hbm.1, ...), custom_call_target="tpu_custom_call" | custom-call | tf_op jit(solution)/shard_map/gather_qkv/pallas_call | solution.py:475
  14.5 0.0 copy-start
  14.5 0.0 copy-start.1
  14.5 0.0 copy-start.2
  14.6 7.4 %attention.1 = (bf16[128,512]{1,0:T(8,128)(2,1)S(1)}, bf16[128,256,128]{2,1,0:T(8,128)(2,1)S(1)}, bf16[128,256,128]{2,1,0:T(8,128)(2,1)S(1)}, bf16[128,256,128]{2,1,0:T(8,128)(2,1)}, bf16[128,256,128]{2,1,0:T(8,128)(2,1)}) custom-call(s32[1,128]{1,0:T(1,128)} %bitcast.24, ...), custom_call_target="tpu_custom_call", output_to_operand_aliasing={{1}: (5, {}), {2}: (6, {})} | custom-call | tf_op jit(solution)/shard_map/attention/pallas_call | solution.py:495
  22.0 0.0 copy-done
  22.0 0.0 copy-done.1
  22.0 0.0 copy-done.2
  22.0 35.7 %reduce_mlp.1 = bf16[16,3072]{1,0:T(8,128)(2,1)S(1)} custom-call(bf16[128,512]{1,0:T(8,128)(2,1)S(1)} %get-tuple-element.18.attn_ref, bf16[16,3072]{1,0:T(8,128)(2,1)S(1)} %copy-done.1, bf16[1,3072]{1,0:T(2,128)(2,1)S(1)} %copy-done.2, bf16[1,512,3072]{2,1,0:T(8,128)(2,1)S(1)} %copy-done, bf16[1,3072,3072]{2,1,0:T(8,128)(2,1)} %w1_hbm.1, ...), custom_call_target="tpu_custom_call" | custom-call | tf_op jit(solution)/shard_map/reduce_mlp/pallas_call | solution.py:520
  57.7 0.6 %copy.25 = bf16[16,3072]{1,0:T(8,128)(2,1)} copy(bf16[16,3072]{1,0:T(8,128)(2,1)S(1)} %reduce_mlp.1) | data formatting | bytes 196608
Async XLA Ops:
  14.5 7.4 %copy-start = (bf16[1,512,3072]{2,1,0:T(8,128)(2,1)S(1)}, bf16[1,512,3072]{2,1,0:T(8,128)(2,1)}, u32[]{:S(2)}) copy-start(bf16[1,512,3072]{2,1,0:T(8,128)(2,1)} %wo_ref.1) | copy-start | bytes 9437188
  14.5 7.4 %copy-start.1 = (bf16[16,3072]{1,0:T(8,128)(2,1)S(1)}, bf16[16,3072]{1,0:T(8,128)(2,1)}, u32[]{:S(2)}) copy-start(bf16[16,3072]{1,0:T(8,128)(2,1)} %x_buf.1) | copy-start | bytes 294916
  14.5 7.4 %copy-start.2 = (bf16[1,3072]{1,0:T(2,128)(2,1)S(1)}, bf16[1,3072]{1,0:T(2,128)(2,1)}, u32[]{:S(2)}) copy-start(bf16[1,3072]{1,0:T(2,128)(2,1)} %gain_ref.1) | copy-start | bytes 18436

commit v10 on v8

--- a/solution.py
+++ b/solution.py
@@ -106,7 +106,7 @@
 LANES = 128
 
 
-def qkv_kernel(x_hbm, gain_hbm, pos_hbm, wq_hbm, wk_hbm, wv_hbm, kc_hbm, vc_hbm, q_ref, k_ref, v_ref, kb_ref, vb_ref, pc_ref,
+def qkv_kernel(x_hbm, gain_hbm, pos_hbm, wq_hbm, wk_hbm, wv_hbm, kc_hbm, vc_hbm, wo_hbm, q_ref, k_ref, v_ref, kb_ref, vb_ref, pc_ref, wo_ref,
                trig_buf, x_buf, gain_ref, pos_ref, h_buf, w_buf, load_sems, cache_sems, send_sems, recv_sems):
     me, core, chip, other, right, left = places()
     knock(other, right, left, lax.rem(chip + 2, CHIPS) * 2 + core)
@@ -119,6 +119,7 @@
         for p in range(pieces):
             toks = pl.ds(p * piece, piece)
             cache_in.append(pltpu.make_async_copy(hbm.at[toks], buf.at[toks], cache_sems.at[kv, p]))
+    cache_in.append(pltpu.make_async_copy(wo_hbm, wo_ref, load_sems.at[6]))
     for copy in loads:
         copy.start()
     for copy in loads:
@@ -292,7 +293,8 @@
 
 
 class Reducer:
-    def __init__(self, part, from_other, chip_sum, far_in, near_in, last_in, send_sems, recv_sems):
+    def __init__(self, part, from_other, chip_sum, far_in, near_in, last_in, send_sems, recv_sems, joint=False):
+        self.joint = joint
         self.part, self.from_other, self.chip_sum = part, from_other, chip_sum
         self.far_in, self.near_in, self.last_in = far_in, near_in, last_in
         self.send_sems, self.recv_sems = send_sems, recv_sems
@@ -306,6 +308,7 @@
         opposite = lax.rem(self.chip + 2, CHIPS)
         if kind < 4:
             k = (opposite, behind, ahead, self.chip)[kind]
+            k = slice(None) if self.joint else k
             src, dst, peer = self.part.at[k, 1 - self.core, :, cols], self.from_other.at[k, :, cols], self.other
         else:
             src, dst, peer = (
@@ -321,11 +324,12 @@
         self.sends.append(copy)
 
     def begin(self, j, cols, way, direct):
-        for kind in range(4):
+        for kind in range(1 if self.joint else 4):
             self.go(kind, j, cols, way, direct)
 
     def pair(self, kind, k, j, cols, way, direct):
-        self.copy(kind, j, cols, way, direct).wait_recv()
+        if kind == 0 or not self.joint:
+            self.copy(kind, j, cols, way, direct).wait_recv()
         return self.part[k, self.core, :, cols].astype(F32) + self.from_other[k, :, cols].astype(F32)
 
     def far(self, j, cols, way, direct):
@@ -399,9 +403,10 @@
     attn = attn_ref[...]
     for item in plan1:
         put_part(item[1], jnp.dot(attn, wo_ref[0, :, item[1]], preferred_element_type=F32))
-        if item[0] == 0:
-            enter(4)
-        rs1.begin(*item)
+    enter(4)
+    for kind in range(4):
+        for item in plan1:
+            rs1.go(kind, *item)
     feed(1)
     for stage, n in ((rs1.far, 0), (rs1.near, 4), (rs1.third, 3)):
         for item in plan1:
@@ -425,7 +430,7 @@
 
     lax.fori_loop(0, n_chunks, gate_up, 0)
 
-    rs2 = Reducer(part, other_in, chip_sum, far_in, near_in, last_in, rs2_send, rs2_recv)
+    rs2 = Reducer(part, other_in, chip_sum, far_in, near_in, last_in, rs2_send, rs2_recv, joint=True)
     plan2 = plan(n_chunks, RS2_STRAIGHT)
     for j in range(n_chunks + RS2_LAG):
         if j < n_chunks:
@@ -462,22 +467,22 @@
     return tiles.reshape(n_tok, n_rows, halves, n_heads, LANES).transpose(0, 1, 3, 2, 4).reshape(like.shape)
 
 
-def run_qkv(x, gain, pos2, wq, wk, wv, k_tiles, v_tiles):
+def run_qkv(x, gain, pos2, wq, wk, wv, k_tiles, v_tiles, wo):
     n_tok = k_tiles.shape[0]
     rows, width = x.shape
     cols = wq.shape[2]
     blocks = n_tok // rows
     dma = pltpu.SemaphoreType.DMA
-    args = (x, gain, pos2, wq, wk, wv, k_tiles, v_tiles)
+    args = (x, gain, pos2, wq, wk, wv, k_tiles, v_tiles, wo)
     return pl.pallas_call(
         qkv_kernel,
-        out_shape=[shape((n_tok, cols))] * 3 + [shape(k_tiles.shape)] * 2 + [shape((cols // (2 * LANES) * n_tok, LANES), F32)],
+        out_shape=[shape((n_tok, cols))] * 3 + [shape(k_tiles.shape)] * 2 + [shape((cols // (2 * LANES) * n_tok, LANES), F32), shape(wo.shape)],
         in_specs=[HBM] * len(args),
-        out_specs=[VMEM] * 6,
+        out_specs=[VMEM] * 7,
         scratch_shapes=[
             pltpu.VMEM((2, n_tok, LANES), F32), pltpu.VMEM((rows, width), BF16), pltpu.VMEM(gain.shape, BF16), pltpu.VMEM(pos2.shape, pos2.dtype),
             pltpu.VMEM((blocks, rows, width), BF16), pltpu.VMEM((3, width, cols), BF16),
-            dma((6,)), dma((2, 8)), dma((GATHER_SEMS,)), dma((GATHER_SEMS,))],
+            dma((7,)), dma((2, 8)), dma((GATHER_SEMS,)), dma((GATHER_SEMS,))],
         compiler_params=pltpu.CompilerParams(collective_id=0, has_side_effects=True, vmem_limit_bytes=16 << 20),
         name='gather_qkv',
     )(*(pltpu.with_memory_space_constraint(a, pltpu.HBM) for a in args))
@@ -541,9 +546,9 @@
     def device_step(hidden, positions, attn_gain, mlp_gain, w_query, w_key, w_value, w_out, w_gate, w_up, w_down, k_cache, v_cache):
         n_tok = positions.shape[0]
         pos2 = positions.reshape(1, n_tok)
-        q, k, v, k_tiles, v_tiles, pos_rows = run_qkv(hidden, attn_gain, pos2, w_query, w_key, w_value, to_tiles(k_cache), to_tiles(v_cache))
+        q, k, v, k_tiles, v_tiles, pos_rows, wo = run_qkv(hidden, attn_gain, pos2, w_query, w_key, w_value, to_tiles(k_cache), to_tiles(v_cache), w_out)
         attn, k_out, v_out = run_attn(pos2, pos_rows, q, k, v, k_tiles, v_tiles)
-        out = run_mlp(attn, hidden, mlp_gain, w_out, w_gate, w_up, w_down)
+        out = run_mlp(attn, hidden, mlp_gain, wo, w_gate, w_up, w_down)
         return out, from_tiles(k_out, k_cache), from_tiles(v_out, v_cache)
 
     return jax.shard_map(device_step, mesh=mesh, in_specs=in_specs, out_specs=out_specs, check_vma=False)

time: 58.3 us -> 57.8 us (level)
    pallas_call x1, Pallas kernels: 35.7 us -> 34.9 us  [run_mlp(): pl.pallas_call(mlp_kernel, out_shape=pltpu.VMEM((rows, width), BF16), in_...]
where the time goes in v10:
time: 57.8 us; the launch traced here: 57.7 us
  Pallas kernels  56.3 us (97%)
  between operations  0.69 us (1%)
  local copies, waits for them, and re-layouts  0.66 us (1%)
    pallas_call x1, Pallas kernels, run_mlp(): pl.pallas_call(mlp_kernel, out_shape=pltpu.VMEM((rows, width), BF16), in_...  34.9 us
    pallas_call x1, Pallas kernels, run_qkv(): pl.pallas_call(qkv_kernel, out_shape=[shape((n_tok, cols))] * 3 + [shape(...  14.2 us
    pallas_call x1, Pallas kernels, run_attn(): pl.pallas_call(attn_kernel, out_shape=[shape(q.shape), tiles, tiles, tile...  7.23 us

profile of v10, /device:TPU:113, one launch (start us, length us, event | category | flops | bytes accessed | tf_op | source)
XLA Modules:
  0.0 57.7 jit_solution(15101813495026146698)
XLA Ops:
  0.6 14.2 %gather_qkv.1 = (bf16[128,512]{1,0:T(8,128)(2,1)S(1)}, bf16[128,512]{1,0:T(8,128)(2,1)S(1)}, bf16[128,512]{1,0:T(8,128)(2,1)S(1)}, bf16[128,256,128]{2,1,0:T(8,1...) custom-call(bf16[16,3072]{1,0:T(8,128)(2,1)} %x_buf.1, ...), custom_call_target="tpu_custom_call" | custom-call | tf_op jit(solution)/shard_map/gather_qkv/pallas_call | solution.py:477
  14.8 0.0 copy-start
  14.8 0.0 copy-start.1
  14.9 7.2 %attention.1 = (bf16[128,512]{1,0:T(8,128)(2,1)S(1)}, bf16[128,256,128]{2,1,0:T(8,128)(2,1)S(1)}, bf16[128,256,128]{2,1,0:T(8,128)(2,1)S(1)}, bf16[128,256,128]{2,1,0:T(8,128)(2,1)}, bf16[128,256,128]{2,1,0:T(8,128)(2,1)}) custom-call(s32[1,128]{1,0:T(1,128)} %bitcast.24, ...), custom_call_target="tpu_custom_call", output_to_operand_aliasing={{1}: (5, {}), {2}: (6, {})} | custom-call | tf_op jit(solution)/shard_map/attention/pallas_call | solution.py:497
  22.1 0.0 copy-done
  22.1 0.0 copy-done.1
  22.1 34.9 %reduce_mlp.1 = bf16[16,3072]{1,0:T(8,128)(2,1)S(1)} custom-call(bf16[128,512]{1,0:T(8,128)(2,1)S(1)} %get-tuple-element.19.attn_ref, bf16[16,3072]{1,0:T(8,128)(2,1)S(1)} %copy-done, bf16[1,3072]{1,0:T(2,128)(2,1)S(1)} %copy-done.1, bf16[1,512,3072]{2,1,0:T(8,128)(2,1)S(1)} %get-tuple-element.20.wo_ref, bf16[1,3072,3072]{2,1,0:T(8,128)(2,1)} %w1_hbm.1, ...), custom_call_target="tpu_custom_call" | custom-call | tf_op jit(solution)/shard_map/reduce_mlp/pallas_call | solution.py:522
  57.0 0.6 %copy.25 = bf16[16,3072]{1,0:T(8,128)(2,1)} copy(bf16[16,3072]{1,0:T(8,128)(2,1)S(1)} %reduce_mlp.1) | data formatting | bytes 196608
Async XLA Ops:
  14.8 7.3 %copy-start = (bf16[16,3072]{1,0:T(8,128)(2,1)S(1)}, bf16[16,3072]{1,0:T(8,128)(2,1)}, u32[]{:S(2)}) copy-start(bf16[16,3072]{1,0:T(8,128)(2,1)} %x_buf.1) | copy-start | bytes 294916
  14.8 7.3 %copy-start.1 = (bf16[1,3072]{1,0:T(2,128)(2,1)S(1)}, bf16[1,3072]{1,0:T(2,128)(2,1)}, u32[]{:S(2)}) copy-start(bf16[1,3072]{1,0:T(2,128)(2,1)} %gain_ref.1) | copy-start | bytes 18436

commit v11 on v10

--- a/solution.py
+++ b/solution.py
@@ -120,7 +120,7 @@
             toks = pl.ds(p * piece, piece)
             cache_in.append(pltpu.make_async_copy(hbm.at[toks], buf.at[toks], cache_sems.at[kv, p]))
     cache_in.append(pltpu.make_async_copy(wo_hbm, wo_ref, load_sems.at[6]))
-    for copy in loads:
+    for copy in loads + w_copies[:1]:
         copy.start()
     for copy in loads:
         copy.wait()
@@ -143,7 +143,7 @@
         rows2 = pc_ref.shape[0]
         pc_ref[...] = jnp.broadcast_to(pick(rows2, rows2 // n_tok), pc_ref.shape)
 
-    gather_rows(h_buf, send_sems, recv_sems, w_copies + cache_in, tables)
+    gather_rows(h_buf, send_sems, recv_sems, w_copies[1:] + cache_in, tables)
     cos_tab, sin_tab = trig_buf[0], trig_buf[1]
     h_all = h_buf[...].reshape(n_tok, h_buf.shape[2])
     for i, out_ref in enumerate((q_ref, k_ref, v_ref)):

time: 57.8 us -> 57.8 us (level)
  no operation moved by 1% of the time
where the time goes in v11:
time: 57.8 us; the launch traced here: 57.7 us
  Pallas kernels  56.4 us (98%)
  between operations  0.69 us (1%)
  local copies, waits for them, and re-layouts  0.66 us (1%)
    pallas_call x1, Pallas kernels, run_mlp(): pl.pallas_call(mlp_kernel, out_shape=pltpu.VMEM((rows, width), BF16), in_...  35.3 us
    pallas_call x1, Pallas kernels, run_qkv(): pl.pallas_call(qkv_kernel, out_shape=[shape((n_tok, cols))] * 3 + [shape(...  13.9 us
    pallas_call x1, Pallas kernels, run_attn(): pl.pallas_call(attn_kernel, out_shape=[shape(q.shape), tiles, tiles, tile...  7.23 us

profile of v11, /device:TPU:113, one launch (start us, length us, event | category | flops | bytes accessed | tf_op | source)
XLA Modules:
  0.0 57.7 jit_solution(584653971413306453)
XLA Ops:
  0.6 13.9 %gather_qkv.1 = (bf16[128,512]{1,0:T(8,128)(2,1)S(1)}, bf16[128,512]{1,0:T(8,128)(2,1)S(1)}, bf16[128,512]{1,0:T(8,128)(2,1)S(1)}, bf16[128,256,128]{2,1,0:T(8,1...) custom-call(bf16[16,3072]{1,0:T(8,128)(2,1)} %x_buf.1, ...), custom_call_target="tpu_custom_call" | custom-call | tf_op jit(solution)/shard_map/gather_qkv/pallas_call | solution.py:477
  14.5 0.0 copy-start
  14.5 0.0 copy-start.1
  14.6 7.2 %attention.1 = (bf16[128,512]{1,0:T(8,128)(2,1)S(1)}, bf16[128,256,128]{2,1,0:T(8,128)(2,1)S(1)}, bf16[128,256,128]{2,1,0:T(8,128)(2,1)S(1)}, bf16[128,256,128]{2,1,0:T(8,128)(2,1)}, bf16[128,256,128]{2,1,0:T(8,128)(2,1)}) custom-call(s32[1,128]{1,0:T(1,128)} %bitcast.24, ...), custom_call_target="tpu_custom_call", output_to_operand_aliasing={{1}: (5, {}), {2}: (6, {})} | custom-call | tf_op jit(solution)/shard_map/attention/pallas_call | solution.py:497
  21.8 0.0 copy-done
  21.8 0.0 copy-done.1
  21.8 35.3 %reduce_mlp.1 = bf16[16,3072]{1,0:T(8,128)(2,1)S(1)} custom-call(bf16[128,512]{1,0:T(8,128)(2,1)S(1)} %get-tuple-element.19.attn_ref, bf16[16,3072]{1,0:T(8,128)(2,1)S(1)} %copy-done, bf16[1,3072]{1,0:T(2,128)(2,1)S(1)} %copy-done.1, bf16[1,512,3072]{2,1,0:T(8,128)(2,1)S(1)} %get-tuple-element.20.wo_ref, bf16[1,3072,3072]{2,1,0:T(8,128)(2,1)} %w1_hbm.1, ...), custom_call_target="tpu_custom_call" | custom-call | tf_op jit(solution)/shard_map/reduce_mlp/pallas_call | solution.py:522
  57.1 0.6 %copy.25 = bf16[16,3072]{1,0:T(8,128)(2,1)} copy(bf16[16,3072]{1,0:T(8,128)(2,1)S(1)} %reduce_mlp.1) | data formatting | bytes 196608
Async XLA Ops:
  14.5 7.3 %copy-start = (bf16[16,3072]{1,0:T(8,128)(2,1)S(1)}, bf16[16,3072]{1,0:T(8,128)(2,1)}, u32[]{:S(2)}) copy-start(bf16[16,3072]{1,0:T(8,128)(2,1)} %x_buf.1) | copy-start | bytes 294916
  14.5 7.3 %copy-start.1 = (bf16[1,3072]{1,0:T(2,128)(2,1)S(1)}, bf16[1,3072]{1,0:T(2,128)(2,1)}, u32[]{:S(2)}) copy-start(bf16[1,3072]{1,0:T(2,128)(2,1)} %gain_ref.1) | copy-start | bytes 18436

commit v12 on v10

--- a/solution.py
+++ b/solution.py
@@ -18,7 +18,7 @@
 MLP_CHUNK = 512
 RS1_PIECES = 4
 RS2_LAG = 2
-RS2_STRAIGHT = 4
+RS2_STRAIGHT = 5
 GATHER_SEMS = 21
 
 

time: 57.8 us -> 57.9 us (level)
  no operation moved by 1% of the time
where the time goes in v12:
time: 57.9 us; the launch traced here: 57.8 us
  Pallas kernels  56.4 us (97%)
  between operations  0.69 us (1%)
  local copies, waits for them, and re-layouts  0.66 us (1%)
    pallas_call x1, Pallas kernels, run_mlp(): pl.pallas_call(mlp_kernel, out_shape=pltpu.VMEM((rows, width), BF16), in_...  35 us
    pallas_call x1, Pallas kernels, run_qkv(): pl.pallas_call(qkv_kernel, out_shape=[shape((n_tok, cols))] * 3 + [shape(...  14.2 us
    pallas_call x1, Pallas kernels, run_attn(): pl.pallas_call(attn_kernel, out_shape=[shape(q.shape), tiles, tiles, tile...  7.23 us

profile of v12, /device:TPU:113, one launch (start us, length us, event | category | flops | bytes accessed | tf_op | source)
XLA Modules:
  0.0 57.8 jit_solution(5669712000041633948)
XLA Ops:
  0.6 14.2 %gather_qkv.1 = (bf16[128,512]{1,0:T(8,128)(2,1)S(1)}, bf16[128,512]{1,0:T(8,128)(2,1)S(1)}, bf16[128,512]{1,0:T(8,128)(2,1)S(1)}, bf16[128,256,128]{2,1,0:T(8,1...) custom-call(bf16[16,3072]{1,0:T(8,128)(2,1)} %x_buf.1, ...), custom_call_target="tpu_custom_call" | custom-call | tf_op jit(solution)/shard_map/gather_qkv/pallas_call | solution.py:477
  14.8 0.0 copy-start
  14.8 0.0 copy-start.1
  14.9 7.2 %attention.1 = (bf16[128,512]{1,0:T(8,128)(2,1)S(1)}, bf16[128,256,128]{2,1,0:T(8,128)(2,1)S(1)}, bf16[128,256,128]{2,1,0:T(8,128)(2,1)S(1)}, bf16[128,256,128]{2,1,0:T(8,128)(2,1)}, bf16[128,256,128]{2,1,0:T(8,128)(2,1)}) custom-call(s32[1,128]{1,0:T(1,128)} %bitcast.24, ...), custom_call_target="tpu_custom_call", output_to_operand_aliasing={{1}: (5, {}), {2}: (6, {})} | custom-call | tf_op jit(solution)/shard_map/attention/pallas_call | solution.py:497
  22.1 0.0 copy-done
  22.1 0.0 copy-done.1
  22.1 35.0 %reduce_mlp.1 = bf16[16,3072]{1,0:T(8,128)(2,1)S(1)} custom-call(bf16[128,512]{1,0:T(8,128)(2,1)S(1)} %get-tuple-element.19.attn_ref, bf16[16,3072]{1,0:T(8,128)(2,1)S(1)} %copy-done, bf16[1,3072]{1,0:T(2,128)(2,1)S(1)} %copy-done.1, bf16[1,512,3072]{2,1,0:T(8,128)(2,1)S(1)} %get-tuple-element.20.wo_ref, bf16[1,3072,3072]{2,1,0:T(8,128)(2,1)} %w1_hbm.1, ...), custom_call_target="tpu_custom_call" | custom-call | tf_op jit(solution)/shard_map/reduce_mlp/pallas_call | solution.py:522
  57.1 0.6 %copy.25 = bf16[16,3072]{1,0:T(8,128)(2,1)} copy(bf16[16,3072]{1,0:T(8,128)(2,1)S(1)} %reduce_mlp.1) | data formatting | bytes 196608
Async XLA Ops:
  14.8 7.3 %copy-start = (bf16[16,3072]{1,0:T(8,128)(2,1)S(1)}, bf16[16,3072]{1,0:T(8,128)(2,1)}, u32[]{:S(2)}) copy-start(bf16[16,3072]{1,0:T(8,128)(2,1)} %x_buf.1) | copy-start | bytes 294916
  14.8 7.3 %copy-start.1 = (bf16[1,3072]{1,0:T(2,128)(2,1)S(1)}, bf16[1,3072]{1,0:T(2,128)(2,1)}, u32[]{:S(2)}) copy-start(bf16[1,3072]{1,0:T(2,128)(2,1)} %gain_ref.1) | copy-start | bytes 18436
